TPU v7x, 1024 devices: a whole 4x4x32 slice. The times are simulated.
1024 devices in a mesh: tensor: 4 (over y), expert: 64 (over z, core), dp: 4 (over x).
Axes of the slice: x: 4, y: 4, z: 32, core: 2. Of those that a mesh axis runs over, the one named last changes fastest.
Arguments:
- grad_out: bfloat16 [16384, 4096], P(('expert', 'dp')), may hold values from -6 to 6
- route_ids: int32 [16384, 8], P(('expert', 'dp')), may hold values from 0 to 127, all different within a row; in each aligned block of 64 rows (0 to 63, 64 to 127, ...) at most 6 rows name the same one
- route_probs: bfloat16 [16384, 8], P(('expert', 'dp')), may hold values from 0.019897461 to 0.5
- gate_act: bfloat16 [4, 128, 384, 768], P('dp', 'expert', None, 'tensor'), may hold values from -8 to 8
- up_act: bfloat16 [4, 128, 384, 768], P('dp', 'expert', None, 'tensor'), may hold values from -6 to 6
- w_down: bfloat16 [128, 768, 4096], P('expert', 'tensor'), may hold values from -0.21875 to 0.21875
Outputs:
- grad_gate: bfloat16 [4, 128, 384, 768], P('dp', 'expert', None, 'tensor')
- grad_up: bfloat16 [4, 128, 384, 768], P('dp', 'expert', None, 'tensor')
- grad_w_down: bfloat16 [128, 768, 4096], P('expert', 'tensor', 'dp')
- grad_probs: float32 [16384, 8], P(('expert', 'dp'))
Inputs may be any that keep to these rules, and one draw needn't show every extreme that they name: `route_ids`: each row names 8 different experts. Within the 64 rows of one index pair of expert and dp no expert is named more than 6 times, and in every draw some expert is named exactly 6 times there.
All inputs are finite; a program needn't handle non-finite values.
Results may differ from a plain program's by a relative error of at most 0.009.
Values may be sent and summed in bfloat16 or wider, within the bound.
No kernel may reach another device: no remote copies, remote signals or barrier semaphores. Data moves between devices by JAX's collectives and lax.ppermute only.
A program may use at most 64 MiB of HBM per device.

v0:
```python
import jax
import jax.numpy as jnp
from jax import lax
from jax.sharding import PartitionSpec as P


def side_by_side(arrays, axis, split_dim, concat_dim, along):
    columns = [a.reshape(*a.shape[:along], -1) for a in arrays]
    both = jnp.concatenate(columns, axis=along)
    whole, at, finished = (
        lax.all_to_all(both, axis, split_axis=split_dim, concat_axis=concat_dim, tiled=True),
        0,
        [],
    )
    for a, column in zip(arrays, columns):
        slab = whole[..., at : at + column.shape[along]]
        finished.append(slab.reshape(*slab.shape[:along], *a.shape[along:]))
        at += column.shape[along]
    return tuple(finished)


def split_up(x, dim, devices):
    dims = x.shape
    tiles = x.reshape(*dims[:dim], devices, dims[dim] // devices, *dims[dim + 1 :])
    return jnp.moveaxis(tiles, dim, 0)


def sent_and_summed(x, axis, dim):
    tiles = split_up(x, dim, lax.axis_size(axis))
    arrived = lax.all_to_all(tiles, axis, split_axis=0, concat_axis=0, tiled=True)
    return arrived.astype(jnp.float32).sum(axis=0)


def copy_for_each(x, axis):
    copies = jnp.broadcast_to(x, (lax.axis_size(axis), *x.shape))
    return lax.all_to_all(copies, axis, split_axis=0, concat_axis=0, tiled=True)


def taken_together(x, axis):
    everything = copy_for_each(x, axis)
    return jnp.sum(everything, axis=0)


def on_device(grad_out, route_ids, route_probs, gate_act, up_act, w_down):
    tok_count = grad_out.shape[0]
    top_count = route_ids.shape[1]
    expert_count = lax.axis_size("expert")
    tensor_count = lax.axis_size("tensor")
    local_experts = w_down.shape[0]
    experts = local_experts * expert_count
    slot_count = gate_act.shape[2]
    capacity = slot_count // expert_count
    model_width = grad_out.shape[1]
    quarter = model_width // tensor_count
    route_flat = route_ids.reshape(-1)
    expert_iota = lax.broadcasted_iota(jnp.int32, (1, experts), 1)
    matches = (route_flat[:, None] == expert_iota).astype(jnp.int32)
    earlier = jnp.cumsum(matches, axis=0) - matches
    position = jnp.sum(earlier * matches, axis=1)
    target = route_flat * capacity + position
    cell_iota = lax.broadcasted_iota(jnp.int32, (1, experts * capacity), 1)
    chosen = target[:, None] == cell_iota
    chosen_weight = chosen.astype(jnp.float32)
    token_chosen = jnp.sum(
        chosen_weight.reshape(tok_count, top_count, experts * capacity), axis=1
    ).astype(jnp.bfloat16)
    own_columns = lax.dynamic_slice_in_dim(grad_out, lax.axis_index("tensor") * quarter, quarter, 1)
    send_rows = jnp.einsum(
        "nf,nd->fd", token_chosen, own_columns, preferred_element_type=jnp.float32
    ).astype(jnp.bfloat16)
    send_probs = jnp.sum(
        chosen_weight * route_probs.reshape(-1).astype(jnp.float32)[:, None], axis=0
    ).astype(jnp.bfloat16)
    send_rows = send_rows.reshape(expert_count, local_experts, capacity, quarter)
    send_probs = send_probs.reshape(expert_count, local_experts, capacity)
    arrived_rows, arrived_probs = side_by_side((send_rows, send_probs), "expert", 0, 0, 3)
    gathered = lax.all_gather(arrived_rows, "tensor", axis=3, tiled=True)
    slot_rows = jnp.transpose(gathered, (1, 0, 2, 3)).reshape(
        local_experts, slot_count, model_width
    )
    slot_probs = (
        jnp.transpose(arrived_probs, (1, 0, 2))
        .reshape(local_experts, slot_count)
        .astype(jnp.float32)
    )
    gate_pre = gate_act[0].astype(jnp.float32)
    up_pre = up_act[0].astype(jnp.float32)
    grad_hidden = jnp.einsum("jsd,jfd->jsf", slot_rows, w_down, preferred_element_type=jnp.float32)
    sigmoid_gate = jax.nn.sigmoid(gate_pre)
    silu_gate = gate_pre * sigmoid_gate
    hidden = (silu_gate * up_pre).astype(jnp.bfloat16)
    partial_dot = jnp.sum(grad_hidden * hidden.astype(jnp.float32), axis=2)
    grad_scaled = slot_probs[:, :, None] * grad_hidden
    grad_up = (grad_scaled * silu_gate).astype(jnp.bfloat16)
    grad_gate = (
        grad_scaled * up_pre * sigmoid_gate * (1.0 + gate_pre * (1.0 - sigmoid_gate))
    ).astype(jnp.bfloat16)
    scaled_rows = (slot_probs[:, :, None] * slot_rows.astype(jnp.float32)).astype(jnp.bfloat16)
    partial_sum = jnp.einsum(
        "jsf,jsd->jfd", hidden, scaled_rows, preferred_element_type=jnp.float32
    )
    grad_weight = sent_and_summed(partial_sum.astype(jnp.bfloat16), "dp", 2).astype(jnp.bfloat16)
    prob_cells = jnp.transpose(
        partial_dot.reshape(local_experts, expert_count, capacity), (1, 0, 2)
    )
    prob_cells = taken_together(prob_cells, "tensor")
    returned = lax.all_to_all(prob_cells, "expert", split_axis=0, concat_axis=0, tiled=True)
    returned_flat = returned.reshape(-1)
    grad_probs = jnp.sum(jnp.where(chosen, returned_flat[None, :], 0.0), axis=1).reshape(
        tok_count, top_count
    )
    return (grad_gate[None], grad_up[None], grad_weight, grad_probs)


def solution(mesh):
    placed = (
        P(("expert", "dp"), None),
        P(("expert", "dp"), None),
        P(("expert", "dp"), None),
        P("dp", "expert", None, "tensor"),
        P("dp", "expert", None, "tensor"),
        P("expert", "tensor", None),
    )
    return jax.shard_map(
        on_device,
        mesh=mesh,
        in_specs=placed,
        out_specs=(
            P("dp", "expert", None, "tensor"),
            P("dp", "expert", None, "tensor"),
            P("expert", "tensor", "dp"),
            P(("expert", "dp"), None),
        ),
        check_vma=False,
    )
```

profile of v0, /device:TPU:1, one launch (start us, length us, event | category | flops | bytes accessed | tf_op | source)
XLA Modules:
  0.0 422.9 jit_solution(5506175471182380034)
XLA Ops:
  7.2 0.0 copy-start
  7.2 0.0 all-gather.2.cloned.1.call-start
  7.2 0.9 copy.119
  8.2 0.1 eq.45
  8.2 0.1 eq.49
  8.3 0.1 copy.121
  8.4 0.2 fusion.19
  8.8 0.2 fusion.18
  9.0 0.1 reduce_sum.69
  9.1 0.8 copy.125
  9.9 0.1 reshape.100
  10.0 0.1 copy.123
  10.0 0.7 multiply_add_fusion
  10.7 0.1 copy.124
  10.8 0.5 convert_reduce_fusion
  11.4 0.2 select_reduce_fusion.1
  11.6 0.3 convert_element_type.121
  11.9 2.7 convolution_convert_fusion
  14.5 3.7 reshape.95
  18.2 2.2 pad_maximum_fusion
  20.5 1.4 copy.127
  21.9 200.1 %all_to_all.20 = bf16[64,2,6,1025]{3,1,2,0:T(2,128)(2,1)S(1)} all-to-all(bf16[64,2,6,1025]{3,1,2,0:T(2,128)(2,1)S(1)} %copy.127), channel_id=1, replica_groups=mesh['tensor'=4,'expert'=64,'dp'=4] {'expert'}, dimensions={0} | all-to-all | bytes 3148800 | tf_op jit(solution)/shard_map/all_to_all | solution.py:11
  222.0 0.0 copy-start.1
  222.0 1.2 copy-done.1
  223.2 2.3 slice.18
  225.5 0.0 all-gather.2.cloned.1.call-update
  225.5 1.1 slice.17
  226.6 0.2 copy.137
  226.8 0.1 copy.129
  226.9 0.1 reshape.101
  227.0 0.1 copy.131
  227.2 67.5 %all-gather.2.cloned.1.call-done = bf16[64,2,6,4096]{3,1,2,0:T(2,128)(2,1)} async-done(((bf16[64,2,6,1024]{3,1,2,0:T(2,128)(2,1)}), bf16[64,2,6,4096]{3,1,2,0:T(2,128)(2,1)}) %all-gather.2.cloned.1.call-update) | async-done | bytes 6291472 | tf_op jit(solution)/shard_map/all_gather | solution.py:77
  294.7 0.0 copy-done
  294.7 11.2 %multiply_reduce_fusion = (f32[2,384]{1,0:T(2,128)S(1)}, bf16[1,2,384,192]{2,3,1,0:T(8,128)(2,1)}, bf16[1,2,384,192]{2,3,1,0:T(8,128)(2,1)}) fusion(bf16[1,2,384,192]{2,3,1,0:T(8,128)(2,1)} %param.10, bf16[1,2,384,192]{2,3,1,0:T(8,128)(2,1)} %param.9, f32[2,384]{1,0:T(2,128)S(1)} %reshape.101, bf16[2,192,4096]{2,1,0:T(8,128)(2,1)S(1)} %copy-done, ...), kind=kOutput, calls=%fused_computation.27 | convolution fusion | flops 1211055360 | bytes 10622976 | tf_op jit(solution)/shard_map/jsd,jfd->jsf/dot_general | solution.py:88
  305.9 0.1 reshape.98
  306.0 0.1 copy.134
  306.1 0.7 reshape.105
  306.8 3.4 all-to-all-start.2
  310.2 9.1 %multiply_convert_fusion = bf16[2,384,4096]{2,0,1:T(2,128)(2,1)} fusion(f32[2,384]{0,1:T(8,128)S(1)} %copy.131, bf16[64,2,6,4096]{3,1,2,0:T(2,128)(2,1)} %all-gather.2.cloned.1.call-done), kind=kLoop, calls=%fused_computation | loop fusion | flops 9437184 | bytes 12585984 | tf_op jit(solution)/shard_map/convert_element_type | solution.py:98
  319.4 0.0 all-to-all-done.2
  319.4 0.5 broadcast.50
  319.9 0.7 reduce.1
  320.6 0.1 reshape.106
  320.7 0.7 copy.135
  321.4 25.4 %all-to-all-start.3 = ((f32[64,2,6]{2,1,0:T(2,128)}), f32[64,2,6]{2,1,0:T(2,128)S(1)}, u32[]{:S(2)}, u32[]{:S(2)}) async-start(f32[64,2,6]{2,1,0:T(2,128)} %copy.135), calls=%async_computation.3 | async-start | bytes 131072 | tf_op jit(solution)/shard_map/all_to_all | solution.py:107
  346.8 10.6 %fusion.4 = bf16[2,192,4096]{2,1,0:T(8,128)(2,1)S(1)} fusion(bf16[2,384,4096]{2,0,1:T(2,128)(2,1)} %multiply_convert_fusion, bf16[1,2,384,192]{2,3,1,0:T(8,128)(2,1)} %param.10, bf16[1,2,384,192]{2,3,1,0:T(8,128)(2,1)} %param.9), kind=kOutput, calls=%fused_computation.5 | convolution fusion | flops 1210712064 | bytes 10027008 | tf_op jit(solution)/shard_map/jsf,jsd->jfd/dot_general | solution.py:99
  357.5 2.0 copy.148
  359.5 12.4 %all-to-all-done.3 = f32[64,2,6]{2,1,0:T(2,128)S(1)} async-done(((f32[64,2,6]{2,1,0:T(2,128)}), f32[64,2,6]{2,1,0:T(2,128)S(1)}, u32[]{:S(2)}, u32[]{:S(2)}) %all-to-all-start.3) | async-done | bytes 3104 | tf_op jit(solution)/shard_map/all_to_all | solution.py:107
  371.9 4.6 %all-to-all-start.1 = ((bf16[4,2,192,1024]{3,2,1,0:T(8,128)(2,1)}), bf16[4,2,192,1024]{3,2,1,0:T(8,128)(2,1)}, u32[]{:S(2)}, u32[]{:S(2)}) async-start(bf16[4,2,192,1024]{3,2,1,0:T(8,128)(2,1)} %bitcast.62), calls=%async_computation.1 | async-start | bytes 6291456 | tf_op jit(solution)/shard_map/all_to_all | solution.py:30
  376.5 0.1 broadcast_in_dim.28
  376.6 0.3 select_reduce_fusion
  377.0 0.1 reshape.99
  377.1 0.7 copy.136
  377.7 34.7 %all-to-all-done.1 = bf16[4,2,192,1024]{3,2,1,0:T(8,128)(2,1)} async-done(((bf16[4,2,192,1024]{3,2,1,0:T(8,128)(2,1)}), bf16[4,2,192,1024]{3,2,1,0:T(8,128)(2,1)}, u32[]{:S(2)}, u32[]{:S(2)}) %all-to-all-start.1) | async-done | bytes 3145760 | tf_op jit(solution)/shard_map/all_to_all | solution.py:30
  412.4 3.6 reduce_sum.72
  (10 shorter events, 0.1 us)
Async XLA Ops:
  7.2 287.5 %copy-start = (bf16[2,192,4096]{2,1,0:T(8,128)(2,1)S(1)}, bf16[2,192,4096]{2,1,0:T(8,128)(2,1)}, u32[]{:S(2)}) copy-start(bf16[2,192,4096]{2,1,0:T(8,128)(2,1)} %param.11) | copy-start | bytes 9437188
  7.2 287.5 %all-gather.2.cloned.1.call-start = ((), (), s32[]{:S(2)}) async-start(), calls=%async_computation.4 | async-start | bytes 7864320 | tf_op jit(solution)/shard_map/all_gather | solution.py:77
  222.0 1.2 copy-start.1
  306.8 12.6 %all-to-all-start.2 = ((f32[4,1,768]{2,1,0:T(1,128)}), f32[4,1,768]{2,1,0:T(1,128)S(1)}, u32[]{:S(2)}, u32[]{:S(2)}) async-start(f32[4,1,768]{2,1,0:T(1,128)} %reshape.105), calls=%async_computation.2 | async-start | bytes 24576 | tf_op jit(solution)/shard_map/all_to_all | solution.py:36
  321.4 50.4 %all-to-all-start.3 = ((f32[64,2,6]{2,1,0:T(2,128)}), f32[64,2,6]{2,1,0:T(2,128)S(1)}, u32[]{:S(2)}, u32[]{:S(2)}) async-start(f32[64,2,6]{2,1,0:T(2,128)} %copy.135), calls=%async_computation.3 | async-start | bytes 131072 | tf_op jit(solution)/shard_map/all_to_all | solution.py:107
  371.9 40.6 %all-to-all-start.1 = ((bf16[4,2,192,1024]{3,2,1,0:T(8,128)(2,1)}), bf16[4,2,192,1024]{3,2,1,0:T(8,128)(2,1)}, u32[]{:S(2)}, u32[]{:S(2)}) async-start(bf16[4,2,192,1024]{3,2,1,0:T(8,128)(2,1)} %bitcast.62), calls=%async_computation.1 | async-start | bytes 6291456 | tf_op jit(solution)/shard_map/all_to_all | solution.py:30
Sparse Core Ops, SparseCore 0:
  225.6 68.9 all-gather.1
where the time goes:
time: 425 us; the launch traced here: 423 us
  blocking collectives  200 us (47%)
  waiting for transfers between devices  115 us (27%)
  starting transfers between devices  33.5 us (8%)
  matrix products  24.4 us (6%)
  local copies, waits for them, and re-layouts  18.1 us (4%)
  other arithmetic  18 us (4%)
  between operations  14.2 us (3%)
    all_to_all x1, blocking collectives, side_by_side(): lax.all_to_all(both, axis, split_axis=split_dim, concat_axis=concat_dim,...  200 us
    all_gather x1, waiting for transfers between devices, on_device(): gathered = lax.all_gather(arrived_rows, 'tensor', axis=3, tiled=True)  67.5 us
    all_to_all x1, waiting for transfers between devices, sent_and_summed(): lax.all_to_all(tiles, axis, split_axis=0, concat_axis=0, tiled=True)  34.7 us
    all_to_all x1, starting transfers between devices, on_device(): lax.all_to_all(prob_cells, 'expert', split_axis=0, concat_axis=0, tiled=T...  25.4 us
    all_to_all x1, waiting for transfers between devices, on_device(): lax.all_to_all(prob_cells, 'expert', split_axis=0, concat_axis=0, tiled=T...  12.4 us
    dot_general x1, matrix products, on_device(): jnp.einsum('jsd,jfd->jsf', slot_rows, w_down, preferred_element_type=jnp....  11.2 us
    dot_general x1, matrix products, on_device(): jnp.einsum('jsf,jsd->jfd', hidden, scaled_rows, preferred_element_type=jn...  10.6 us
    convert_element_type x1, other arithmetic, on_device(): (slot_probs[:, :, None] * slot_rows.astype(jnp.float32)).astype(jnp.bfloa...  9.13 us
  transfers between devices with their start and end apart: 4, of which 3 were waited for; matrix products, arithmetic and copies ran while one was open for 6% of the time, Pallas kernels for 0%

commit v1 on v0

v1 whole, which is shorter than its diff:
```python
import jax
import jax.numpy as jnp
import numpy as np
from jax import lax
from jax.experimental import pallas as pl
from jax.experimental.pallas import tpu as pltpu
from jax.sharding import PartitionSpec as P

STRIDE = 8
OFFSETS = (0, -1, -2, -3, 1, 2, 3, 4)
SHIFTS = (-4, 3, -3, 2, -2, 1, -1, 0)
VMEM = pltpu.VMEM
LIMIT = 60 * 1024 * 1024


def spec():
    return pl.BlockSpec(memory_space=VMEM)


def call(body, outs, *args, scratch=(), flops=0, moved=0):
    smem = pl.BlockSpec(memory_space=pltpu.SMEM)
    return pl.pallas_call(
        body,
        out_shape=outs,
        in_specs=[smem if a.dtype == jnp.int32 and a.shape == (1,) else spec() for a in args],
        out_specs=jax.tree.map(lambda _: spec(), outs),
        scratch_shapes=list(scratch),
        compiler_params=pltpu.CompilerParams(vmem_limit_bytes=LIMIT),
        cost_estimate=pl.CostEstimate(flops=flops, bytes_accessed=moved, transcendentals=0),
    )(*args)


def dot(a, b):
    return jnp.dot(a, b, preferred_element_type=jnp.float32)


def dot_nt(a, b):
    return lax.dot_general(a, b, (((1,), (1,)), ((), ())), preferred_element_type=jnp.float32)


def earlier_matrix(n, block):
    row = lax.broadcasted_iota(jnp.int32, (n, n), 0)
    col = lax.broadcasted_iota(jnp.int32, (n, n), 1)
    same = (row // block) == (col // block)
    return jnp.where((row < col) & same, 1.0, 0.0).astype(jnp.bfloat16)


def pack_body(t_ref, x_ref, ids_ref, probs_ref, out_ref):
    t = t_ref[0]
    toks = x_ref.shape[0]
    for c in range(8):
        start = pl.multiple_of((c // 2) * 1024 + t * 256 + (c % 2) * 128, 128)
        out_ref[c * toks : (c + 1) * toks, :] = x_ref[:, pl.ds(start, 128)]
    both = jnp.concatenate(
        [ids_ref[...].astype(jnp.float32), probs_ref[...].astype(jnp.float32)], axis=1
    )
    out_ref[8 * toks : 8 * toks + 8, :] = both.astype(jnp.bfloat16)


def select_body(s_ref, onehot_ref, code_ref, exp_ref, *refs):
    blocks, outs = refs[:9], refs[9:]
    s = s_ref[0]
    routes = [b[512:520, :].astype(jnp.float32) for b in blocks[:7]]
    routes.append(blocks[8][256:264, :].astype(jnp.float32))
    ids = jnp.concatenate([r[:, :64] for r in routes], axis=1)
    probs = jnp.concatenate([r[:, 64:] for r in routes], axis=1)
    base = exp_ref[...]
    mine = (2 * s + base) & 127
    mine = mine.astype(jnp.float32)
    match = jnp.zeros((16, 512), jnp.float32)
    prob = jnp.zeros((16, 512), jnp.float32)
    for k in range(8):
        hit = ids[k : k + 1, :] == mine
        match = jnp.where(hit, 1.0, match)
        prob = jnp.where(hit, probs[k : k + 1, :], prob)
    before = earlier_matrix(128, 64)
    low = match.astype(jnp.bfloat16)
    pos = jnp.concatenate(
        [dot(low[:, 128 * c : 128 * (c + 1)], before) for c in range(4)], axis=1
    )
    block = lax.broadcasted_iota(jnp.int32, (16, 512), 1) >> 6
    code = jnp.where(match > 0.0, pos + 6.0 * block.astype(jnp.float32), -1.0)
    onehot = onehot_ref[...]
    spread = dot(onehot, code.astype(jnp.bfloat16))
    chosen = spread == code_ref[...]
    pick = jnp.where(chosen, 1.0, 0.0).astype(jnp.bfloat16)
    weights = dot(onehot, prob.astype(jnp.bfloat16))
    weighted = jnp.where(chosen, weights, 0.0).astype(jnp.bfloat16)
    slot_probs = dot_nt(jnp.ones((8, 512), jnp.bfloat16), weighted).astype(jnp.bfloat16)
    for c in range(8):
        parts = [b[c * 64 : (c + 1) * 64, :] for b in blocks[:7]]
        last = blocks[7] if c < 4 else blocks[8]
        parts.append(last[(c % 4) * 64 : (c % 4 + 1) * 64, :])
        rows = dot(pick, jnp.concatenate(parts, axis=0)).astype(jnp.bfloat16)
        for v in range(8):
            outs[v][c * 96 : (c + 1) * 96, :] = rows[v * 96 : (v + 1) * 96, :]
    for v in range(8):
        for c in range(6):
            outs[v][768 + 8 * c : 776 + 8 * c, :] = slot_probs[:, 128 * c : 128 * (c + 1)]


def expert_body(s_ref, place_ref, *refs):
    pieces = refs[:8]
    w_ref, h_ref = refs[8:10]
    gh_ref, dots_ref, gw_ref, prob_ref = refs[10:14]
    arrived_ref, rows_ref, scaled_ref = refs[14:]
    s = s_ref[0]
    for v in range(8):
        for c in range(8):
            arrived_ref[v * 96 : (v + 1) * 96, c * 128 : (c + 1) * 128] = pieces[v][
                c * 96 : (c + 1) * 96, :
            ]
    lane = lax.broadcasted_iota(jnp.int32, (8, 768), 1)
    probs = jnp.zeros((8, 768), jnp.float32)
    for v in range(8):
        wide = jnp.concatenate(
            [pieces[v][768 + 8 * c : 776 + 8 * c, :] for c in range(6)], axis=1
        ).astype(jnp.float32)
        probs = jnp.where((lane >= v * 96) & (lane < (v + 1) * 96), wide, probs)
    target = ((s + place_ref[0:1, :]) & 63) * 6 + place_ref[1:2, :]
    row = lax.broadcasted_iota(jnp.int32, (768, 768), 0)
    perm = jnp.where(row == target, 1.0, 0.0).astype(jnp.bfloat16)
    low = probs.astype(jnp.bfloat16)
    prob_ref[...] = dot_nt(low, perm)
    column = dot_nt(perm, low)[:, :1]
    for c in range(4):
        part = dot(perm, arrived_ref[:, c * 256 : (c + 1) * 256])
        rows_ref[:, c * 256 : (c + 1) * 256] = part.astype(jnp.bfloat16)
        scaled_ref[:, c * 256 : (c + 1) * 256] = (part * column).astype(jnp.bfloat16)
    for e in range(2):
        total = jnp.zeros((1, 384), jnp.float32)
        for t in range(4):
            part = dot_nt(w_ref[t, e], rows_ref[e * 384 : (e + 1) * 384, :])
            gh_ref[t, e] = part.astype(jnp.bfloat16)
            total += jnp.sum(part * h_ref[t, e].astype(jnp.float32), axis=0, keepdims=True)
        dots_ref[e : e + 1, :] = total
    for e in range(2):
        for t in range(4):
            part = dot(h_ref[t, e], scaled_ref[e * 384 : (e + 1) * 384, :]).astype(jnp.bfloat16)
            for r in range(4):
                gw_ref[r, t, e] = part[:, r * 256 : (r + 1) * 256]


def local_body(prob_ref, gh_ref, gate_ref, up_ref, gg_ref, gu_ref):
    for e in range(2):
        total = gh_ref[0, e].astype(jnp.float32)
        for t in range(1, 4):
            total += gh_ref[t, e].astype(jnp.float32)
        gate = gate_ref[e].astype(jnp.float32)
        up = up_ref[e].astype(jnp.float32)
        sig = jax.nn.sigmoid(gate)
        scaled = prob_ref[0:1, e * 384 : (e + 1) * 384] * total
        gu_ref[e] = (scaled * (gate * sig)).astype(jnp.bfloat16)
        gg_ref[e] = (scaled * up * sig * (1.0 + gate * (1.0 - sig))).astype(jnp.bfloat16)


def lookup_body(ids_ref, table_ref, out_ref):
    experts, capacity = 128, 6
    ids = ids_ref[...]
    expert = lax.broadcasted_iota(jnp.int32, (experts, 64), 0)
    match = jnp.zeros((experts, 64), jnp.float32)
    for k in range(8):
        match = jnp.where(ids[k : k + 1, :] == expert, 1.0, match)
    pos = dot(match.astype(jnp.bfloat16), earlier_matrix(64, 64))
    value = jnp.zeros((experts, 64), jnp.float32)
    for j in range(capacity):
        value = jnp.where(pos == float(j), table_ref[:, j : j + 1], value)
    for k in range(8):
        hit = ids[k : k + 1, :] == expert
        out_ref[k : k + 1, :] = jnp.sum(jnp.where(hit, value, 0.0), axis=0, keepdims=True)


def shifted(x, by, count):
    return lax.ppermute(x, "expert", [(i, (i + by) % count) for i in range(count)])


def on_device(x, ids, probs, gate, up, w):
    bf16, f32, shape = jnp.bfloat16, jnp.float32, jax.ShapeDtypeStruct
    count = lax.axis_size("expert")
    s = lax.axis_index("expert").astype(jnp.int32).reshape(1)
    t = lax.axis_index("tensor").astype(jnp.int32).reshape(1)
    ids_t = ids.T
    gate_t = jnp.transpose(gate[0], (0, 2, 1))
    up_t = jnp.transpose(up[0], (0, 2, 1))

    packed = call(pack_body, shape((520, 128), bf16), t, x, ids_t, probs.T)

    w_send = w.reshape(2, 192, 4, 4, 256).transpose(3, 0, 1, 2, 4).reshape(4, 2, 192, 1024)
    w_all = lax.all_to_all(w_send, "tensor", split_axis=0, concat_axis=0, tiled=True)
    gate_f = gate_t.astype(f32)
    hidden = (gate_f * jax.nn.sigmoid(gate_f) * up_t.astype(f32)).astype(bf16)
    h_send = jnp.broadcast_to(hidden[None], (4, 2, 192, 384))
    h_all = lax.all_to_all(h_send, "tensor", split_axis=0, concat_axis=0, tiled=True)

    blocks = {0: packed}
    for step in (1, 2, 3):
        blocks[-step] = shifted(blocks[1 - step], STRIDE, count)
        blocks[step] = shifted(blocks[step - 1], -STRIDE, count)
    far_low = shifted(blocks[-3][:256], STRIDE, count)
    far_high = shifted(blocks[3][256:], -STRIDE, count)

    row = np.arange(768)
    place = row // 48
    onehot = np.zeros((768, 16), np.float32)
    onehot[row, place] = 1.0
    code = (row % 48).astype(np.float32)[:, None]
    shift = np.array(SHIFTS)
    expert = (2 * shift[:, None] + np.arange(2)[None, :]).reshape(16, 1).astype(np.int32)
    pieces = call(
        select_body,
        [shape((816, 128), bf16)] * 8,
        s,
        jnp.asarray(onehot, bf16),
        jnp.asarray(code),
        jnp.asarray(expert),
        *[blocks[o] for o in OFFSETS[:7]],
        far_low,
        far_high,
        flops=2 * 768 * 512 * 1024,
        moved=4 * 1024 * 1024,
    )
    pieces = [p if j == 0 else shifted(p, j, count) for p, j in zip(pieces, SHIFTS)]

    e, o, j = (row // 48) % 2, (row // 6) % 8, row % 6
    source = STRIDE * np.array(OFFSETS)[o] - shift[row // 96]
    tables = np.zeros((8, 768), np.int32)
    tables[0], tables[1] = source, e * 384 + j
    gh, dots, gw, prob = call(
        expert_body,
        [
            shape((4, 2, 192, 384), bf16),
            shape((2, 384), f32),
            shape((4, 4, 2, 192, 256), bf16),
            shape((8, 768), f32),
        ],
        s,
        jnp.asarray(tables),
        *pieces,
        w_all,
        h_all,
        scratch=[VMEM((768, 1024), bf16)] * 3,
        flops=6 * 10**9,
        moved=12 * 1024 * 1024,
    )

    gw_all = lax.all_to_all(gw, "dp", split_axis=0, concat_axis=0, tiled=True)
    gh_all = lax.all_to_all(gh, "tensor", split_axis=0, concat_axis=0, tiled=True)
    cells = jnp.transpose(dots.reshape(2, count, 6), (1, 0, 2)).reshape(count, 12)
    cells = jnp.broadcast_to(cells[None], (4, count, 12)).reshape(4 * count, 12)
    back = lax.all_to_all(cells, ("tensor", "expert"), split_axis=0, concat_axis=0, tiled=True)
    table = back.reshape(4, 2 * count, 6).sum(axis=0)

    grad_gate, grad_up = call(
        local_body,
        [shape((2, 192, 384), bf16)] * 2,
        prob,
        gh_all,
        gate_t,
        up_t,
        flops=10**7,
        moved=4 * 1024 * 1024,
    )
    grad_probs = call(lookup_body, shape((8, 64), f32), ids_t, table).T
    summed = gw_all.astype(f32).sum(axis=0).astype(bf16)
    mine = lax.all_to_all(summed, "tensor", split_axis=0, concat_axis=0, tiled=True)
    grad_w = jnp.transpose(mine, (1, 2, 0, 3)).reshape(2, 192, 1024)
    return (
        jnp.transpose(grad_gate, (0, 2, 1))[None],
        jnp.transpose(grad_up, (0, 2, 1))[None],
        grad_w,
        grad_probs,
    )


def solution(mesh):
    act = P("dp", "expert", None, "tensor")
    tok = P(("expert", "dp"), None)
    return jax.shard_map(
        on_device,
        mesh=mesh,
        in_specs=(tok, tok, tok, act, act, P("expert", "tensor", None)),
        out_specs=(act, act, P("expert", "tensor", "dp"), tok),
        check_vma=False,
    )
```

time: 425 us -> 288 us (0.68)
  blocking collectives: 200 us -> 89.1 us
  starting transfers between devices: 33.5 us -> 105 us
  waiting for transfers between devices: 115 us -> 48.7 us
  matrix products: 24.4 us -> 0 us
  Pallas kernels: 0 us -> 21.5 us
  other arithmetic: 18 us -> 4.61 us
  between operations: 14.2 us -> 0.94 us
    all_to_all x1 -> x2, blocking collectives: 200 us -> 89.1 us  [the longest x1 49.2 us: on_device(): lax.all_to_all(cells, ('tensor', 'expert'), split_axis=0, concat_axis=0,...]
    ppermute x0 -> x15, starting transfers between devices: none -> 87.9 us  [shifted(): lax.ppermute(x, 'expert', [(i, (i + by) % count) for i in range(count)])]
    all_gather x1 -> x0, waiting for transfers between devices: 67.5 us -> none  [on_device(): gathered = lax.all_gather(arrived_rows, 'tensor', axis=3, tiled=True)]
    ppermute x0 -> x15, waiting for transfers between devices: none -> 28.2 us  [shifted(): lax.ppermute(x, 'expert', [(i, (i + by) % count) for i in range(count)])]
    all_to_all x3 -> x4, waiting for transfers between devices: 47.1 us -> 20.5 us  [the longest x1 15.1 us: on_device(): lax.all_to_all(gh, 'tensor', split_axis=0, concat_axis=0, tiled=True)]
    dot_general x3 -> x0, matrix products: 24.4 us -> none  [the longest x1 11.2 us: on_device(): jnp.einsum('jsd,jfd->jsf', slot_rows, w_down, preferred_element_type=jnp....]
    pallas_call x0 -> x5, Pallas kernels: none -> 21.5 us  [call(): pl.pallas_call(body, out_shape=outs, in_specs=[smem if a.dtype == jnp.int...]
    all_to_all x3 -> x4, starting transfers between devices: 33.5 us -> 17 us  [the longest x1 5 us: on_device(): lax.all_to_all(h_send, 'tensor', split_axis=0, concat_axis=0, tiled=True)]
  transfers between devices with their start and end apart: 4 -> 19, of which waited for: 3 -> 11; matrix products, arithmetic and copies ran while one was open for 6% -> 5% of each run, Pallas kernels for 0% -> 4%
where the time goes in v1:
time: 288 us; the launch traced here: 287 us
  starting transfers between devices  105 us (36%)
  blocking collectives  89.1 us (31%)
  waiting for transfers between devices  48.7 us (17%)
  Pallas kernels  21.5 us (7%)
  local copies, waits for them, and re-layouts  17.1 us (6%)
  other arithmetic  4.61 us (2%)
    ppermute x15, starting transfers between devices, shifted(): lax.ppermute(x, 'expert', [(i, (i + by) % count) for i in range(count)])  87.9 us
    all_to_all x1, blocking collectives, on_device(): lax.all_to_all(cells, ('tensor', 'expert'), split_axis=0, concat_axis=0,...  49.2 us
    all_to_all x1, blocking collectives, on_device(): gw_all = lax.all_to_all(gw, 'dp', split_axis=0, concat_axis=0, tiled=True)  39.9 us
    ppermute x15, waiting for transfers between devices, shifted(): lax.ppermute(x, 'expert', [(i, (i + by) % count) for i in range(count)])  28.2 us
    pallas_call x5, Pallas kernels, call(): pl.pallas_call(body, out_shape=outs, in_specs=[smem if a.dtype == jnp.int...  21.5 us
    all_to_all x1, waiting for transfers between devices, on_device(): lax.all_to_all(gh, 'tensor', split_axis=0, concat_axis=0, tiled=True)  15.1 us
    reshape x3, local copies, waits for them, and re-layouts, on_device(): w.reshape(2, 192, 4, 4, 256).transpose(3, 0, 1, 2, 4)  10.9 us
  transfers between devices with their start and end apart: 19, of which 11 were waited for; matrix products, arithmetic and copies ran while one was open for 5% of the time, Pallas kernels for 4%

profile of v1, /device:TPU:1, one launch (start us, length us, event | category | flops | bytes accessed | tf_op | source)
XLA Modules:
  0.0 286.9 jit_solution(9217992808413454444)
XLA Ops:
  0.6 1.4 fusion.4
  2.0 1.1 broadcast_in_dim.19
  3.2 5.0 %all-to-all-start.1 = ((bf16[4,2,192,384]{3,2,1,0:T(8,128)(2,1)}), bf16[4,2,192,384]{3,2,1,0:T(8,128)(2,1)}, u32[]{:S(2)}, u32[]{:S(2)}) async-start(bf16[4,2,192,384]{3,2,1,0:T(8,128)(2,1)} %broadcast_in_dim.19), calls=%async_computation.1 | async-start | bytes 2359296 | tf_op jit(solution)/shard_map/all_to_all | solution.py:193
  8.2 3.9 %reshape.38 = bf16[2,192,4,4,256]{4,3,2,1,0:T(4,128)(2,1)} reshape(bf16[2,192,4096]{2,1,0:T(8,128)(2,1)S(1)} %copy-done) | data formatting | bytes 6291456 | tf_op jit(solution)/shard_map/reshape | solution.py:188
  12.1 3.1 %copy.27 = bf16[2,192,4,4,256]{4,2,1,0,3:T(4,128)(2,1)S(1)} copy(bf16[2,192,4,4,256]{4,3,2,1,0:T(4,128)(2,1)} %reshape.38) | data formatting | bytes 6291456 | tf_op jit(solution)/shard_map/reshape | solution.py:188
  15.2 3.9 %reshape.39 = bf16[4,2,192,1024]{3,2,1,0:T(8,128)(2,1)} reshape(bf16[4,2,192,4,256]{4,3,2,1,0:T(4,128)(2,1)S(1)} %bitcast.29) | data formatting | bytes 6291456 | tf_op jit(solution)/shard_map/reshape | solution.py:188
  19.1 0.0 all-to-all-done.1.refs_9_
  19.1 4.3 %all-to-all-start = ((bf16[4,2,192,1024]{3,2,1,0:T(8,128)(2,1)}), bf16[4,2,192,1024]{3,2,1,0:T(8,128)(2,1)S(1)}, u32[]{:S(2)}, u32[]{:S(2)}) async-start(bf16[4,2,192,1024]{3,2,1,0:T(8,128)(2,1)} %reshape.39), calls=%async_computation | async-start | bytes 6291456 | tf_op jit(solution)/shard_map/all_to_all | solution.py:189
  23.4 1.8 shard_map.129.refs_0_
  25.2 24.1 %collective-permute-start.3 = (bf16[520,128]{1,0:T(8,128)(2,1)}, bf16[520,128]{1,0:T(8,128)(2,1)S(1)}, u32[]{:S(2)}, u32[]{:S(2)}) collective-permute-start(bf16[520,128]{1,0:T(8,128)(2,1)} %shard_map.129.refs_0_), channel_id=1, source_target_pairs={{0,224},{4,228},{8,232},{12,236},{16,240},{20,244},{24,248},{28,25... | collective-permute-start | bytes 399368 | tf_op jit(solution)/shard_map/ppermute | solution.py:174
  49.3 1.9 collective-permute-start
  51.2 2.7 collective-permute-done.3.refs_4_
  53.9 14.9 %collective-permute-start.4 = (bf16[520,128]{1,0:T(8,128)(2,1)S(1)}, bf16[520,128]{1,0:T(8,128)(2,1)S(1)}, u32[]{:S(2)}, u32[]{:S(2)}) collective-permute-start(bf16[520,128]{1,0:T(8,128)(2,1)S(1)} %collective-permute-done.3.refs_4_), channel_id=1, source_target_pairs={{0,224},{4,228},{8,232},{12,236},{16,240},{20,244},{24,248},{28,25... | collective-permute-start | bytes 399368 | tf_op jit(solution)/shard_map/ppermute | solution.py:174
  68.9 0.0 collective-permute-done.refs_1_
  68.9 1.9 collective-permute-start.1
  70.8 4.5 %collective-permute-done.4.refs_5_ = bf16[520,128]{1,0:T(8,128)(2,1)S(1)} collective-permute-done((bf16[520,128]{1,0:T(8,128)(2,1)S(1)}, bf16[520,128]{1,0:T(8,128)(2,1)S(1)}, u32[]{:S(2)}, u32[]{:S(2)}) %collective-permute-start.4) | collective-permute-done | bytes 133152 | tf_op jit(solution)/shard_map/ppermute | solution.py:174
  75.3 8.1 %collective-permute-start.5 = (bf16[520,128]{1,0:T(8,128)(2,1)S(1)}, bf16[520,128]{1,0:T(8,128)(2,1)S(1)}, u32[]{:S(2)}, u32[]{:S(2)}) collective-permute-start(bf16[520,128]{1,0:T(8,128)(2,1)S(1)} %collective-permute-done.4.refs_5_), channel_id=1, source_target_pairs={{0,224},{4,228},{8,232},{12,236},{16,240},{20,244},{24,248},{28,25... | collective-permute-start | bytes 399368 | tf_op jit(solution)/shard_map/ppermute | solution.py:174
  83.5 1.3 collective-permute-done.1.refs_2_
  84.8 1.9 collective-permute-start.2
  86.8 5.0 %collective-permute-done.5.refs_6_ = bf16[520,128]{1,0:T(8,128)(2,1)S(1)} collective-permute-done((bf16[520,128]{1,0:T(8,128)(2,1)S(1)}, bf16[520,128]{1,0:T(8,128)(2,1)S(1)}, u32[]{:S(2)}, u32[]{:S(2)}) %collective-permute-start.5) | collective-permute-done | bytes 133152 | tf_op jit(solution)/shard_map/ppermute | solution.py:174
  91.7 6.7 %collective-permute-start.7 = (bf16[264,128]{1,0:T(8,128)(2,1)S(1)}, bf16[264,128]{1,0:T(8,128)(2,1)}, u32[]{:S(2)}, u32[]{:S(2)}) collective-permute-start(bf16[264,128]{1,0:T(8,128)(2,1)S(1)} %slice.9), channel_id=1, source_target_pairs={{0,224},{4,228},{8,232},{12,236},{16,240},{20,244},{24,248},{28,25... | collective-permute-start | bytes 202760 | tf_op jit(solution)/shard_map/ppermute | solution.py:174
  98.4 0.9 collective-permute-done.2.refs_3_
  99.3 4.8 %collective-permute-start.6 = (bf16[256,128]{1,0:T(8,128)(2,1)S(1)}, bf16[256,128]{1,0:T(8,128)(2,1)}, u32[]{:S(2)}, u32[]{:S(2)}) collective-permute-start(bf16[256,128]{1,0:T(8,128)(2,1)S(1)} %slice.8), channel_id=1, source_target_pairs={{0,32},{4,36},{8,40},{12,44},{16,48},{20,52},{24,56},{28,60},{32,6... | collective-permute-start | bytes 196616 | tf_op jit(solution)/shard_map/ppermute | solution.py:174
  104.2 4.3 %collective-permute-done.6.refs_7_ = bf16[256,128]{1,0:T(8,128)(2,1)} collective-permute-done((bf16[256,128]{1,0:T(8,128)(2,1)S(1)}, bf16[256,128]{1,0:T(8,128)(2,1)}, u32[]{:S(2)}, u32[]{:S(2)}) %collective-permute-start.6) | collective-permute-done | bytes 65568 | tf_op jit(solution)/shard_map/ppermute | solution.py:174
  108.5 0.0 collective-permute-done.7.refs_8_
  108.5 0.0 copy-done.2
  108.5 5.0 %shard_map.130 = (bf16[816,128]{1,0:T(8,128)(2,1)}, bf16[816,128]{1,0:T(8,128)(2,1)}, bf16[816,128]{1,0:T(8,128)(2,1)}, bf16[816,128]{1,0:T(8,128)(2,1)}, bf16[8...) custom-call(s32[1]{0:T(128)} %bitcast.s_ref, ...), custom_call_target="tpu_custom_call" | custom-call | flops 805306368 | bytes 4194304 | tf_op jit(solution)/shard_map/pallas_call | solution.py:22
  113.6 8.9 %collective-permute-start.10 = (bf16[816,128]{1,0:T(8,128)(2,1)}, bf16[816,128]{1,0:T(8,128)(2,1)S(1)}, u32[]{:S(2)}, u32[]{:S(2)}) collective-permute-start(bf16[816,128]{1,0:T(8,128)(2,1)} %get-tuple-element.20), channel_id=1, source_target_pairs={{0,244},{4,248},{8,252},{12,0},{16,4},{20,8},{24,12},{28,16},{32,2... | collective-permute-start | bytes 626696 | tf_op jit(solution)/shard_map/ppermute | solution.py:174
  122.5 1.9 collective-permute-start.11
  124.4 4.6 %collective-permute-start.12 = (bf16[816,128]{1,0:T(8,128)(2,1)}, bf16[816,128]{1,0:T(8,128)(2,1)S(1)}, u32[]{:S(2)}, u32[]{:S(2)}) collective-permute-start(bf16[816,128]{1,0:T(8,128)(2,1)} %get-tuple-element.22), channel_id=1, source_target_pairs={{0,248},{4,252},{8,0},{12,4},{16,8},{20,12},{24,16},{28,20},{32,24... | collective-permute-start | bytes 626696 | tf_op jit(solution)/shard_map/ppermute | solution.py:174
  129.0 0.4 collective-permute-start.13
  129.4 0.1 collective-permute-start.14
  129.5 0.0 collective-permute-done.10.refs_2_
  129.5 4.1 %collective-permute-start.8 = (bf16[816,128]{1,0:T(8,128)(2,1)}, bf16[816,128]{1,0:T(8,128)(2,1)S(1)}, u32[]{:S(2)}, u32[]{:S(2)}) collective-permute-start(bf16[816,128]{1,0:T(8,128)(2,1)} %get-tuple-element.18), channel_id=1, source_target_pairs={{0,240},{4,244},{8,248},{12,252},{16,0},{20,4},{24,8},{28,12},{32,... | collective-permute-start | bytes 626696 | tf_op jit(solution)/shard_map/ppermute | solution.py:174
  133.7 0.0 collective-permute-done.11.refs_3_
  133.7 3.4 %collective-permute-start.9 = (bf16[816,128]{1,0:T(8,128)(2,1)}, bf16[816,128]{1,0:T(8,128)(2,1)}, u32[]{:S(2)}, u32[]{:S(2)}) collective-permute-start(bf16[816,128]{1,0:T(8,128)(2,1)} %get-tuple-element.19), channel_id=1, source_target_pairs={{0,12},{4,16},{8,20},{12,24},{16,28},{20,32},{24,36},{28,40},{32,4... | collective-permute-start | bytes 626696 | tf_op jit(solution)/shard_map/ppermute | solution.py:174
  137.1 0.0 collective-permute-done.12.refs_4_
  137.1 0.0 collective-permute-done.13.refs_5_
  137.1 0.0 copy-start.7
  137.1 1.4 collective-permute-done.14.refs_6_
  138.5 4.9 %collective-permute-done.8.refs_0_ = bf16[816,128]{1,0:T(8,128)(2,1)S(1)} collective-permute-done((bf16[816,128]{1,0:T(8,128)(2,1)}, bf16[816,128]{1,0:T(8,128)(2,1)S(1)}, u32[]{:S(2)}, u32[]{:S(2)}) %collective-permute-start.8) | collective-permute-done | bytes 208928 | tf_op jit(solution)/shard_map/ppermute | solution.py:174
  143.3 0.0 copy-start.9
  143.4 0.7 copy-done.9
  144.0 3.2 %collective-permute-done.9.refs_1_ = bf16[816,128]{1,0:T(8,128)(2,1)} collective-permute-done((bf16[816,128]{1,0:T(8,128)(2,1)}, bf16[816,128]{1,0:T(8,128)(2,1)}, u32[]{:S(2)}, u32[]{:S(2)}) %collective-permute-start.9) | collective-permute-done | bytes 208928 | tf_op jit(solution)/shard_map/ppermute | solution.py:174
  147.3 0.0 all-to-all-done.refs_8_
  147.3 1.6 copy-done.1
  148.9 10.4 %shard_map.131 = (bf16[4,2,192,384]{3,2,1,0:T(8,128)(2,1)}, f32[2,384]{1,0:T(2,128)}, bf16[4,4,2,192,256]{4,3,2,1,0:T(8,128)(2,1)}, f32[8,768]{1,0:T(8,128)}) custom-call(s32[1]{0:T(128)} %bitcast.s_ref, s32[8,768]{1,0:T(8,128)} %constant.28.clone.place_ref, bf16[816,128]{1,0:T(8,128)(2,1)} %copy-done.9, bf16[816,128]{1,0:T(8,128)(2,1)} %collective-permute-done.9.refs_1_, ...), custom_call_target="tpu_custom_call" | custom-call | flops 6000000000 | bytes 12582912 | tf_op jit(solution)/shard_map/pallas_call | solution.py:22
  159.3 0.8 reshape.41
  160.2 0.1 copy.23
  160.3 0.1 copy.24
  160.4 49.2 %all_to_all.34 = f32[256,1,12]{2,1,0:T(1,128)S(1)} all-to-all(f32[256,1,12]{2,1,0:T(1,128)S(1)} %bitcast.34), channel_id=1, replica_groups=mesh['tensor'=4,'expert'=64,'dp'=4] {'tensor','expert'}, dimensions={0} | all-to-all | bytes 24576 | tf_op jit(solution)/shard_map/all_to_all | solution.py:250
  209.6 39.9 %all_to_all.35 = bf16[4,4,2,192,256]{4,3,2,1,0:T(8,128)(2,1)S(1)} all-to-all(bf16[4,4,2,192,256]{4,3,2,1,0:T(8,128)(2,1)} %get-tuple-element.30), channel_id=1, replica_groups=mesh['tensor'=4,'expert'=64,'dp'=4] {'dp'}, dimensions={0} | all-to-all | bytes 6291456 | tf_op jit(solution)/shard_map/all_to_all | solution.py:246
  249.5 4.3 %all-to-all-start.2 = ((bf16[4,2,192,384]{3,2,1,0:T(8,128)(2,1)}), bf16[4,2,192,384]{3,2,1,0:T(8,128)(2,1)}, u32[]{:S(2)}, u32[]{:S(2)}) async-start(bf16[4,2,192,384]{3,2,1,0:T(8,128)(2,1)} %get-tuple-element.27), calls=%async_computation.2 | async-start | bytes 2359296 | tf_op jit(solution)/shard_map/all_to_all | solution.py:247
  253.7 1.6 reduce_sum.21
  255.3 15.1 %all-to-all-done.2.gh_ref = bf16[4,2,192,384]{3,2,1,0:T(8,128)(2,1)} async-done(((bf16[4,2,192,384]{3,2,1,0:T(8,128)(2,1)}), bf16[4,2,192,384]{3,2,1,0:T(8,128)(2,1)}, u32[]{:S(2)}, u32[]{:S(2)}) %all-to-all-start.2) | async-done | bytes 1179680 | tf_op jit(solution)/shard_map/all_to_all | solution.py:247
  270.4 3.5 %all-to-all-start.4 = ((bf16[4,2,192,256]{3,2,1,0:T(8,128)(2,1)}), bf16[4,2,192,256]{3,2,1,0:T(8,128)(2,1)S(1)}, u32[]{:S(2)}, u32[]{:S(2)}) async-start(bf16[4,2,192,256]{3,2,1,0:T(8,128)(2,1)} %reduce_sum.21), calls=%async_computation.4 | async-start | bytes 1572864 | tf_op jit(solution)/shard_map/all_to_all | solution.py:265
  274.0 0.5 broadcast.9
  274.5 1.0 reduce.4
  275.4 0.1 reshape.42
  275.5 0.7 reduce_sum.22.table_ref
  276.2 1.7 shard_map.133
  277.9 2.6 shard_map.132
  280.5 5.4 %all-to-all-done.4 = bf16[4,2,192,256]{3,2,1,0:T(8,128)(2,1)S(1)} async-done(((bf16[4,2,192,256]{3,2,1,0:T(8,128)(2,1)}), bf16[4,2,192,256]{3,2,1,0:T(8,128)(2,1)S(1)}, u32[]{:S(2)}, u32[]{:S(2)}) %all-to-all-start.4) | async-done | bytes 786464 | tf_op jit(solution)/shard_map/all_to_all | solution.py:265
  285.9 1.0 copy.25
  (27 shorter events, 0.1 us)
Async XLA Ops:
  0.6 7.5 %copy-start = (bf16[2,192,4096]{2,1,0:T(8,128)(2,1)S(1)}, bf16[2,192,4096]{2,1,0:T(8,128)(2,1)}, u32[]{:S(2)}) copy-start(bf16[2,192,4096]{2,1,0:T(8,128)(2,1)} %param.15) | copy-start | bytes 9437188
  3.2 16.0 %all-to-all-start.1 = ((bf16[4,2,192,384]{3,2,1,0:T(8,128)(2,1)}), bf16[4,2,192,384]{3,2,1,0:T(8,128)(2,1)}, u32[]{:S(2)}, u32[]{:S(2)}) async-start(bf16[4,2,192,384]{3,2,1,0:T(8,128)(2,1)} %broadcast_in_dim.19), calls=%async_computation.1 | async-start | bytes 2359296 | tf_op jit(solution)/shard_map/all_to_all | solution.py:193
  19.1 128.1 %all-to-all-start = ((bf16[4,2,192,1024]{3,2,1,0:T(8,128)(2,1)}), bf16[4,2,192,1024]{3,2,1,0:T(8,128)(2,1)S(1)}, u32[]{:S(2)}, u32[]{:S(2)}) async-start(bf16[4,2,192,1024]{3,2,1,0:T(8,128)(2,1)} %reshape.39), calls=%async_computation | async-start | bytes 6291456 | tf_op jit(solution)/shard_map/all_to_all | solution.py:189
  25.2 28.7 %collective-permute-start.3 = (bf16[520,128]{1,0:T(8,128)(2,1)}, bf16[520,128]{1,0:T(8,128)(2,1)S(1)}, u32[]{:S(2)}, u32[]{:S(2)}) collective-permute-start(bf16[520,128]{1,0:T(8,128)(2,1)} %shard_map.129.refs_0_), channel_id=1, source_target_pairs={{0,224},{4,228},{8,232},{12,236},{16,240},{20,244},{24,248},{28,25... | collective-permute-start | bytes 399368 | tf_op jit(solution)/shard_map/ppermute | solution.py:174
  49.3 19.6 %collective-permute-start = (bf16[520,128]{1,0:T(8,128)(2,1)}, bf16[520,128]{1,0:T(8,128)(2,1)S(1)}, u32[]{:S(2)}, u32[]{:S(2)}) collective-permute-start(bf16[520,128]{1,0:T(8,128)(2,1)} %shard_map.129.refs_0_), channel_id=1, source_target_pairs={{0,32},{4,36},{8,40},{12,44},{16,48},{20,52},{24,56},{28,60},{32,6... | collective-permute-start | bytes 399368 | tf_op jit(solution)/shard_map/ppermute | solution.py:174
  53.9 32.8 %copy-start.10 = (bf16[520,128]{1,0:T(8,128)(2,1)}, bf16[520,128]{1,0:T(8,128)(2,1)S(1)}, u32[]{:S(2)}) copy-start(bf16[520,128]{1,0:T(8,128)(2,1)S(1)} %collective-permute-done.3.refs_4_) | copy-start | bytes 399364
  53.9 21.4 %collective-permute-start.4 = (bf16[520,128]{1,0:T(8,128)(2,1)S(1)}, bf16[520,128]{1,0:T(8,128)(2,1)S(1)}, u32[]{:S(2)}, u32[]{:S(2)}) collective-permute-start(bf16[520,128]{1,0:T(8,128)(2,1)S(1)} %collective-permute-done.3.refs_4_), channel_id=1, source_target_pairs={{0,224},{4,228},{8,232},{12,236},{16,240},{20,244},{24,248},{28,25... | collective-permute-start | bytes 399368 | tf_op jit(solution)/shard_map/ppermute | solution.py:174
  68.9 17.9 %copy-start.11 = (bf16[520,128]{1,0:T(8,128)(2,1)}, bf16[520,128]{1,0:T(8,128)(2,1)S(1)}, u32[]{:S(2)}) copy-start(bf16[520,128]{1,0:T(8,128)(2,1)S(1)} %collective-permute-done.refs_1_) | copy-start | bytes 399364
  68.9 15.9 %collective-permute-start.1 = (bf16[520,128]{1,0:T(8,128)(2,1)S(1)}, bf16[520,128]{1,0:T(8,128)(2,1)S(1)}, u32[]{:S(2)}, u32[]{:S(2)}) collective-permute-start(bf16[520,128]{1,0:T(8,128)(2,1)S(1)} %collective-permute-done.refs_1_), channel_id=1, source_target_pairs={{0,32},{4,36},{8,40},{12,44},{16,48},{20,52},{24,56},{28,60},{32,6... | collective-permute-start | bytes 399368 | tf_op jit(solution)/shard_map/ppermute | solution.py:174
  75.3 11.4 %copy-start.12 = (bf16[520,128]{1,0:T(8,128)(2,1)}, bf16[520,128]{1,0:T(8,128)(2,1)S(1)}, u32[]{:S(2)}) copy-start(bf16[520,128]{1,0:T(8,128)(2,1)S(1)} %collective-permute-done.4.refs_5_) | copy-start | bytes 399364
  75.3 16.4 %collective-permute-start.5 = (bf16[520,128]{1,0:T(8,128)(2,1)S(1)}, bf16[520,128]{1,0:T(8,128)(2,1)S(1)}, u32[]{:S(2)}, u32[]{:S(2)}) collective-permute-start(bf16[520,128]{1,0:T(8,128)(2,1)S(1)} %collective-permute-done.4.refs_5_), channel_id=1, source_target_pairs={{0,224},{4,228},{8,232},{12,236},{16,240},{20,244},{24,248},{28,25... | collective-permute-start | bytes 399368 | tf_op jit(solution)/shard_map/ppermute | solution.py:174
  84.8 14.5 %copy-start.13 = (bf16[520,128]{1,0:T(8,128)(2,1)}, bf16[520,128]{1,0:T(8,128)(2,1)S(1)}, u32[]{:S(2)}) copy-start(bf16[520,128]{1,0:T(8,128)(2,1)S(1)} %collective-permute-done.1.refs_2_) | copy-start | bytes 399364
  84.8 14.5 %collective-permute-start.2 = (bf16[520,128]{1,0:T(8,128)(2,1)S(1)}, bf16[520,128]{1,0:T(8,128)(2,1)S(1)}, u32[]{:S(2)}, u32[]{:S(2)}) collective-permute-start(bf16[520,128]{1,0:T(8,128)(2,1)S(1)} %collective-permute-done.1.refs_2_), channel_id=1, source_target_pairs={{0,32},{4,36},{8,40},{12,44},{16,48},{20,52},{24,56},{28,60},{32,6... | collective-permute-start | bytes 399368 | tf_op jit(solution)/shard_map/ppermute | solution.py:174
  91.7 16.8 %copy-start.2 = (bf16[520,128]{1,0:T(8,128)(2,1)}, bf16[520,128]{1,0:T(8,128)(2,1)S(1)}, u32[]{:S(2)}) copy-start(bf16[520,128]{1,0:T(8,128)(2,1)S(1)} %collective-permute-done.5.refs_6_) | copy-start | bytes 399364
  91.7 16.8 %collective-permute-start.7 = (bf16[264,128]{1,0:T(8,128)(2,1)S(1)}, bf16[264,128]{1,0:T(8,128)(2,1)}, u32[]{:S(2)}, u32[]{:S(2)}) collective-permute-start(bf16[264,128]{1,0:T(8,128)(2,1)S(1)} %slice.9), channel_id=1, source_target_pairs={{0,224},{4,228},{8,232},{12,236},{16,240},{20,244},{24,248},{28,25... | collective-permute-start | bytes 202760 | tf_op jit(solution)/shard_map/ppermute | solution.py:174
  99.3 9.2 %copy-start.3 = (bf16[520,128]{1,0:T(8,128)(2,1)}, bf16[520,128]{1,0:T(8,128)(2,1)S(1)}, u32[]{:S(2)}) copy-start(bf16[520,128]{1,0:T(8,128)(2,1)S(1)} %collective-permute-done.2.refs_3_) | copy-start | bytes 399364
  99.3 9.2 %collective-permute-start.6 = (bf16[256,128]{1,0:T(8,128)(2,1)S(1)}, bf16[256,128]{1,0:T(8,128)(2,1)}, u32[]{:S(2)}, u32[]{:S(2)}) collective-permute-start(bf16[256,128]{1,0:T(8,128)(2,1)S(1)} %slice.8), channel_id=1, source_target_pairs={{0,32},{4,36},{8,40},{12,44},{16,48},{20,52},{24,56},{28,60},{32,6... | collective-permute-start | bytes 196616 | tf_op jit(solution)/shard_map/ppermute | solution.py:174
  113.6 15.9 %collective-permute-start.10 = (bf16[816,128]{1,0:T(8,128)(2,1)}, bf16[816,128]{1,0:T(8,128)(2,1)S(1)}, u32[]{:S(2)}, u32[]{:S(2)}) collective-permute-start(bf16[816,128]{1,0:T(8,128)(2,1)} %get-tuple-element.20), channel_id=1, source_target_pairs={{0,244},{4,248},{8,252},{12,0},{16,4},{20,8},{24,12},{28,16},{32,2... | collective-permute-start | bytes 626696 | tf_op jit(solution)/shard_map/ppermute | solution.py:174
  122.5 11.2 %collective-permute-start.11 = (bf16[816,128]{1,0:T(8,128)(2,1)}, bf16[816,128]{1,0:T(8,128)(2,1)S(1)}, u32[]{:S(2)}, u32[]{:S(2)}) collective-permute-start(bf16[816,128]{1,0:T(8,128)(2,1)} %get-tuple-element.21), channel_id=1, source_target_pairs={{0,8},{4,12},{8,16},{12,20},{16,24},{20,28},{24,32},{28,36},{32,40... | collective-permute-start | bytes 626696 | tf_op jit(solution)/shard_map/ppermute | solution.py:174
  124.4 12.7 %collective-permute-start.12 = (bf16[816,128]{1,0:T(8,128)(2,1)}, bf16[816,128]{1,0:T(8,128)(2,1)S(1)}, u32[]{:S(2)}, u32[]{:S(2)}) collective-permute-start(bf16[816,128]{1,0:T(8,128)(2,1)} %get-tuple-element.22), channel_id=1, source_target_pairs={{0,248},{4,252},{8,0},{12,4},{16,8},{20,12},{24,16},{28,20},{32,24... | collective-permute-start | bytes 626696 | tf_op jit(solution)/shard_map/ppermute | solution.py:174
  129.0 8.1 %collective-permute-start.13 = (bf16[816,128]{1,0:T(8,128)(2,1)}, bf16[816,128]{1,0:T(8,128)(2,1)S(1)}, u32[]{:S(2)}, u32[]{:S(2)}) collective-permute-start(bf16[816,128]{1,0:T(8,128)(2,1)} %get-tuple-element.23), channel_id=1, source_target_pairs={{0,4},{4,8},{8,12},{12,16},{16,20},{20,24},{24,28},{28,32},{32,36}... | collective-permute-start | bytes 626696 | tf_op jit(solution)/shard_map/ppermute | solution.py:174
  129.4 9.1 %collective-permute-start.14 = (bf16[816,128]{1,0:T(8,128)(2,1)}, bf16[816,128]{1,0:T(8,128)(2,1)S(1)}, u32[]{:S(2)}, u32[]{:S(2)}) collective-permute-start(bf16[816,128]{1,0:T(8,128)(2,1)} %get-tuple-element.24), channel_id=1, source_target_pairs={{0,252},{4,0},{8,4},{12,8},{16,12},{20,16},{24,20},{28,24},{32,28}... | collective-permute-start | bytes 626696 | tf_op jit(solution)/shard_map/ppermute | solution.py:174
  129.5 17.8 %copy-start.4 = (bf16[816,128]{1,0:T(8,128)(2,1)}, bf16[816,128]{1,0:T(8,128)(2,1)S(1)}, u32[]{:S(2)}) copy-start(bf16[816,128]{1,0:T(8,128)(2,1)S(1)} %collective-permute-done.10.refs_2_) | copy-start | bytes 626692
  129.5 13.8 %collective-permute-start.8 = (bf16[816,128]{1,0:T(8,128)(2,1)}, bf16[816,128]{1,0:T(8,128)(2,1)S(1)}, u32[]{:S(2)}, u32[]{:S(2)}) collective-permute-start(bf16[816,128]{1,0:T(8,128)(2,1)} %get-tuple-element.18), channel_id=1, source_target_pairs={{0,240},{4,244},{8,248},{12,252},{16,0},{20,4},{24,8},{28,12},{32,... | collective-permute-start | bytes 626696 | tf_op jit(solution)/shard_map/ppermute | solution.py:174
  133.7 9.7 %copy-start.5 = (bf16[816,128]{1,0:T(8,128)(2,1)}, bf16[816,128]{1,0:T(8,128)(2,1)S(1)}, u32[]{:S(2)}) copy-start(bf16[816,128]{1,0:T(8,128)(2,1)S(1)} %collective-permute-done.11.refs_3_) | copy-start | bytes 626692
  133.7 13.6 %collective-permute-start.9 = (bf16[816,128]{1,0:T(8,128)(2,1)}, bf16[816,128]{1,0:T(8,128)(2,1)}, u32[]{:S(2)}, u32[]{:S(2)}) collective-permute-start(bf16[816,128]{1,0:T(8,128)(2,1)} %get-tuple-element.19), channel_id=1, source_target_pairs={{0,12},{4,16},{8,20},{12,24},{16,28},{20,32},{24,36},{28,40},{32,4... | collective-permute-start | bytes 626696 | tf_op jit(solution)/shard_map/ppermute | solution.py:174
  137.1 6.3 %copy-start.6 = (bf16[816,128]{1,0:T(8,128)(2,1)}, bf16[816,128]{1,0:T(8,128)(2,1)S(1)}, u32[]{:S(2)}) copy-start(bf16[816,128]{1,0:T(8,128)(2,1)S(1)} %collective-permute-done.12.refs_4_) | copy-start | bytes 626692
  137.1 6.2 %copy-start.7 = (bf16[816,128]{1,0:T(8,128)(2,1)}, bf16[816,128]{1,0:T(8,128)(2,1)S(1)}, u32[]{:S(2)}) copy-start(bf16[816,128]{1,0:T(8,128)(2,1)S(1)} %collective-permute-done.13.refs_5_) | copy-start | bytes 626692
  138.5 4.9 %copy-start.8 = (bf16[816,128]{1,0:T(8,128)(2,1)}, bf16[816,128]{1,0:T(8,128)(2,1)S(1)}, u32[]{:S(2)}) copy-start(bf16[816,128]{1,0:T(8,128)(2,1)S(1)} %collective-permute-done.14.refs_6_) | copy-start | bytes 626692
  143.3 0.7 copy-start.9
  147.3 1.6 copy-start.1
  249.5 21.0 %all-to-all-start.2 = ((bf16[4,2,192,384]{3,2,1,0:T(8,128)(2,1)}), bf16[4,2,192,384]{3,2,1,0:T(8,128)(2,1)}, u32[]{:S(2)}, u32[]{:S(2)}) async-start(bf16[4,2,192,384]{3,2,1,0:T(8,128)(2,1)} %get-tuple-element.27), calls=%async_computation.2 | async-start | bytes 2359296 | tf_op jit(solution)/shard_map/all_to_all | solution.py:247
  270.4 15.5 %all-to-all-start.4 = ((bf16[4,2,192,256]{3,2,1,0:T(8,128)(2,1)}), bf16[4,2,192,256]{3,2,1,0:T(8,128)(2,1)S(1)}, u32[]{:S(2)}, u32[]{:S(2)}) async-start(bf16[4,2,192,256]{3,2,1,0:T(8,128)(2,1)} %reduce_sum.21), calls=%async_computation.4 | async-start | bytes 1572864 | tf_op jit(solution)/shard_map/all_to_all | solution.py:265

commit v2 on v1

v2 whole, which is shorter than its diff:
```python
import jax
import jax.numpy as jnp
import numpy as np
from jax import lax
from jax.experimental import pallas as pl
from jax.experimental.pallas import tpu as pltpu
from jax.sharding import PartitionSpec as P


STRIDE = 8
OFFSETS = (0, -1, -2, -3, 1, 2, 3, 4)
SHIFTS = (-4, 3, -3, 2, -2, 1, -1, 0)
VMEM = pltpu.VMEM
LIMIT = 60 * 1024 * 1024


def spec():
    return pl.BlockSpec(memory_space=VMEM)


def call(body, outs, *args, scratch=(), untouched=(), flops=10**6, moved=10**6):
    smem = pl.BlockSpec(memory_space=pltpu.SMEM)
    specs = [smem if a.dtype == jnp.int32 and a.shape == (3,) else spec() for a in args]
    for i in untouched:
        specs[i] = pl.BlockSpec(memory_space=pl.ANY)
    return pl.pallas_call(
        body,
        out_shape=outs,
        in_specs=specs,
        out_specs=jax.tree.map(lambda _: spec(), outs),
        scratch_shapes=list(scratch),
        compiler_params=pltpu.CompilerParams(vmem_limit_bytes=LIMIT),
        cost_estimate=pl.CostEstimate(flops=flops, bytes_accessed=moved, transcendentals=0),
    )(*args)


def dot(a, b):
    return jnp.dot(a, b, preferred_element_type=jnp.float32)


def dot_nt(a, b):
    return lax.dot_general(a, b, (((1,), (1,)), ((), ())), preferred_element_type=jnp.float32)


def earlier_matrix(n, block):
    row = lax.broadcasted_iota(jnp.int32, (n, n), 0)
    col = lax.broadcasted_iota(jnp.int32, (n, n), 1)
    same = (row // block) == (col // block)
    return jnp.where((row < col) & same, 1.0, 0.0).astype(jnp.bfloat16)


def pack_body(self_ref, x_ref, ids_ref, probs_ref, out_ref):
    t = self_ref[1]
    toks = x_ref.shape[0]
    for c in range(8):
        start = pl.multiple_of((c // 2) * 1024 + t * 256 + (c % 2) * 128, 128)
        out_ref[c * toks : (c + 1) * toks, :] = x_ref[:, pl.ds(start, 128)]
    both = jnp.concatenate(
        [ids_ref[...].astype(jnp.float32), probs_ref[...].astype(jnp.float32)], axis=1
    )
    out_ref[8 * toks : 8 * toks + 8, :] = both.astype(jnp.bfloat16)


def prepare_body(w_ref, gate_ref, up_ref, _, out_ref):
    for e in range(2):
        gate = gate_ref[e].astype(jnp.float32)
        hidden = (gate * jax.nn.sigmoid(gate) * up_ref[e].astype(jnp.float32)).astype(jnp.bfloat16)
        for t in range(4):
            for r in range(4):
                start = r * 1024 + t * 256
                out_ref[t, e, :, r * 256 : (r + 1) * 256] = w_ref[e, :, start : start + 256]
            out_ref[t, e, :, 1024:1408] = hidden


def select_body(self_ref, onehot_ref, code_ref, exp_ref, *refs):
    blocks, outs = refs[:9], refs[9:]
    s = self_ref[0]
    routes = [b[512:520, :].astype(jnp.float32) for b in blocks[:7]]
    routes.append(blocks[8][256:264, :].astype(jnp.float32))
    ids = jnp.concatenate([r[:, :64] for r in routes], axis=1)
    probs = jnp.concatenate([r[:, 64:] for r in routes], axis=1)
    base = exp_ref[...]
    mine = (2 * s + base) & 127
    mine = mine.astype(jnp.float32)
    match = jnp.zeros((16, 512), jnp.float32)
    prob = jnp.zeros((16, 512), jnp.float32)
    for k in range(8):
        hit = ids[k : k + 1, :] == mine
        match = jnp.where(hit, 1.0, match)
        prob = jnp.where(hit, probs[k : k + 1, :], prob)
    before = earlier_matrix(128, 64)
    low = match.astype(jnp.bfloat16)
    pos = jnp.concatenate(
        [dot(low[:, 128 * c : 128 * (c + 1)], before) for c in range(4)], axis=1
    )
    block = lax.broadcasted_iota(jnp.int32, (16, 512), 1) >> 6
    code = jnp.where(match > 0.0, pos + 6.0 * block.astype(jnp.float32), -1.0)
    onehot = onehot_ref[...]
    spread = dot(onehot, code.astype(jnp.bfloat16))
    chosen = spread == code_ref[...]
    pick = jnp.where(chosen, 1.0, 0.0).astype(jnp.bfloat16)
    weights = dot(onehot, prob.astype(jnp.bfloat16))
    weighted = jnp.where(chosen, weights, 0.0).astype(jnp.bfloat16)
    slot_probs = dot_nt(jnp.ones((8, 512), jnp.bfloat16), weighted).astype(jnp.bfloat16)
    for c in range(8):
        parts = [b[c * 64 : (c + 1) * 64, :] for b in blocks[:7]]
        last = blocks[7] if c < 4 else blocks[8]
        parts.append(last[(c % 4) * 64 : (c % 4 + 1) * 64, :])
        rows = dot(pick, jnp.concatenate(parts, axis=0)).astype(jnp.bfloat16)
        for v in range(8):
            for e in range(2):
                outs[v][c * 96 + e * 48 : c * 96 + (e + 1) * 48, :] = rows[
                    e * 384 + v * 48 : e * 384 + (v + 1) * 48, :
                ]
    for v in range(8):
        for c in range(6):
            outs[v][768 + 8 * c : 776 + 8 * c, :] = slot_probs[:, 128 * c : 128 * (c + 1)]


def expert_body(self_ref, place_ref, *refs):
    pieces = refs[:8]
    wh_ref = refs[8]
    gh_refs, gw_refs = refs[9:13], refs[13:17]
    dots_ref, prob_ref = refs[17:19]
    arrived_ref, rows_ref, scaled_ref = refs[19:]
    s, t, r = self_ref[0], self_ref[1], self_ref[2]
    for v in range(8):
        for c in range(8):
            for e in range(2):
                arrived_ref[
                    e * 384 + v * 48 : e * 384 + (v + 1) * 48, c * 128 : (c + 1) * 128
                ] = pieces[v][c * 96 + e * 48 : c * 96 + (e + 1) * 48, :]
    lane = lax.broadcasted_iota(jnp.int32, (8, 768), 1)
    probs = jnp.zeros((8, 768), jnp.float32)
    for v in range(8):
        wide = jnp.concatenate(
            [pieces[v][768 + 8 * c : 776 + 8 * c, :] for c in range(6)], axis=1
        ).astype(jnp.float32)
        mine = place_ref[2:3, :] == v
        probs = jnp.where(mine, wide, probs)
    low = probs.astype(jnp.bfloat16)
    target = ((s + place_ref[0:1, :]) & 63) * 6 + place_ref[1:2, :]
    row = lax.broadcasted_iota(jnp.int32, (384, 384), 0)
    for e in range(2):
        perm = jnp.where(row == target[:, e * 384 : (e + 1) * 384], 1.0, 0.0).astype(jnp.bfloat16)
        mine = low[:, e * 384 : (e + 1) * 384]
        prob_ref[:, e * 384 : (e + 1) * 384] = dot_nt(mine, perm)
        column = dot_nt(perm, mine)[:, :1]
        here = slice(e * 384, (e + 1) * 384)
        for c in range(4):
            part = dot(perm, arrived_ref[here, c * 256 : (c + 1) * 256])
            rows_ref[here, c * 256 : (c + 1) * 256] = part.astype(jnp.bfloat16)
            scaled_ref[here, c * 256 : (c + 1) * 256] = (part * column).astype(jnp.bfloat16)
    for e in range(2):
        hidden = jnp.concatenate([wh_ref[k, e, :, 1024:1408] for k in range(4)], axis=0)
        for rho in range(4):
            start = pl.multiple_of(((r + rho) & 3) * 256, 256)
            part = dot(hidden, scaled_ref[e * 384 : (e + 1) * 384, pl.ds(start, 256)])
            part = part.astype(jnp.bfloat16)
            for k in range(4):
                gw_refs[rho][k, e] = part[k * 192 : (k + 1) * 192, :]
    for e in range(2):
        total = jnp.zeros((1, 384), jnp.float32)
        for delta in range(4):
            k = (t + delta) & 3
            part = dot_nt(wh_ref[k, e, :, :1024], rows_ref[e * 384 : (e + 1) * 384, :])
            gh_refs[delta][e] = part.astype(jnp.bfloat16)
            hidden = wh_ref[k, e, :, 1024:1408].astype(jnp.float32)
            total += jnp.sum(part * hidden, axis=0, keepdims=True)
        dots_ref[e : e + 1, :] = total


def local_body(prob_ref, *refs):
    gh_refs, gate_ref, up_ref, gg_ref, gu_ref = refs[:4], *refs[4:]
    for e in range(2):
        total = gh_refs[0][e].astype(jnp.float32)
        for k in range(1, 4):
            total += gh_refs[k][e].astype(jnp.float32)
        gate = gate_ref[e].astype(jnp.float32)
        up = up_ref[e].astype(jnp.float32)
        sig = jax.nn.sigmoid(gate)
        scaled = prob_ref[0:1, e * 384 : (e + 1) * 384] * total
        gu_ref[e] = (scaled * (gate * sig)).astype(jnp.bfloat16)
        gg_ref[e] = (scaled * up * sig * (1.0 + gate * (1.0 - sig))).astype(jnp.bfloat16)


def replica_body(self_ref, *refs):
    parts, outs = refs[:4], refs[4:]
    for delta in range(4):
        k = (self_ref[1] + delta) & 3
        for e in range(2):
            total = parts[0][k, e].astype(jnp.float32)
            for part in parts[1:]:
                total += part[k, e].astype(jnp.float32)
            outs[delta][e] = total.astype(jnp.bfloat16)


def place_body(self_ref, *refs):
    parts, out_ref = refs[:4], refs[4]
    for delta in range(4):
        start = pl.multiple_of(((self_ref[1] - delta) & 3) * 256, 256)
        for e in range(2):
            out_ref[e, :, pl.ds(start, 256)] = parts[delta][e]


def lookup_body(ids_ref, table_ref, out_ref):
    experts, capacity = 128, 6
    ids = ids_ref[...]
    expert = lax.broadcasted_iota(jnp.int32, (experts, 64), 0)
    match = jnp.zeros((experts, 64), jnp.float32)
    for k in range(8):
        match = jnp.where(ids[k : k + 1, :] == expert, 1.0, match)
    pos = dot(match.astype(jnp.bfloat16), earlier_matrix(64, 64))
    value = jnp.zeros((experts, 64), jnp.float32)
    for j in range(capacity):
        value = jnp.where(pos == float(j), table_ref[:, j : j + 1], value)
    for k in range(8):
        hit = ids[k : k + 1, :] == expert
        out_ref[k : k + 1, :] = jnp.sum(jnp.where(hit, value, 0.0), axis=0, keepdims=True)


def shifted(x, by, axis):
    count = lax.axis_size(axis)
    return lax.ppermute(x, axis, [(i, (i + by) % count) for i in range(count)])


def spread(parts, axis):
    return [parts[0], *(shifted(parts[d], d, axis) for d in (1, 2, 3))]


def slot_tables():
    row = np.arange(768)
    onehot = np.zeros((768, 16), np.float32)
    onehot[row, row // 48] = 1.0
    code = (row % 48).astype(np.float32)[:, None]
    shift = np.array(SHIFTS)
    expert = (2 * shift[None, :] + np.arange(2)[:, None]).reshape(16, 1).astype(np.int32)
    piece, o, j = (row % 384) // 48, (row // 6) % 8, row % 6
    tables = np.zeros((8, 768), np.int32)
    tables[0] = STRIDE * np.array(OFFSETS)[o] - shift[piece]
    tables[1] = j
    tables[2] = piece
    return onehot, code, expert, tables


def backward(x, ids, probs, gate, up, w):
    bf16, f32, shape = jnp.bfloat16, jnp.float32, jax.ShapeDtypeStruct
    count = lax.axis_size("expert")
    own = jnp.stack([lax.axis_index(a).astype(jnp.int32) for a in ("expert", "tensor", "dp")])
    ids_t = ids.T
    gate_t = jnp.transpose(gate[0], (0, 2, 1))
    up_t = jnp.transpose(up[0], (0, 2, 1))

    packed = call(pack_body, shape((520, 128), bf16), own, x, ids_t, probs.T)
    blocks = {0: packed}
    for step in (1, 2, 3):
        blocks[-step] = shifted(blocks[1 - step], STRIDE, "expert")
        blocks[step] = shifted(blocks[step - 1], -STRIDE, "expert")
    far_low = shifted(blocks[-3][:256], STRIDE, "expert")
    far_high = shifted(blocks[3][256:], -STRIDE, "expert")

    to_send = call(
        prepare_body,
        shape((4, 2, 192, 1408), bf16),
        w,
        gate_t,
        up_t,
        blocks[-1],
        untouched=(3,),
        flops=10**7,
        moved=8 * 1024 * 1024,
    )
    wh_all = lax.all_to_all(to_send, "tensor", split_axis=0, concat_axis=0, tiled=True)

    onehot, code, expert, tables = slot_tables()
    pieces = call(
        select_body,
        [shape((816, 128), bf16)] * 8,
        own,
        jnp.asarray(onehot, bf16),
        jnp.asarray(code),
        jnp.asarray(expert),
        *[blocks[o] for o in OFFSETS[:7]],
        far_low,
        far_high,
        flops=2 * 768 * 512 * 1024,
        moved=4 * 1024 * 1024,
    )
    pieces = [p if j == 0 else shifted(p, j, "expert") for p, j in zip(pieces, SHIFTS)]

    results = call(
        expert_body,
        [shape((2, 192, 384), bf16)] * 4
        + [shape((4, 2, 192, 256), bf16)] * 4
        + [shape((2, 384), f32), shape((8, 768), f32)],
        own,
        jnp.asarray(tables),
        *pieces,
        wh_all,
        scratch=[VMEM((768, 1024), bf16)] * 3,
        flops=6 * 10**9,
        moved=12 * 1024 * 1024,
    )
    gh, gw, dots, prob = results[:4], results[4:8], results[8], results[9]

    gw = spread(gw, "dp")
    gh = spread(gh, "tensor")
    cells = jnp.transpose(dots.reshape(2, count, 6), (1, 0, 2)).reshape(count, 12)
    cells = jnp.broadcast_to(cells[None], (4, count, 12)).reshape(4 * count, 12)
    back = lax.all_to_all(cells, ("tensor", "expert"), split_axis=0, concat_axis=0, tiled=True)
    table = back.reshape(4, 2 * count, 6).sum(axis=0)

    summed = call(replica_body, [shape((2, 192, 256), bf16)] * 4, own, *gw, moved=4 * 1024 * 1024, flops=10**7)
    summed = spread(summed, "tensor")
    grad_gate, grad_up = call(
        local_body,
        [shape((2, 192, 384), bf16)] * 2,
        prob,
        *gh,
        gate_t,
        up_t,
        flops=10**7,
        moved=4 * 1024 * 1024,
    )
    grad_w = call(place_body, shape((2, 192, 1024), bf16), own, *summed, moved=2 * 1024 * 1024, flops=10**6)
    grad_probs = call(lookup_body, shape((8, 64), f32), ids_t, table, flops=10**6, moved=10**5).T
    return (
        jnp.transpose(grad_gate, (0, 2, 1))[None],
        jnp.transpose(grad_up, (0, 2, 1))[None],
        grad_w,
        grad_probs,
    )


def solution(mesh):
    act = P("dp", "expert", None, "tensor")
    tok = P(("expert", "dp"), None)
    return jax.shard_map(
        backward,
        mesh=mesh,
        in_specs=(tok, tok, tok, act, act, P("expert", "tensor", None)),
        out_specs=(act, act, P("expert", "tensor", "dp"), tok),
        check_vma=False,
    )
```

time: 288 us -> 273 us (0.948)
  blocking collectives: 89.1 us -> 50.8 us
  waiting for transfers between devices: 48.7 us -> 69.7 us
  local copies, waits for them, and re-layouts: 17.1 us -> 6.68 us
  Pallas kernels: 21.5 us -> 30 us
  starting transfers between devices: 105 us -> 112 us
    ppermute x15 -> x24, waiting for transfers between devices: 28.2 us -> 69.7 us  [shifted(): return lax.ppermute(x, axis, [(i, (i + by) % count) for i in range(count)])]
    all_to_all x2 -> x1, blocking collectives: 89.1 us -> 50.8 us  [backward(): lax.all_to_all(cells, ('tensor', 'expert'), split_axis=0, concat_axis=0,...]
    all_to_all x4 -> x1, waiting for transfers between devices: 20.5 us -> 0.01 us  [backward(): lax.all_to_all(to_send, 'tensor', split_axis=0, concat_axis=0, tiled=True)]
    ppermute x15 -> x24, starting transfers between devices: 87.9 us -> 107 us  [shifted(): return lax.ppermute(x, axis, [(i, (i + by) % count) for i in range(count)])]
    all_to_all x4 -> x1, starting transfers between devices: 17 us -> 5.02 us  [backward(): lax.all_to_all(to_send, 'tensor', split_axis=0, concat_axis=0, tiled=True)]
    reshape x6 -> x2, local copies, waits for them, and re-layouts: 12.8 us -> 0.92 us  [the longest x1 0.82 us: backward(): dots.reshape(2, count, 6)]
    pallas_call x5 -> x8, Pallas kernels: 21.5 us -> 30 us  [call(): pl.pallas_call(body, out_shape=outs, in_specs=specs, out_specs=jax.tree.m...]
  transfers between devices with their start and end apart: 19 -> 25, of which waited for: 11 -> 11; matrix products, arithmetic and copies ran while one was open for 5% -> 1% of each run, Pallas kernels for 4% -> 5%
where the time goes in v2:
time: 273 us; the launch traced here: 272 us
  starting transfers between devices  112 us (41%)
  waiting for transfers between devices  69.7 us (26%)
  blocking collectives  50.8 us (19%)
  Pallas kernels  30 us (11%)
  local copies, waits for them, and re-layouts  6.68 us (2%)
    ppermute x24, starting transfers between devices, shifted(): return lax.ppermute(x, axis, [(i, (i + by) % count) for i in range(count)])  107 us
    ppermute x24, waiting for transfers between devices, shifted(): return lax.ppermute(x, axis, [(i, (i + by) % count) for i in range(count)])  69.7 us
    all_to_all x1, blocking collectives, backward(): lax.all_to_all(cells, ('tensor', 'expert'), split_axis=0, concat_axis=0,...  50.8 us
    pallas_call x8, Pallas kernels, call(): pl.pallas_call(body, out_shape=outs, in_specs=specs, out_specs=jax.tree.m...  30 us
  transfers between devices with their start and end apart: 25, of which 11 were waited for; matrix products, arithmetic and copies ran while one was open for 1% of the time, Pallas kernels for 5%

profile of v2, /device:TPU:1, one launch (start us, length us, event | category | flops | bytes accessed | tf_op | source)
XLA Modules:
  0.0 272.3 jit_solution(2695427047225649358)
XLA Ops:
  0.6 0.7 pad_add_fusion.self_ref
  1.3 1.8 shard_map.129.refs_0_
  3.1 9.6 %collective-permute-start = (bf16[520,128]{1,0:T(8,128)(2,1)}, bf16[520,128]{1,0:T(8,128)(2,1)S(1)}, u32[]{:S(2)}, u32[]{:S(2)}) collective-permute-start(bf16[520,128]{1,0:T(8,128)(2,1)} %shard_map.129.refs_0_), channel_id=1, source_target_pairs={{0,32},{4,36},{8,40},{12,44},{16,48},{20,52},{24,56},{28,60},{32,6... | collective-permute-start | bytes 399368 | tf_op jit(solution)/shard_map/ppermute | solution.py:224
  12.7 14.0 %collective-permute-done.refs_1_._ = bf16[520,128]{1,0:T(8,128)(2,1)S(1)} collective-permute-done((bf16[520,128]{1,0:T(8,128)(2,1)}, bf16[520,128]{1,0:T(8,128)(2,1)S(1)}, u32[]{:S(2)}, u32[]{:S(2)}) %collective-permute-start) | collective-permute-done | bytes 133152 | tf_op jit(solution)/shard_map/ppermute | solution.py:224
  26.8 0.7 copy-done.9
  27.4 4.5 %shard_map.131 = bf16[4,2,192,1408]{3,2,1,0:T(8,128)(2,1)} custom-call(bf16[2,192,4096]{2,1,0:T(8,128)(2,1)} %w_ref.1, bf16[2,192,384]{2,1,0:T(8,128)(2,1)} %bitcast.22, bf16[2,192,384]{2,1,0:T(8,128)(2,1)} %bitcast.24, bf16[520,128]{1,0:T(8,128)(2,1)} %copy-done.9), custom_call_target="tpu_custom_call" | custom-call | flops 10000000 | bytes 8388608 | tf_op jit(solution)/shard_map/pallas_call | solution.py:26
  31.9 5.0 %all-to-all-start = ((bf16[4,2,192,1408]{3,2,1,0:T(8,128)(2,1)}), bf16[4,2,192,1408]{3,2,1,0:T(8,128)(2,1)}, u32[]{:S(2)}, u32[]{:S(2)}) async-start(bf16[4,2,192,1408]{3,2,1,0:T(8,128)(2,1)} %shard_map.131), calls=%async_computation | async-start | bytes 8650752 | tf_op jit(solution)/shard_map/all_to_all | solution.py:273
  36.9 9.1 %collective-permute-start.3 = (bf16[520,128]{1,0:T(8,128)(2,1)S(1)}, bf16[520,128]{1,0:T(8,128)(2,1)S(1)}, u32[]{:S(2)}, u32[]{:S(2)}) collective-permute-start(bf16[520,128]{1,0:T(8,128)(2,1)S(1)} %copy-done.11), channel_id=1, source_target_pairs={{0,224},{4,228},{8,232},{12,236},{16,240},{20,244},{24,248},{28,25... | collective-permute-start | bytes 399368 | tf_op jit(solution)/shard_map/ppermute | solution.py:224
  46.1 1.9 collective-permute-done.3.refs_4_
  48.0 7.7 %collective-permute-start.4 = (bf16[520,128]{1,0:T(8,128)(2,1)S(1)}, bf16[520,128]{1,0:T(8,128)(2,1)S(1)}, u32[]{:S(2)}, u32[]{:S(2)}) collective-permute-start(bf16[520,128]{1,0:T(8,128)(2,1)S(1)} %collective-permute-done.3.refs_4_), channel_id=1, source_target_pairs={{0,224},{4,228},{8,232},{12,236},{16,240},{20,244},{24,248},{28,25... | collective-permute-start | bytes 399368 | tf_op jit(solution)/shard_map/ppermute | solution.py:224
  55.7 7.8 %collective-permute-start.1 = (bf16[520,128]{1,0:T(8,128)(2,1)S(1)}, bf16[520,128]{1,0:T(8,128)(2,1)S(1)}, u32[]{:S(2)}, u32[]{:S(2)}) collective-permute-start(bf16[520,128]{1,0:T(8,128)(2,1)S(1)} %copy-done.10), channel_id=1, source_target_pairs={{0,32},{4,36},{8,40},{12,44},{16,48},{20,52},{24,56},{28,60},{32,6... | collective-permute-start | bytes 399368 | tf_op jit(solution)/shard_map/ppermute | solution.py:224
  63.5 6.1 %collective-permute-done.4.refs_5_ = bf16[520,128]{1,0:T(8,128)(2,1)S(1)} collective-permute-done((bf16[520,128]{1,0:T(8,128)(2,1)S(1)}, bf16[520,128]{1,0:T(8,128)(2,1)S(1)}, u32[]{:S(2)}, u32[]{:S(2)}) %collective-permute-start.4) | collective-permute-done | bytes 133152 | tf_op jit(solution)/shard_map/ppermute | solution.py:224
  69.6 2.2 collective-permute-start.5
  71.8 7.0 %collective-permute-start.2 = (bf16[520,128]{1,0:T(8,128)(2,1)S(1)}, bf16[520,128]{1,0:T(8,128)(2,1)S(1)}, u32[]{:S(2)}, u32[]{:S(2)}) collective-permute-start(bf16[520,128]{1,0:T(8,128)(2,1)S(1)} %collective-permute-done.1.refs_2_), channel_id=1, source_target_pairs={{0,32},{4,36},{8,40},{12,44},{16,48},{20,52},{24,56},{28,60},{32,6... | collective-permute-start | bytes 399368 | tf_op jit(solution)/shard_map/ppermute | solution.py:224
  78.8 2.4 collective-permute-done.5.refs_6_
  81.2 5.4 %collective-permute-start.7 = (bf16[264,128]{1,0:T(8,128)(2,1)S(1)}, bf16[264,128]{1,0:T(8,128)(2,1)S(1)}, u32[]{:S(2)}, u32[]{:S(2)}) collective-permute-start(bf16[264,128]{1,0:T(8,128)(2,1)S(1)} %slice.9), channel_id=1, source_target_pairs={{0,224},{4,228},{8,232},{12,236},{16,240},{20,244},{24,248},{28,25... | collective-permute-start | bytes 202760 | tf_op jit(solution)/shard_map/ppermute | solution.py:224
  86.6 3.8 %collective-permute-start.6 = (bf16[256,128]{1,0:T(8,128)(2,1)S(1)}, bf16[256,128]{1,0:T(8,128)(2,1)S(1)}, u32[]{:S(2)}, u32[]{:S(2)}) collective-permute-start(bf16[256,128]{1,0:T(8,128)(2,1)S(1)} %slice.8), channel_id=1, source_target_pairs={{0,32},{4,36},{8,40},{12,44},{16,48},{20,52},{24,56},{28,60},{32,6... | collective-permute-start | bytes 196616 | tf_op jit(solution)/shard_map/ppermute | solution.py:224
  90.5 11.1 %collective-permute-done.6.refs_7_ = bf16[256,128]{1,0:T(8,128)(2,1)S(1)} collective-permute-done((bf16[256,128]{1,0:T(8,128)(2,1)S(1)}, bf16[256,128]{1,0:T(8,128)(2,1)S(1)}, u32[]{:S(2)}, u32[]{:S(2)}) %collective-permute-start.6) | collective-permute-done | bytes 65568 | tf_op jit(solution)/shard_map/ppermute | solution.py:224
  101.6 0.6 copy-done.25
  102.2 0.6 copy-done.24
  102.8 5.1 %shard_map.130 = (bf16[816,128]{1,0:T(8,128)(2,1)}, bf16[816,128]{1,0:T(8,128)(2,1)}, bf16[816,128]{1,0:T(8,128)(2,1)}, bf16[816,128]{1,0:T(8,128)(2,1)}, bf16[8...) custom-call(s32[3]{0:T(128)} %pad_add_fusion.self_ref, ...), custom_call_target="tpu_custom_call" | custom-call | flops 805306368 | bytes 4194304 | tf_op jit(solution)/shard_map/pallas_call | solution.py:26
  107.9 14.2 %collective-permute-start.10 = (bf16[816,128]{1,0:T(8,128)(2,1)}, bf16[816,128]{1,0:T(8,128)(2,1)S(1)}, u32[]{:S(2)}, u32[]{:S(2)}) collective-permute-start(bf16[816,128]{1,0:T(8,128)(2,1)} %get-tuple-element.30), channel_id=1, source_target_pairs={{0,244},{4,248},{8,252},{12,0},{16,4},{20,8},{24,12},{28,16},{32,2... | collective-permute-start | bytes 626696 | tf_op jit(solution)/shard_map/ppermute | solution.py:224
  122.1 1.9 collective-permute-start.11
  124.1 4.6 %collective-permute-start.12 = (bf16[816,128]{1,0:T(8,128)(2,1)}, bf16[816,128]{1,0:T(8,128)(2,1)S(1)}, u32[]{:S(2)}, u32[]{:S(2)}) collective-permute-start(bf16[816,128]{1,0:T(8,128)(2,1)} %get-tuple-element.32), channel_id=1, source_target_pairs={{0,248},{4,252},{8,0},{12,4},{16,8},{20,12},{24,16},{28,20},{32,24... | collective-permute-start | bytes 626696 | tf_op jit(solution)/shard_map/ppermute | solution.py:224
  128.6 0.4 collective-permute-start.13
  129.0 0.2 collective-permute-start.14
  129.2 4.0 %collective-permute-start.8 = (bf16[816,128]{1,0:T(8,128)(2,1)}, bf16[816,128]{1,0:T(8,128)(2,1)S(1)}, u32[]{:S(2)}, u32[]{:S(2)}) collective-permute-start(bf16[816,128]{1,0:T(8,128)(2,1)} %get-tuple-element.28), channel_id=1, source_target_pairs={{0,240},{4,244},{8,248},{12,252},{16,0},{20,4},{24,8},{28,12},{32,... | collective-permute-start | bytes 626696 | tf_op jit(solution)/shard_map/ppermute | solution.py:224
  133.2 3.5 %collective-permute-start.9 = (bf16[816,128]{1,0:T(8,128)(2,1)}, bf16[816,128]{1,0:T(8,128)(2,1)S(1)}, u32[]{:S(2)}, u32[]{:S(2)}) collective-permute-start(bf16[816,128]{1,0:T(8,128)(2,1)} %get-tuple-element.29), channel_id=1, source_target_pairs={{0,12},{4,16},{8,20},{12,24},{16,28},{20,32},{24,36},{28,40},{32,4... | collective-permute-start | bytes 626696 | tf_op jit(solution)/shard_map/ppermute | solution.py:224
  136.8 1.7 collective-permute-done.14.refs_6_
  138.5 2.9 %collective-permute-done.8.refs_0_ = bf16[816,128]{1,0:T(8,128)(2,1)S(1)} collective-permute-done((bf16[816,128]{1,0:T(8,128)(2,1)}, bf16[816,128]{1,0:T(8,128)(2,1)S(1)}, u32[]{:S(2)}, u32[]{:S(2)}) %collective-permute-start.8) | collective-permute-done | bytes 208928 | tf_op jit(solution)/shard_map/ppermute | solution.py:224
  141.3 5.4 %collective-permute-done.9.refs_1_ = bf16[816,128]{1,0:T(8,128)(2,1)S(1)} collective-permute-done((bf16[816,128]{1,0:T(8,128)(2,1)}, bf16[816,128]{1,0:T(8,128)(2,1)S(1)}, u32[]{:S(2)}, u32[]{:S(2)}) %collective-permute-start.9) | collective-permute-done | bytes 208928 | tf_op jit(solution)/shard_map/ppermute | solution.py:224
  146.7 0.6 copy-done.20
  147.4 9.0 %shard_map.132 = (bf16[2,192,384]{2,1,0:T(8,128)(2,1)}, bf16[2,192,384]{2,1,0:T(8,128)(2,1)}, bf16[2,192,384]{2,1,0:T(8,128)(2,1)}, bf16[2,192,384]{2,1,0:T(8,12...) custom-call(s32[3]{0:T(128)} %pad_add_fusion.self_ref, ...), custom_call_target="tpu_custom_call" | custom-call | flops 6000000000 | bytes 12582912 | tf_op jit(solution)/shard_map/pallas_call | solution.py:26
  156.4 1.9 collective-permute-start.18
  158.3 4.1 %collective-permute-start.19 = (bf16[4,2,192,256]{3,2,1,0:T(8,128)(2,1)}, bf16[4,2,192,256]{3,2,1,0:T(8,128)(2,1)S(1)}, u32[]{:S(2)}, u32[]{:S(2)}) collective-permute-start(bf16[4,2,192,256]{3,2,1,0:T(8,128)(2,1)} %get-tuple-element.45), channel_id=1, source_target_pairs={{0,2},{1,3},{2,0},{3,1},{4,6},{5,7},{6,4},{7,5},{8,10},{9,11},{10,... | collective-permute-start | bytes 2359304 | tf_op jit(solution)/shard_map/ppermute | solution.py:224
  162.5 3.1 %collective-permute-start.20 = (bf16[4,2,192,256]{3,2,1,0:T(8,128)(2,1)}, bf16[4,2,192,256]{3,2,1,0:T(8,128)(2,1)S(1)}, u32[]{:S(2)}, u32[]{:S(2)}) collective-permute-start(bf16[4,2,192,256]{3,2,1,0:T(8,128)(2,1)} %get-tuple-element.46), channel_id=1, source_target_pairs={{0,3},{1,0},{2,1},{3,2},{4,7},{5,4},{6,5},{7,6},{8,11},{9,8},{10,9... | collective-permute-start | bytes 2359304 | tf_op jit(solution)/shard_map/ppermute | solution.py:224
  165.6 1.9 collective-permute-start.15
  167.5 4.0 %collective-permute-start.16 = (bf16[2,192,384]{2,1,0:T(8,128)(2,1)}, bf16[2,192,384]{2,1,0:T(8,128)(2,1)S(1)}, u32[]{:S(2)}, u32[]{:S(2)}) collective-permute-start(bf16[2,192,384]{2,1,0:T(8,128)(2,1)} %get-tuple-element.39), channel_id=1, source_target_pairs={{0,512},{256,768},{512,0},{768,256},{1,513},{257,769},{513,1},{769... | collective-permute-start | bytes 884744 | tf_op jit(solution)/shard_map/ppermute | solution.py:224
  171.5 7.3 %collective-permute-done.18.refs_1_ = bf16[4,2,192,256]{3,2,1,0:T(8,128)(2,1)S(1)} collective-permute-done((bf16[4,2,192,256]{3,2,1,0:T(8,128)(2,1)}, bf16[4,2,192,256]{3,2,1,0:T(8,128)(2,1)S(1)}, u32[]{:S(2)}, u32[]{:S(2)}) %collective-permute-start.18) | collective-permute-done | bytes 786464 | tf_op jit(solution)/shard_map/ppermute | solution.py:224
  178.8 1.9 collective-permute-start.17
  180.7 14.2 %collective-permute-done.19.refs_2_ = bf16[4,2,192,256]{3,2,1,0:T(8,128)(2,1)S(1)} collective-permute-done((bf16[4,2,192,256]{3,2,1,0:T(8,128)(2,1)}, bf16[4,2,192,256]{3,2,1,0:T(8,128)(2,1)S(1)}, u32[]{:S(2)}, u32[]{:S(2)}) %collective-permute-start.19) | collective-permute-done | bytes 786464 | tf_op jit(solution)/shard_map/ppermute | solution.py:224
  195.0 2.7 collective-permute-done.20.refs_3_
  197.6 0.9 copy-done.2
  198.5 3.0 %shard_map.134 = (bf16[2,192,256]{2,1,0:T(8,128)(2,1)}, bf16[2,192,256]{2,1,0:T(8,128)(2,1)}, bf16[2,192,256]{2,1,0:T(8,128)(2,1)}, bf16[2,192,256]{2,1,0:T(8,128)(2,1)}) custom-call(s32[3]{0:T(128)} %pad_add_fusion.self_ref, bf16[4,2,192,256]{3,2,1,0:T(8,128)(2,1)} %get-tuple-element.43.refs_0_, bf16[4,2,192,256]{3,2,1,0:T(8,128)(2,1)} %copy-done, ...), custom_call_target="tpu_custom_call" | custom-call | flops 10000000 | bytes 4194304 | tf_op jit(solution)/shard_map/pallas_call | solution.py:26
  201.6 1.9 collective-permute-start.21
  203.5 2.5 collective-permute-start.22
  206.0 0.0 copy-start.3
  206.0 4.0 %collective-permute-start.23 = (bf16[2,192,256]{2,1,0:T(8,128)(2,1)}, bf16[2,192,256]{2,1,0:T(8,128)(2,1)S(1)}, u32[]{:S(2)}, u32[]{:S(2)}) collective-permute-start(bf16[2,192,256]{2,1,0:T(8,128)(2,1)} %get-tuple-element.50), channel_id=1, source_target_pairs={{0,768},{256,0},{512,256},{768,512},{1,769},{257,1},{513,257},{769... | collective-permute-start | bytes 589832 | tf_op jit(solution)/shard_map/ppermute | solution.py:224
  210.0 0.8 reshape.20
  210.8 0.1 copy.16
  210.9 0.1 copy.17
  211.0 50.8 %all_to_all.14 = f32[256,1,12]{2,1,0:T(1,128)S(1)} all-to-all(f32[256,1,12]{2,1,0:T(1,128)S(1)} %bitcast.26), channel_id=1, replica_groups=mesh['tensor'=4,'expert'=64,'dp'=4] {'tensor','expert'}, dimensions={0} | all-to-all | bytes 24576 | tf_op jit(solution)/shard_map/all_to_all | solution.py:310
  261.9 0.5 broadcast.3
  262.4 1.0 reduce.3
  263.4 0.1 reshape.21
  263.5 0.7 reduce_sum.9.table_ref
  264.1 1.7 shard_map.136
  265.9 0.7 copy-done.4
  266.6 0.1 copy-done.5
  266.7 2.6 shard_map.133
  269.3 0.7 copy-done.6
  270.0 0.0 copy-done.7
  270.0 0.1 copy-done.8
  270.1 2.2 shard_map.135
  (59 shorter events, 0.1 us)
Async XLA Ops:
  3.1 23.7 %collective-permute-start = (bf16[520,128]{1,0:T(8,128)(2,1)}, bf16[520,128]{1,0:T(8,128)(2,1)S(1)}, u32[]{:S(2)}, u32[]{:S(2)}) collective-permute-start(bf16[520,128]{1,0:T(8,128)(2,1)} %shard_map.129.refs_0_), channel_id=1, source_target_pairs={{0,32},{4,36},{8,40},{12,44},{16,48},{20,52},{24,56},{28,60},{32,6... | collective-permute-start | bytes 399368 | tf_op jit(solution)/shard_map/ppermute | solution.py:224
  26.8 0.7 copy-start.9
  31.9 5.0 %copy-start.11 = (bf16[520,128]{1,0:T(8,128)(2,1)S(1)}, bf16[520,128]{1,0:T(8,128)(2,1)}, u32[]{:S(2)}) copy-start(bf16[520,128]{1,0:T(8,128)(2,1)} %shard_map.129.refs_0_) | copy-start | bytes 399364
  31.9 23.8 %copy-start.10 = (bf16[520,128]{1,0:T(8,128)(2,1)S(1)}, bf16[520,128]{1,0:T(8,128)(2,1)}, u32[]{:S(2)}) copy-start(bf16[520,128]{1,0:T(8,128)(2,1)} %copy-done.9) | copy-start | bytes 399364
  31.9 114.8 %all-to-all-start = ((bf16[4,2,192,1408]{3,2,1,0:T(8,128)(2,1)}), bf16[4,2,192,1408]{3,2,1,0:T(8,128)(2,1)}, u32[]{:S(2)}, u32[]{:S(2)}) async-start(bf16[4,2,192,1408]{3,2,1,0:T(8,128)(2,1)} %shard_map.131), calls=%async_computation | async-start | bytes 8650752 | tf_op jit(solution)/shard_map/all_to_all | solution.py:273
  36.9 11.1 %collective-permute-start.3 = (bf16[520,128]{1,0:T(8,128)(2,1)S(1)}, bf16[520,128]{1,0:T(8,128)(2,1)S(1)}, u32[]{:S(2)}, u32[]{:S(2)}) collective-permute-start(bf16[520,128]{1,0:T(8,128)(2,1)S(1)} %copy-done.11), channel_id=1, source_target_pairs={{0,224},{4,228},{8,232},{12,236},{16,240},{20,244},{24,248},{28,25... | collective-permute-start | bytes 399368 | tf_op jit(solution)/shard_map/ppermute | solution.py:224
  48.0 53.6 %copy-start.21 = (bf16[520,128]{1,0:T(8,128)(2,1)}, bf16[520,128]{1,0:T(8,128)(2,1)S(1)}, u32[]{:S(2)}) copy-start(bf16[520,128]{1,0:T(8,128)(2,1)S(1)} %collective-permute-done.3.refs_4_) | copy-start | bytes 399364
  48.0 21.6 %collective-permute-start.4 = (bf16[520,128]{1,0:T(8,128)(2,1)S(1)}, bf16[520,128]{1,0:T(8,128)(2,1)S(1)}, u32[]{:S(2)}, u32[]{:S(2)}) collective-permute-start(bf16[520,128]{1,0:T(8,128)(2,1)S(1)} %collective-permute-done.3.refs_4_), channel_id=1, source_target_pairs={{0,224},{4,228},{8,232},{12,236},{16,240},{20,244},{24,248},{28,25... | collective-permute-start | bytes 399368 | tf_op jit(solution)/shard_map/ppermute | solution.py:224
  55.7 16.1 %collective-permute-start.1 = (bf16[520,128]{1,0:T(8,128)(2,1)S(1)}, bf16[520,128]{1,0:T(8,128)(2,1)S(1)}, u32[]{:S(2)}, u32[]{:S(2)}) collective-permute-start(bf16[520,128]{1,0:T(8,128)(2,1)S(1)} %copy-done.10), channel_id=1, source_target_pairs={{0,32},{4,36},{8,40},{12,44},{16,48},{20,52},{24,56},{28,60},{32,6... | collective-permute-start | bytes 399368 | tf_op jit(solution)/shard_map/ppermute | solution.py:224
  69.6 32.0 %copy-start.22 = (bf16[520,128]{1,0:T(8,128)(2,1)}, bf16[520,128]{1,0:T(8,128)(2,1)S(1)}, u32[]{:S(2)}) copy-start(bf16[520,128]{1,0:T(8,128)(2,1)S(1)} %collective-permute-done.4.refs_5_) | copy-start | bytes 399364
  69.6 11.6 %collective-permute-start.5 = (bf16[520,128]{1,0:T(8,128)(2,1)S(1)}, bf16[520,128]{1,0:T(8,128)(2,1)S(1)}, u32[]{:S(2)}, u32[]{:S(2)}) collective-permute-start(bf16[520,128]{1,0:T(8,128)(2,1)S(1)} %collective-permute-done.4.refs_5_), channel_id=1, source_target_pairs={{0,224},{4,228},{8,232},{12,236},{16,240},{20,244},{24,248},{28,25... | collective-permute-start | bytes 399368 | tf_op jit(solution)/shard_map/ppermute | solution.py:224
  71.8 29.8 %copy-start.23 = (bf16[520,128]{1,0:T(8,128)(2,1)}, bf16[520,128]{1,0:T(8,128)(2,1)S(1)}, u32[]{:S(2)}) copy-start(bf16[520,128]{1,0:T(8,128)(2,1)S(1)} %collective-permute-done.1.refs_2_) | copy-start | bytes 399364
  71.8 14.8 %collective-permute-start.2 = (bf16[520,128]{1,0:T(8,128)(2,1)S(1)}, bf16[520,128]{1,0:T(8,128)(2,1)S(1)}, u32[]{:S(2)}, u32[]{:S(2)}) collective-permute-start(bf16[520,128]{1,0:T(8,128)(2,1)S(1)} %collective-permute-done.1.refs_2_), channel_id=1, source_target_pairs={{0,32},{4,36},{8,40},{12,44},{16,48},{20,52},{24,56},{28,60},{32,6... | collective-permute-start | bytes 399368 | tf_op jit(solution)/shard_map/ppermute | solution.py:224
  81.2 20.4 %copy-start.12 = (bf16[520,128]{1,0:T(8,128)(2,1)}, bf16[520,128]{1,0:T(8,128)(2,1)S(1)}, u32[]{:S(2)}) copy-start(bf16[520,128]{1,0:T(8,128)(2,1)S(1)} %collective-permute-done.5.refs_6_) | copy-start | bytes 399364
  81.2 20.3 %collective-permute-start.7 = (bf16[264,128]{1,0:T(8,128)(2,1)S(1)}, bf16[264,128]{1,0:T(8,128)(2,1)S(1)}, u32[]{:S(2)}, u32[]{:S(2)}) collective-permute-start(bf16[264,128]{1,0:T(8,128)(2,1)S(1)} %slice.9), channel_id=1, source_target_pairs={{0,224},{4,228},{8,232},{12,236},{16,240},{20,244},{24,248},{28,25... | collective-permute-start | bytes 202760 | tf_op jit(solution)/shard_map/ppermute | solution.py:224
  86.6 15.0 %copy-start.13 = (bf16[520,128]{1,0:T(8,128)(2,1)}, bf16[520,128]{1,0:T(8,128)(2,1)S(1)}, u32[]{:S(2)}) copy-start(bf16[520,128]{1,0:T(8,128)(2,1)S(1)} %collective-permute-done.2.refs_3_) | copy-start | bytes 399364
  86.6 14.9 %collective-permute-start.6 = (bf16[256,128]{1,0:T(8,128)(2,1)S(1)}, bf16[256,128]{1,0:T(8,128)(2,1)S(1)}, u32[]{:S(2)}, u32[]{:S(2)}) collective-permute-start(bf16[256,128]{1,0:T(8,128)(2,1)S(1)} %slice.8), channel_id=1, source_target_pairs={{0,32},{4,36},{8,40},{12,44},{16,48},{20,52},{24,56},{28,60},{32,6... | collective-permute-start | bytes 196616 | tf_op jit(solution)/shard_map/ppermute | solution.py:224
  101.6 0.6 copy-start.25
  102.2 0.6 copy-start.24
  107.9 21.2 %collective-permute-start.10 = (bf16[816,128]{1,0:T(8,128)(2,1)}, bf16[816,128]{1,0:T(8,128)(2,1)S(1)}, u32[]{:S(2)}, u32[]{:S(2)}) collective-permute-start(bf16[816,128]{1,0:T(8,128)(2,1)} %get-tuple-element.30), channel_id=1, source_target_pairs={{0,244},{4,248},{8,252},{12,0},{16,4},{20,8},{24,12},{28,16},{32,2... | collective-permute-start | bytes 626696 | tf_op jit(solution)/shard_map/ppermute | solution.py:224
  122.1 11.1 %collective-permute-start.11 = (bf16[816,128]{1,0:T(8,128)(2,1)}, bf16[816,128]{1,0:T(8,128)(2,1)S(1)}, u32[]{:S(2)}, u32[]{:S(2)}) collective-permute-start(bf16[816,128]{1,0:T(8,128)(2,1)} %get-tuple-element.31), channel_id=1, source_target_pairs={{0,8},{4,12},{8,16},{12,20},{16,24},{20,28},{24,32},{28,36},{32,40... | collective-permute-start | bytes 626696 | tf_op jit(solution)/shard_map/ppermute | solution.py:224
  124.1 12.7 %collective-permute-start.12 = (bf16[816,128]{1,0:T(8,128)(2,1)}, bf16[816,128]{1,0:T(8,128)(2,1)S(1)}, u32[]{:S(2)}, u32[]{:S(2)}) collective-permute-start(bf16[816,128]{1,0:T(8,128)(2,1)} %get-tuple-element.32), channel_id=1, source_target_pairs={{0,248},{4,252},{8,0},{12,4},{16,8},{20,12},{24,16},{28,20},{32,24... | collective-permute-start | bytes 626696 | tf_op jit(solution)/shard_map/ppermute | solution.py:224
  128.6 8.1 %collective-permute-start.13 = (bf16[816,128]{1,0:T(8,128)(2,1)}, bf16[816,128]{1,0:T(8,128)(2,1)S(1)}, u32[]{:S(2)}, u32[]{:S(2)}) collective-permute-start(bf16[816,128]{1,0:T(8,128)(2,1)} %get-tuple-element.33), channel_id=1, source_target_pairs={{0,4},{4,8},{8,12},{12,16},{16,20},{20,24},{24,28},{28,32},{32,36}... | collective-permute-start | bytes 626696 | tf_op jit(solution)/shard_map/ppermute | solution.py:224
  129.0 9.5 %collective-permute-start.14 = (bf16[816,128]{1,0:T(8,128)(2,1)}, bf16[816,128]{1,0:T(8,128)(2,1)S(1)}, u32[]{:S(2)}, u32[]{:S(2)}) collective-permute-start(bf16[816,128]{1,0:T(8,128)(2,1)} %get-tuple-element.34), channel_id=1, source_target_pairs={{0,252},{4,0},{8,4},{12,8},{16,12},{20,16},{24,20},{28,24},{32,28}... | collective-permute-start | bytes 626696 | tf_op jit(solution)/shard_map/ppermute | solution.py:224
  129.2 17.5 %copy-start.14 = (bf16[816,128]{1,0:T(8,128)(2,1)}, bf16[816,128]{1,0:T(8,128)(2,1)S(1)}, u32[]{:S(2)}) copy-start(bf16[816,128]{1,0:T(8,128)(2,1)S(1)} %collective-permute-done.10.refs_2_) | copy-start | bytes 626692
  129.2 12.2 %collective-permute-start.8 = (bf16[816,128]{1,0:T(8,128)(2,1)}, bf16[816,128]{1,0:T(8,128)(2,1)S(1)}, u32[]{:S(2)}, u32[]{:S(2)}) collective-permute-start(bf16[816,128]{1,0:T(8,128)(2,1)} %get-tuple-element.28), channel_id=1, source_target_pairs={{0,240},{4,244},{8,248},{12,252},{16,0},{20,4},{24,8},{28,12},{32,... | collective-permute-start | bytes 626696 | tf_op jit(solution)/shard_map/ppermute | solution.py:224
  133.2 13.5 %copy-start.15 = (bf16[816,128]{1,0:T(8,128)(2,1)}, bf16[816,128]{1,0:T(8,128)(2,1)S(1)}, u32[]{:S(2)}) copy-start(bf16[816,128]{1,0:T(8,128)(2,1)S(1)} %collective-permute-done.11.refs_3_) | copy-start | bytes 626692
  133.2 13.5 %collective-permute-start.9 = (bf16[816,128]{1,0:T(8,128)(2,1)}, bf16[816,128]{1,0:T(8,128)(2,1)S(1)}, u32[]{:S(2)}, u32[]{:S(2)}) collective-permute-start(bf16[816,128]{1,0:T(8,128)(2,1)} %get-tuple-element.29), channel_id=1, source_target_pairs={{0,12},{4,16},{8,20},{12,24},{16,28},{20,32},{24,36},{28,40},{32,4... | collective-permute-start | bytes 626696 | tf_op jit(solution)/shard_map/ppermute | solution.py:224
  136.7 10.0 %copy-start.16 = (bf16[816,128]{1,0:T(8,128)(2,1)}, bf16[816,128]{1,0:T(8,128)(2,1)S(1)}, u32[]{:S(2)}) copy-start(bf16[816,128]{1,0:T(8,128)(2,1)S(1)} %collective-permute-done.12.refs_4_) | copy-start | bytes 626692
  136.7 10.0 %copy-start.17 = (bf16[816,128]{1,0:T(8,128)(2,1)}, bf16[816,128]{1,0:T(8,128)(2,1)S(1)}, u32[]{:S(2)}) copy-start(bf16[816,128]{1,0:T(8,128)(2,1)S(1)} %collective-permute-done.13.refs_5_) | copy-start | bytes 626692
  138.5 8.3 %copy-start.18 = (bf16[816,128]{1,0:T(8,128)(2,1)}, bf16[816,128]{1,0:T(8,128)(2,1)S(1)}, u32[]{:S(2)}) copy-start(bf16[816,128]{1,0:T(8,128)(2,1)S(1)} %collective-permute-done.14.refs_6_) | copy-start | bytes 626692
  141.3 5.4 %copy-start.19 = (bf16[816,128]{1,0:T(8,128)(2,1)}, bf16[816,128]{1,0:T(8,128)(2,1)S(1)}, u32[]{:S(2)}) copy-start(bf16[816,128]{1,0:T(8,128)(2,1)S(1)} %collective-permute-done.8.refs_0_) | copy-start | bytes 626692
  146.7 0.7 copy-start.20
  156.4 22.4 %collective-permute-start.18 = (bf16[4,2,192,256]{3,2,1,0:T(8,128)(2,1)}, bf16[4,2,192,256]{3,2,1,0:T(8,128)(2,1)S(1)}, u32[]{:S(2)}, u32[]{:S(2)}) collective-permute-start(bf16[4,2,192,256]{3,2,1,0:T(8,128)(2,1)} %get-tuple-element.44), channel_id=1, source_target_pairs={{0,1},{1,2},{2,3},{3,0},{4,5},{5,6},{6,7},{7,4},{8,9},{9,10},{10,1... | collective-permute-start | bytes 2359304 | tf_op jit(solution)/shard_map/ppermute | solution.py:224
  158.3 36.6 %collective-permute-start.19 = (bf16[4,2,192,256]{3,2,1,0:T(8,128)(2,1)}, bf16[4,2,192,256]{3,2,1,0:T(8,128)(2,1)S(1)}, u32[]{:S(2)}, u32[]{:S(2)}) collective-permute-start(bf16[4,2,192,256]{3,2,1,0:T(8,128)(2,1)} %get-tuple-element.45), channel_id=1, source_target_pairs={{0,2},{1,3},{2,0},{3,1},{4,6},{5,7},{6,4},{7,5},{8,10},{9,11},{10,... | collective-permute-start | bytes 2359304 | tf_op jit(solution)/shard_map/ppermute | solution.py:224
  162.5 35.1 %collective-permute-start.20 = (bf16[4,2,192,256]{3,2,1,0:T(8,128)(2,1)}, bf16[4,2,192,256]{3,2,1,0:T(8,128)(2,1)S(1)}, u32[]{:S(2)}, u32[]{:S(2)}) collective-permute-start(bf16[4,2,192,256]{3,2,1,0:T(8,128)(2,1)} %get-tuple-element.46), channel_id=1, source_target_pairs={{0,3},{1,0},{2,1},{3,2},{4,7},{5,4},{6,5},{7,6},{8,11},{9,8},{10,9... | collective-permute-start | bytes 2359304 | tf_op jit(solution)/shard_map/ppermute | solution.py:224
  165.6 40.4 %collective-permute-start.15 = (bf16[2,192,384]{2,1,0:T(8,128)(2,1)}, bf16[2,192,384]{2,1,0:T(8,128)(2,1)S(1)}, u32[]{:S(2)}, u32[]{:S(2)}) collective-permute-start(bf16[2,192,384]{2,1,0:T(8,128)(2,1)} %get-tuple-element.38), channel_id=1, source_target_pairs={{0,256},{256,512},{512,768},{768,0},{1,257},{257,513},{513,769},{7... | collective-permute-start | bytes 884744 | tf_op jit(solution)/shard_map/ppermute | solution.py:224
  167.5 98.4 %collective-permute-start.16 = (bf16[2,192,384]{2,1,0:T(8,128)(2,1)}, bf16[2,192,384]{2,1,0:T(8,128)(2,1)S(1)}, u32[]{:S(2)}, u32[]{:S(2)}) collective-permute-start(bf16[2,192,384]{2,1,0:T(8,128)(2,1)} %get-tuple-element.39), channel_id=1, source_target_pairs={{0,512},{256,768},{512,0},{768,256},{1,513},{257,769},{513,1},{769... | collective-permute-start | bytes 884744 | tf_op jit(solution)/shard_map/ppermute | solution.py:224
  178.8 18.8 %copy-start = (bf16[4,2,192,256]{3,2,1,0:T(8,128)(2,1)}, bf16[4,2,192,256]{3,2,1,0:T(8,128)(2,1)S(1)}, u32[]{:S(2)}) copy-start(bf16[4,2,192,256]{3,2,1,0:T(8,128)(2,1)S(1)} %collective-permute-done.18.refs_1_) | copy-start | bytes 2359300
  178.8 87.0 %collective-permute-start.17 = (bf16[2,192,384]{2,1,0:T(8,128)(2,1)}, bf16[2,192,384]{2,1,0:T(8,128)(2,1)S(1)}, u32[]{:S(2)}, u32[]{:S(2)}) collective-permute-start(bf16[2,192,384]{2,1,0:T(8,128)(2,1)} %get-tuple-element.40), channel_id=1, source_target_pairs={{0,768},{256,0},{512,256},{768,512},{1,769},{257,1},{513,257},{769... | collective-permute-start | bytes 884744 | tf_op jit(solution)/shard_map/ppermute | solution.py:224
  195.0 2.7 copy-start.1
  197.6 0.9 copy-start.2
  201.6 67.7 %collective-permute-start.21 = (bf16[2,192,256]{2,1,0:T(8,128)(2,1)}, bf16[2,192,256]{2,1,0:T(8,128)(2,1)S(1)}, u32[]{:S(2)}, u32[]{:S(2)}) collective-permute-start(bf16[2,192,256]{2,1,0:T(8,128)(2,1)} %get-tuple-element.48), channel_id=1, source_target_pairs={{0,256},{256,512},{512,768},{768,0},{1,257},{257,513},{513,769},{7... | collective-permute-start | bytes 589832 | tf_op jit(solution)/shard_map/ppermute | solution.py:224
  203.5 65.8 %collective-permute-start.22 = (bf16[2,192,256]{2,1,0:T(8,128)(2,1)}, bf16[2,192,256]{2,1,0:T(8,128)(2,1)S(1)}, u32[]{:S(2)}, u32[]{:S(2)}) collective-permute-start(bf16[2,192,256]{2,1,0:T(8,128)(2,1)} %get-tuple-element.49), channel_id=1, source_target_pairs={{0,512},{256,768},{512,0},{768,256},{1,513},{257,769},{513,1},{769... | collective-permute-start | bytes 589832 | tf_op jit(solution)/shard_map/ppermute | solution.py:224
  206.0 59.9 %copy-start.3 = (bf16[2,192,384]{2,1,0:T(8,128)(2,1)}, bf16[2,192,384]{2,1,0:T(8,128)(2,1)S(1)}, u32[]{:S(2)}) copy-start(bf16[2,192,384]{2,1,0:T(8,128)(2,1)S(1)} %collective-permute-done.15.refs_1_) | copy-start | bytes 884740
  206.0 63.3 %collective-permute-start.23 = (bf16[2,192,256]{2,1,0:T(8,128)(2,1)}, bf16[2,192,256]{2,1,0:T(8,128)(2,1)S(1)}, u32[]{:S(2)}, u32[]{:S(2)}) collective-permute-start(bf16[2,192,256]{2,1,0:T(8,128)(2,1)} %get-tuple-element.50), channel_id=1, source_target_pairs={{0,768},{256,0},{512,256},{768,512},{1,769},{257,1},{513,257},{769... | collective-permute-start | bytes 589832 | tf_op jit(solution)/shard_map/ppermute | solution.py:224
  265.9 0.7 copy-start.4
  265.9 0.8 copy-start.5
  269.3 0.7 copy-start.6
  269.3 0.7 copy-start.7
  269.3 0.8 copy-start.8

commit v3 on v2

--- a/solution.py
+++ b/solution.py
@@ -42,6 +42,10 @@
     return lax.dot_general(a, b, (((1,), (1,)), ((), ())), preferred_element_type=jnp.float32)
 
 
+def way(self_ref):
+    return 1 - 2 * (self_ref[0] & 1)
+
+
 def earlier_matrix(n, block):
     row = lax.broadcasted_iota(jnp.int32, (n, n), 0)
     col = lax.broadcasted_iota(jnp.int32, (n, n), 1)
@@ -79,8 +83,7 @@
     routes.append(blocks[8][256:264, :].astype(jnp.float32))
     ids = jnp.concatenate([r[:, :64] for r in routes], axis=1)
     probs = jnp.concatenate([r[:, 64:] for r in routes], axis=1)
-    base = exp_ref[...]
-    mine = (2 * s + base) & 127
+    mine = (2 * (s + way(self_ref) * exp_ref[:, :1]) + exp_ref[:, 1:2]) & 127
     mine = mine.astype(jnp.float32)
     match = jnp.zeros((16, 512), jnp.float32)
     prob = jnp.zeros((16, 512), jnp.float32)
@@ -124,6 +127,7 @@
     dots_ref, prob_ref = refs[17:19]
     arrived_ref, rows_ref, scaled_ref = refs[19:]
     s, t, r = self_ref[0], self_ref[1], self_ref[2]
+    turn = way(self_ref)
     for v in range(8):
         for c in range(8):
             for e in range(2):
@@ -139,7 +143,8 @@
         mine = place_ref[2:3, :] == v
         probs = jnp.where(mine, wide, probs)
     low = probs.astype(jnp.bfloat16)
-    target = ((s + place_ref[0:1, :]) & 63) * 6 + place_ref[1:2, :]
+    sign = 1 - 2 * ((s + place_ref[3:4, :]) & 1)
+    target = ((s + sign * place_ref[0:1, :]) & 63) * 6 + place_ref[1:2, :]
     row = lax.broadcasted_iota(jnp.int32, (384, 384), 0)
     for e in range(2):
         perm = jnp.where(row == target[:, e * 384 : (e + 1) * 384], 1.0, 0.0).astype(jnp.bfloat16)
@@ -154,7 +159,7 @@
     for e in range(2):
         hidden = jnp.concatenate([wh_ref[k, e, :, 1024:1408] for k in range(4)], axis=0)
         for rho in range(4):
-            start = pl.multiple_of(((r + rho) & 3) * 256, 256)
+            start = pl.multiple_of(((r + turn * rho) & 3) * 256, 256)
             part = dot(hidden, scaled_ref[e * 384 : (e + 1) * 384, pl.ds(start, 256)])
             part = part.astype(jnp.bfloat16)
             for k in range(4):
@@ -162,7 +167,7 @@
     for e in range(2):
         total = jnp.zeros((1, 384), jnp.float32)
         for delta in range(4):
-            k = (t + delta) & 3
+            k = (t + turn * delta) & 3
             part = dot_nt(wh_ref[k, e, :, :1024], rows_ref[e * 384 : (e + 1) * 384, :])
             gh_refs[delta][e] = part.astype(jnp.bfloat16)
             hidden = wh_ref[k, e, :, 1024:1408].astype(jnp.float32)
@@ -187,7 +192,7 @@
 def replica_body(self_ref, *refs):
     parts, outs = refs[:4], refs[4:]
     for delta in range(4):
-        k = (self_ref[1] + delta) & 3
+        k = (self_ref[1] + way(self_ref) * delta) & 3
         for e in range(2):
             total = parts[0][k, e].astype(jnp.float32)
             for part in parts[1:]:
@@ -198,7 +203,7 @@
 def place_body(self_ref, *refs):
     parts, out_ref = refs[:4], refs[4]
     for delta in range(4):
-        start = pl.multiple_of(((self_ref[1] - delta) & 3) * 256, 256)
+        start = pl.multiple_of(((self_ref[1] - way(self_ref) * delta) & 3) * 256, 256)
         for e in range(2):
             out_ref[e, :, pl.ds(start, 256)] = parts[delta][e]
 
@@ -220,8 +225,22 @@
 
 
 def shifted(x, by, axis):
-    count = lax.axis_size(axis)
-    return lax.ppermute(x, axis, [(i, (i + by) % count) for i in range(count)])
+    count, others = lax.axis_size(axis), lax.axis_size("expert")
+    if axis == "expert":
+        axes, pairs = axis, [(i, (i + by * (1 - 2 * (i & 1))) % count) for i in range(count)]
+    else:
+        major = axis == "tensor"
+        axes = (axis, "expert") if major else ("expert", axis)
+
+        def at(s, i):
+            return i * others + s if major else s * count + i
+
+        pairs = [
+            (at(s, i), at(s, (i + by * (1 - 2 * (s & 1))) % count))
+            for s in range(others)
+            for i in range(count)
+        ]
+    return lax.ppermute(x, axes, pairs)
 
 
 def spread(parts, axis):
@@ -234,12 +253,13 @@
     onehot[row, row // 48] = 1.0
     code = (row % 48).astype(np.float32)[:, None]
     shift = np.array(SHIFTS)
-    expert = (2 * shift[None, :] + np.arange(2)[:, None]).reshape(16, 1).astype(np.int32)
+    expert = np.stack([np.tile(shift, 2), np.repeat(np.arange(2), 8)], axis=1).astype(np.int32)
     piece, o, j = (row % 384) // 48, (row // 6) % 8, row % 6
     tables = np.zeros((8, 768), np.int32)
     tables[0] = STRIDE * np.array(OFFSETS)[o] - shift[piece]
     tables[1] = j
     tables[2] = piece
+    tables[3] = shift[piece] & 1
     return onehot, code, expert, tables
 
 
@@ -265,7 +285,7 @@
         w,
         gate_t,
         up_t,
-        blocks[-1],
+        packed,
         untouched=(3,),
         flops=10**7,
         moved=8 * 1024 * 1024,

time: 273 us -> 261 us (0.956)
  waiting for transfers between devices: 69.7 us -> 57.6 us
  starting transfers between devices: 112 us -> 107 us
  blocking collectives: 50.8 us -> 55.6 us
    ppermute x24, waiting for transfers between devices: 69.7 us -> 57.6 us  [shifted(): return lax.ppermute(x, axes, pairs)]
    all_to_all x1, blocking collectives: 50.8 us -> 55.6 us  [backward(): lax.all_to_all(cells, ('tensor', 'expert'), split_axis=0, concat_axis=0,...]
    ppermute x24, starting transfers between devices: 107 us -> 102 us  [shifted(): return lax.ppermute(x, axes, pairs)]
  transfers between devices with their start and end apart: 25 -> 25, of which waited for: 11 -> 9; matrix products, arithmetic and copies ran while one was open for 1% -> 1% of each run, Pallas kernels for 5% -> 5%
where the time goes in v3:
time: 261 us; the launch traced here: 260 us
  starting transfers between devices  107 us (41%)
  waiting for transfers between devices  57.6 us (22%)
  blocking collectives  55.6 us (21%)
  Pallas kernels  30.3 us (12%)
  local copies, waits for them, and re-layouts  5.96 us (2%)
    ppermute x24, starting transfers between devices, shifted(): return lax.ppermute(x, axes, pairs)  102 us
    ppermute x24, waiting for transfers between devices, shifted(): return lax.ppermute(x, axes, pairs)  57.6 us
    all_to_all x1, blocking collectives, backward(): lax.all_to_all(cells, ('tensor', 'expert'), split_axis=0, concat_axis=0,...  55.6 us
    pallas_call x8, Pallas kernels, call(): pl.pallas_call(body, out_shape=outs, in_specs=specs, out_specs=jax.tree.m...  30.3 us
  transfers between devices with their start and end apart: 25, of which 9 were waited for; matrix products, arithmetic and copies ran while one was open for 1% of the time, Pallas kernels for 5%

profile of v3, /device:TPU:1, one launch (start us, length us, event | category | flops | bytes accessed | tf_op | source)
XLA Modules:
  0.0 259.9 jit_solution(4997935930199541825)
XLA Ops:
  0.6 0.6 pad_add_fusion.self_ref
  1.3 1.8 shard_map.129.refs_0_._
  3.1 4.5 %shard_map.131 = bf16[4,2,192,1408]{3,2,1,0:T(8,128)(2,1)} custom-call(bf16[2,192,4096]{2,1,0:T(8,128)(2,1)} %w_ref.1, bf16[2,192,384]{2,1,0:T(8,128)(2,1)} %bitcast.22, bf16[2,192,384]{2,1,0:T(8,128)(2,1)} %bitcast.24, bf16[520,128]{1,0:T(8,128)(2,1)} %shard_map.129.refs_0_._), custom_call_target="tpu_custom_call" | custom-call | flops 10000000 | bytes 8388608 | tf_op jit(solution)/shard_map/pallas_call | solution.py:26
  7.5 5.1 %all-to-all-start = ((bf16[4,2,192,1408]{3,2,1,0:T(8,128)(2,1)}), bf16[4,2,192,1408]{3,2,1,0:T(8,128)(2,1)}, u32[]{:S(2)}, u32[]{:S(2)}) async-start(bf16[4,2,192,1408]{3,2,1,0:T(8,128)(2,1)} %shard_map.131), calls=%async_computation | async-start | bytes 8650752 | tf_op jit(solution)/shard_map/all_to_all | solution.py:293
  12.7 9.5 %collective-permute-start.3 = (bf16[520,128]{1,0:T(8,128)(2,1)S(1)}, bf16[520,128]{1,0:T(8,128)(2,1)S(1)}, u32[]{:S(2)}, u32[]{:S(2)}) collective-permute-start(bf16[520,128]{1,0:T(8,128)(2,1)S(1)} %copy-done.3), channel_id=1, source_target_pairs={{0,224},{4,36},{8,232},{12,44},{16,240},{20,52},{24,248},{28,60},{... | collective-permute-start | bytes 399368 | tf_op jit(solution)/shard_map/ppermute | solution.py:243
  22.2 12.8 %collective-permute-start = (bf16[520,128]{1,0:T(8,128)(2,1)S(1)}, bf16[520,128]{1,0:T(8,128)(2,1)S(1)}, u32[]{:S(2)}, u32[]{:S(2)}) collective-permute-start(bf16[520,128]{1,0:T(8,128)(2,1)S(1)} %copy-done.3), channel_id=1, source_target_pairs={{0,32},{4,228},{8,40},{12,236},{16,48},{20,244},{24,56},{28,252},{... | collective-permute-start | bytes 399368 | tf_op jit(solution)/shard_map/ppermute | solution.py:243
  35.0 0.8 collective-permute-done.3.refs_4_
  35.9 1.9 collective-permute-start.4
  37.8 8.4 %collective-permute-done.refs_1_ = bf16[520,128]{1,0:T(8,128)(2,1)S(1)} collective-permute-done((bf16[520,128]{1,0:T(8,128)(2,1)S(1)}, bf16[520,128]{1,0:T(8,128)(2,1)S(1)}, u32[]{:S(2)}, u32[]{:S(2)}) %collective-permute-start) | collective-permute-done | bytes 133152 | tf_op jit(solution)/shard_map/ppermute | solution.py:243
  46.1 8.0 %collective-permute-start.1 = (bf16[520,128]{1,0:T(8,128)(2,1)S(1)}, bf16[520,128]{1,0:T(8,128)(2,1)S(1)}, u32[]{:S(2)}, u32[]{:S(2)}) collective-permute-start(bf16[520,128]{1,0:T(8,128)(2,1)S(1)} %collective-permute-done.refs_1_), channel_id=1, source_target_pairs={{0,32},{4,228},{8,40},{12,236},{16,48},{20,244},{24,56},{28,252},{... | collective-permute-start | bytes 399368 | tf_op jit(solution)/shard_map/ppermute | solution.py:243
  54.2 0.0 collective-permute-done.4.refs_5_
  54.2 1.9 collective-permute-start.5
  56.1 7.1 %collective-permute-done.1.refs_2_ = bf16[520,128]{1,0:T(8,128)(2,1)S(1)} collective-permute-done((bf16[520,128]{1,0:T(8,128)(2,1)S(1)}, bf16[520,128]{1,0:T(8,128)(2,1)S(1)}, u32[]{:S(2)}, u32[]{:S(2)}) %collective-permute-start.1) | collective-permute-done | bytes 133152 | tf_op jit(solution)/shard_map/ppermute | solution.py:243
  63.2 8.1 %collective-permute-start.2 = (bf16[520,128]{1,0:T(8,128)(2,1)S(1)}, bf16[520,128]{1,0:T(8,128)(2,1)S(1)}, u32[]{:S(2)}, u32[]{:S(2)}) collective-permute-start(bf16[520,128]{1,0:T(8,128)(2,1)S(1)} %collective-permute-done.1.refs_2_), channel_id=1, source_target_pairs={{0,32},{4,228},{8,40},{12,236},{16,48},{20,244},{24,56},{28,252},{... | collective-permute-start | bytes 399368 | tf_op jit(solution)/shard_map/ppermute | solution.py:243
  71.4 0.0 collective-permute-done.5.refs_6_
  71.4 1.9 collective-permute-start.7
  73.4 7.0 %collective-permute-done.2.refs_3_ = bf16[520,128]{1,0:T(8,128)(2,1)S(1)} collective-permute-done((bf16[520,128]{1,0:T(8,128)(2,1)S(1)}, bf16[520,128]{1,0:T(8,128)(2,1)S(1)}, u32[]{:S(2)}, u32[]{:S(2)}) %collective-permute-start.2) | collective-permute-done | bytes 133152 | tf_op jit(solution)/shard_map/ppermute | solution.py:243
  80.3 4.7 %collective-permute-start.6 = (bf16[256,128]{1,0:T(8,128)(2,1)S(1)}, bf16[256,128]{1,0:T(8,128)(2,1)S(1)}, u32[]{:S(2)}, u32[]{:S(2)}) collective-permute-start(bf16[256,128]{1,0:T(8,128)(2,1)S(1)} %slice.8), channel_id=1, source_target_pairs={{0,32},{4,228},{8,40},{12,236},{16,48},{20,244},{24,56},{28,252},{... | collective-permute-start | bytes 196616 | tf_op jit(solution)/shard_map/ppermute | solution.py:243
  85.1 4.7 %collective-permute-done.6.refs_7_ = bf16[256,128]{1,0:T(8,128)(2,1)S(1)} collective-permute-done((bf16[256,128]{1,0:T(8,128)(2,1)S(1)}, bf16[256,128]{1,0:T(8,128)(2,1)S(1)}, u32[]{:S(2)}, u32[]{:S(2)}) %collective-permute-start.6) | collective-permute-done | bytes 65568 | tf_op jit(solution)/shard_map/ppermute | solution.py:243
  89.8 0.0 collective-permute-done.7.refs_8_
  89.8 0.6 copy-done.24
  90.4 0.6 copy-done.23
  91.0 5.2 %shard_map.130 = (bf16[816,128]{1,0:T(8,128)(2,1)}, bf16[816,128]{1,0:T(8,128)(2,1)}, bf16[816,128]{1,0:T(8,128)(2,1)}, bf16[816,128]{1,0:T(8,128)(2,1)}, bf16[8...) custom-call(s32[3]{0:T(128)} %pad_add_fusion.self_ref, ...), custom_call_target="tpu_custom_call" | custom-call | flops 805306368 | bytes 4194304 | tf_op jit(solution)/shard_map/pallas_call | solution.py:26
  96.2 6.5 %collective-permute-start.10 = (bf16[816,128]{1,0:T(8,128)(2,1)}, bf16[816,128]{1,0:T(8,128)(2,1)S(1)}, u32[]{:S(2)}, u32[]{:S(2)}) collective-permute-start(bf16[816,128]{1,0:T(8,128)(2,1)} %get-tuple-element.30), channel_id=1, source_target_pairs={{0,244},{4,16},{8,252},{12,24},{16,4},{20,32},{24,12},{28,40},{32,... | collective-permute-start | bytes 626696 | tf_op jit(solution)/shard_map/ppermute | solution.py:243
  102.7 3.3 %collective-permute-start.11 = (bf16[816,128]{1,0:T(8,128)(2,1)}, bf16[816,128]{1,0:T(8,128)(2,1)S(1)}, u32[]{:S(2)}, u32[]{:S(2)}) collective-permute-start(bf16[816,128]{1,0:T(8,128)(2,1)} %get-tuple-element.31), channel_id=1, source_target_pairs={{0,8},{4,252},{8,16},{12,4},{16,24},{20,12},{24,32},{28,20},{32,40... | collective-permute-start | bytes 626696 | tf_op jit(solution)/shard_map/ppermute | solution.py:243
  106.1 1.9 collective-permute-start.12
  108.0 5.5 %collective-permute-start.13 = (bf16[816,128]{1,0:T(8,128)(2,1)}, bf16[816,128]{1,0:T(8,128)(2,1)S(1)}, u32[]{:S(2)}, u32[]{:S(2)}) collective-permute-start(bf16[816,128]{1,0:T(8,128)(2,1)} %get-tuple-element.33), channel_id=1, source_target_pairs={{0,4},{4,0},{8,12},{12,8},{16,20},{20,16},{24,28},{28,24},{32,36},... | collective-permute-start | bytes 626696 | tf_op jit(solution)/shard_map/ppermute | solution.py:243
  113.6 2.3 collective-permute-start.14
  115.9 3.1 %collective-permute-start.8 = (bf16[816,128]{1,0:T(8,128)(2,1)}, bf16[816,128]{1,0:T(8,128)(2,1)S(1)}, u32[]{:S(2)}, u32[]{:S(2)}) collective-permute-start(bf16[816,128]{1,0:T(8,128)(2,1)} %get-tuple-element.28), channel_id=1, source_target_pairs={{0,240},{4,20},{8,248},{12,28},{16,0},{20,36},{24,8},{28,44},{32,1... | collective-permute-start | bytes 626696 | tf_op jit(solution)/shard_map/ppermute | solution.py:243
  119.0 3.6 %collective-permute-start.9 = (bf16[816,128]{1,0:T(8,128)(2,1)}, bf16[816,128]{1,0:T(8,128)(2,1)S(1)}, u32[]{:S(2)}, u32[]{:S(2)}) collective-permute-start(bf16[816,128]{1,0:T(8,128)(2,1)} %get-tuple-element.29), channel_id=1, source_target_pairs={{0,12},{4,248},{8,20},{12,0},{16,28},{20,8},{24,36},{28,16},{32,44... | collective-permute-start | bytes 626696 | tf_op jit(solution)/shard_map/ppermute | solution.py:243
  122.7 2.1 collective-permute-done.8.refs_0_
  124.9 4.4 %collective-permute-done.9.refs_1_ = bf16[816,128]{1,0:T(8,128)(2,1)S(1)} collective-permute-done((bf16[816,128]{1,0:T(8,128)(2,1)}, bf16[816,128]{1,0:T(8,128)(2,1)S(1)}, u32[]{:S(2)}, u32[]{:S(2)}) %collective-permute-start.9) | collective-permute-done | bytes 208928 | tf_op jit(solution)/shard_map/ppermute | solution.py:243
  129.3 0.6 copy-done.18
  129.9 9.3 %shard_map.132 = (bf16[2,192,384]{2,1,0:T(8,128)(2,1)}, bf16[2,192,384]{2,1,0:T(8,128)(2,1)}, bf16[2,192,384]{2,1,0:T(8,128)(2,1)}, bf16[2,192,384]{2,1,0:T(8,12...) custom-call(s32[3]{0:T(128)} %pad_add_fusion.self_ref, ...), custom_call_target="tpu_custom_call" | custom-call | flops 6000000000 | bytes 12582912 | tf_op jit(solution)/shard_map/pallas_call | solution.py:26
  139.2 4.0 %collective-permute-start.18 = (bf16[4,2,192,256]{3,2,1,0:T(8,128)(2,1)}, bf16[4,2,192,256]{3,2,1,0:T(8,128)(2,1)S(1)}, u32[]{:S(2)}, u32[]{:S(2)}) collective-permute-start(bf16[4,2,192,256]{3,2,1,0:T(8,128)(2,1)} %get-tuple-element.44), channel_id=1, source_target_pairs={{0,1},{1,2},{2,3},{3,0},{4,7},{5,4},{6,5},{7,6},{8,9},{9,10},{10,1... | collective-permute-start | bytes 2359304 | tf_op jit(solution)/shard_map/ppermute | solution.py:243
  143.3 2.4 collective-permute-start.19
  145.7 2.5 collective-permute-start.20
  148.2 3.6 %collective-permute-start.15 = (bf16[2,192,384]{2,1,0:T(8,128)(2,1)}, bf16[2,192,384]{2,1,0:T(8,128)(2,1)S(1)}, u32[]{:S(2)}, u32[]{:S(2)}) collective-permute-start(bf16[2,192,384]{2,1,0:T(8,128)(2,1)} %get-tuple-element.38), channel_id=1, source_target_pairs={{0,256},{256,512},{512,768},{768,0},{4,772},{260,4},{516,260},{772... | collective-permute-start | bytes 884744 | tf_op jit(solution)/shard_map/ppermute | solution.py:243
  151.8 2.8 %collective-permute-start.16 = (bf16[2,192,384]{2,1,0:T(8,128)(2,1)}, bf16[2,192,384]{2,1,0:T(8,128)(2,1)S(1)}, u32[]{:S(2)}, u32[]{:S(2)}) collective-permute-start(bf16[2,192,384]{2,1,0:T(8,128)(2,1)} %get-tuple-element.39), channel_id=1, source_target_pairs={{0,512},{256,768},{512,0},{768,256},{4,516},{260,772},{516,4},{772... | collective-permute-start | bytes 884744 | tf_op jit(solution)/shard_map/ppermute | solution.py:243
  154.6 16.9 %collective-permute-done.18.refs_1_ = bf16[4,2,192,256]{3,2,1,0:T(8,128)(2,1)S(1)} collective-permute-done((bf16[4,2,192,256]{3,2,1,0:T(8,128)(2,1)}, bf16[4,2,192,256]{3,2,1,0:T(8,128)(2,1)S(1)}, u32[]{:S(2)}, u32[]{:S(2)}) %collective-permute-start.18) | collective-permute-done | bytes 786464 | tf_op jit(solution)/shard_map/ppermute | solution.py:243
  171.6 1.9 collective-permute-start.17
  173.5 6.1 %collective-permute-done.20.refs_3_ = bf16[4,2,192,256]{3,2,1,0:T(8,128)(2,1)S(1)} collective-permute-done((bf16[4,2,192,256]{3,2,1,0:T(8,128)(2,1)}, bf16[4,2,192,256]{3,2,1,0:T(8,128)(2,1)S(1)}, u32[]{:S(2)}, u32[]{:S(2)}) %collective-permute-start.20) | collective-permute-done | bytes 786464 | tf_op jit(solution)/shard_map/ppermute | solution.py:243
  179.6 0.9 copy-done.2
  180.5 3.0 %shard_map.134 = (bf16[2,192,256]{2,1,0:T(8,128)(2,1)}, bf16[2,192,256]{2,1,0:T(8,128)(2,1)}, bf16[2,192,256]{2,1,0:T(8,128)(2,1)}, bf16[2,192,256]{2,1,0:T(8,128)(2,1)}) custom-call(s32[3]{0:T(128)} %pad_add_fusion.self_ref, bf16[4,2,192,256]{3,2,1,0:T(8,128)(2,1)} %get-tuple-element.43.refs_0_, bf16[4,2,192,256]{3,2,1,0:T(8,128)(2,1)} %copy-done, ...), custom_call_target="tpu_custom_call" | custom-call | flops 10000000 | bytes 4194304 | tf_op jit(solution)/shard_map/pallas_call | solution.py:26
  183.6 4.9 %collective-permute-start.21 = (bf16[2,192,256]{2,1,0:T(8,128)(2,1)}, bf16[2,192,256]{2,1,0:T(8,128)(2,1)S(1)}, u32[]{:S(2)}, u32[]{:S(2)}) collective-permute-start(bf16[2,192,256]{2,1,0:T(8,128)(2,1)} %get-tuple-element.48), channel_id=1, source_target_pairs={{0,256},{256,512},{512,768},{768,0},{4,772},{260,4},{516,260},{772... | collective-permute-start | bytes 589832 | tf_op jit(solution)/shard_map/ppermute | solution.py:243
  188.4 1.9 collective-permute-start.22
  190.4 0.0 copy-start.4
  190.4 2.5 collective-permute-start.23
  192.9 0.8 reshape.20
  193.7 0.1 copy.16
  193.8 0.1 copy.17
  193.9 55.6 %all_to_all.14 = f32[256,1,12]{2,1,0:T(1,128)S(1)} all-to-all(f32[256,1,12]{2,1,0:T(1,128)S(1)} %bitcast.26), channel_id=1, replica_groups=mesh['tensor'=4,'expert'=64,'dp'=4] {'tensor','expert'}, dimensions={0} | all-to-all | bytes 24576 | tf_op jit(solution)/shard_map/all_to_all | solution.py:330
  249.5 0.5 broadcast.3
  250.0 1.0 reduce.3
  251.0 0.1 reshape.21
  251.1 0.7 reduce_sum.9.table_ref
  251.8 1.7 shard_map.136
  253.5 0.7 copy-done.5
  254.2 0.1 copy-done.6
  254.3 2.6 shard_map.133
  256.9 0.6 copy-done.7
  257.6 0.1 copy-done.8
  257.6 0.1 copy-done.9
  257.7 2.2 shard_map.135
  (57 shorter events, 0.1 us)
Async XLA Ops:
  7.5 5.1 %copy-start.3 = (bf16[520,128]{1,0:T(8,128)(2,1)S(1)}, bf16[520,128]{1,0:T(8,128)(2,1)}, u32[]{:S(2)}) copy-start(bf16[520,128]{1,0:T(8,128)(2,1)} %shard_map.129.refs_0_._) | copy-start | bytes 399364
  7.5 121.7 %all-to-all-start = ((bf16[4,2,192,1408]{3,2,1,0:T(8,128)(2,1)}), bf16[4,2,192,1408]{3,2,1,0:T(8,128)(2,1)}, u32[]{:S(2)}, u32[]{:S(2)}) async-start(bf16[4,2,192,1408]{3,2,1,0:T(8,128)(2,1)} %shard_map.131), calls=%async_computation | async-start | bytes 8650752 | tf_op jit(solution)/shard_map/all_to_all | solution.py:293
  12.7 23.2 %collective-permute-start.3 = (bf16[520,128]{1,0:T(8,128)(2,1)S(1)}, bf16[520,128]{1,0:T(8,128)(2,1)S(1)}, u32[]{:S(2)}, u32[]{:S(2)}) collective-permute-start(bf16[520,128]{1,0:T(8,128)(2,1)S(1)} %copy-done.3), channel_id=1, source_target_pairs={{0,224},{4,36},{8,232},{12,44},{16,240},{20,52},{24,248},{28,60},{... | collective-permute-start | bytes 399368 | tf_op jit(solution)/shard_map/ppermute | solution.py:243
  22.2 23.9 %collective-permute-start = (bf16[520,128]{1,0:T(8,128)(2,1)S(1)}, bf16[520,128]{1,0:T(8,128)(2,1)S(1)}, u32[]{:S(2)}, u32[]{:S(2)}) collective-permute-start(bf16[520,128]{1,0:T(8,128)(2,1)S(1)} %copy-done.3), channel_id=1, source_target_pairs={{0,32},{4,228},{8,40},{12,236},{16,48},{20,244},{24,56},{28,252},{... | collective-permute-start | bytes 399368 | tf_op jit(solution)/shard_map/ppermute | solution.py:243
  35.9 53.9 %copy-start.19 = (bf16[520,128]{1,0:T(8,128)(2,1)}, bf16[520,128]{1,0:T(8,128)(2,1)S(1)}, u32[]{:S(2)}) copy-start(bf16[520,128]{1,0:T(8,128)(2,1)S(1)} %collective-permute-done.3.refs_4_) | copy-start | bytes 399364
  35.9 18.3 %collective-permute-start.4 = (bf16[520,128]{1,0:T(8,128)(2,1)S(1)}, bf16[520,128]{1,0:T(8,128)(2,1)S(1)}, u32[]{:S(2)}, u32[]{:S(2)}) collective-permute-start(bf16[520,128]{1,0:T(8,128)(2,1)S(1)} %collective-permute-done.3.refs_4_), channel_id=1, source_target_pairs={{0,224},{4,36},{8,232},{12,44},{16,240},{20,52},{24,248},{28,60},{... | collective-permute-start | bytes 399368 | tf_op jit(solution)/shard_map/ppermute | solution.py:243
  46.1 43.6 %copy-start.20 = (bf16[520,128]{1,0:T(8,128)(2,1)}, bf16[520,128]{1,0:T(8,128)(2,1)S(1)}, u32[]{:S(2)}) copy-start(bf16[520,128]{1,0:T(8,128)(2,1)S(1)} %collective-permute-done.refs_1_) | copy-start | bytes 399364
  46.1 17.1 %collective-permute-start.1 = (bf16[520,128]{1,0:T(8,128)(2,1)S(1)}, bf16[520,128]{1,0:T(8,128)(2,1)S(1)}, u32[]{:S(2)}, u32[]{:S(2)}) collective-permute-start(bf16[520,128]{1,0:T(8,128)(2,1)S(1)} %collective-permute-done.refs_1_), channel_id=1, source_target_pairs={{0,32},{4,228},{8,40},{12,236},{16,48},{20,244},{24,56},{28,252},{... | collective-permute-start | bytes 399368 | tf_op jit(solution)/shard_map/ppermute | solution.py:243
  54.2 35.6 %copy-start.21 = (bf16[520,128]{1,0:T(8,128)(2,1)}, bf16[520,128]{1,0:T(8,128)(2,1)S(1)}, u32[]{:S(2)}) copy-start(bf16[520,128]{1,0:T(8,128)(2,1)S(1)} %collective-permute-done.4.refs_5_) | copy-start | bytes 399364
  54.2 17.2 %collective-permute-start.5 = (bf16[520,128]{1,0:T(8,128)(2,1)S(1)}, bf16[520,128]{1,0:T(8,128)(2,1)S(1)}, u32[]{:S(2)}, u32[]{:S(2)}) collective-permute-start(bf16[520,128]{1,0:T(8,128)(2,1)S(1)} %collective-permute-done.4.refs_5_), channel_id=1, source_target_pairs={{0,224},{4,36},{8,232},{12,44},{16,240},{20,52},{24,248},{28,60},{... | collective-permute-start | bytes 399368 | tf_op jit(solution)/shard_map/ppermute | solution.py:243
  63.2 26.6 %copy-start.22 = (bf16[520,128]{1,0:T(8,128)(2,1)}, bf16[520,128]{1,0:T(8,128)(2,1)S(1)}, u32[]{:S(2)}) copy-start(bf16[520,128]{1,0:T(8,128)(2,1)S(1)} %collective-permute-done.1.refs_2_) | copy-start | bytes 399364
  63.2 17.1 %collective-permute-start.2 = (bf16[520,128]{1,0:T(8,128)(2,1)S(1)}, bf16[520,128]{1,0:T(8,128)(2,1)S(1)}, u32[]{:S(2)}, u32[]{:S(2)}) collective-permute-start(bf16[520,128]{1,0:T(8,128)(2,1)S(1)} %collective-permute-done.1.refs_2_), channel_id=1, source_target_pairs={{0,32},{4,228},{8,40},{12,236},{16,48},{20,244},{24,56},{28,252},{... | collective-permute-start | bytes 399368 | tf_op jit(solution)/shard_map/ppermute | solution.py:243
  71.4 18.4 %copy-start.10 = (bf16[520,128]{1,0:T(8,128)(2,1)}, bf16[520,128]{1,0:T(8,128)(2,1)S(1)}, u32[]{:S(2)}) copy-start(bf16[520,128]{1,0:T(8,128)(2,1)S(1)} %collective-permute-done.5.refs_6_) | copy-start | bytes 399364
  71.4 18.3 %collective-permute-start.7 = (bf16[264,128]{1,0:T(8,128)(2,1)S(1)}, bf16[264,128]{1,0:T(8,128)(2,1)S(1)}, u32[]{:S(2)}, u32[]{:S(2)}) collective-permute-start(bf16[264,128]{1,0:T(8,128)(2,1)S(1)} %slice.9), channel_id=1, source_target_pairs={{0,224},{4,36},{8,232},{12,44},{16,240},{20,52},{24,248},{28,60},{... | collective-permute-start | bytes 202760 | tf_op jit(solution)/shard_map/ppermute | solution.py:243
  80.3 9.5 %copy-start.11 = (bf16[520,128]{1,0:T(8,128)(2,1)}, bf16[520,128]{1,0:T(8,128)(2,1)S(1)}, u32[]{:S(2)}) copy-start(bf16[520,128]{1,0:T(8,128)(2,1)S(1)} %collective-permute-done.2.refs_3_) | copy-start | bytes 399364
  80.3 9.4 %collective-permute-start.6 = (bf16[256,128]{1,0:T(8,128)(2,1)S(1)}, bf16[256,128]{1,0:T(8,128)(2,1)S(1)}, u32[]{:S(2)}, u32[]{:S(2)}) collective-permute-start(bf16[256,128]{1,0:T(8,128)(2,1)S(1)} %slice.8), channel_id=1, source_target_pairs={{0,32},{4,228},{8,40},{12,236},{16,48},{20,244},{24,56},{28,252},{... | collective-permute-start | bytes 196616 | tf_op jit(solution)/shard_map/ppermute | solution.py:243
  89.8 0.6 copy-start.24
  90.4 0.6 copy-start.23
  96.2 19.7 %collective-permute-start.10 = (bf16[816,128]{1,0:T(8,128)(2,1)}, bf16[816,128]{1,0:T(8,128)(2,1)S(1)}, u32[]{:S(2)}, u32[]{:S(2)}) collective-permute-start(bf16[816,128]{1,0:T(8,128)(2,1)} %get-tuple-element.30), channel_id=1, source_target_pairs={{0,244},{4,16},{8,252},{12,24},{16,4},{20,32},{24,12},{28,40},{32,... | collective-permute-start | bytes 626696 | tf_op jit(solution)/shard_map/ppermute | solution.py:243
  102.7 16.3 %collective-permute-start.11 = (bf16[816,128]{1,0:T(8,128)(2,1)}, bf16[816,128]{1,0:T(8,128)(2,1)S(1)}, u32[]{:S(2)}, u32[]{:S(2)}) collective-permute-start(bf16[816,128]{1,0:T(8,128)(2,1)} %get-tuple-element.31), channel_id=1, source_target_pairs={{0,8},{4,252},{8,16},{12,4},{16,24},{20,12},{24,32},{28,20},{32,40... | collective-permute-start | bytes 626696 | tf_op jit(solution)/shard_map/ppermute | solution.py:243
  106.1 16.6 %collective-permute-start.12 = (bf16[816,128]{1,0:T(8,128)(2,1)}, bf16[816,128]{1,0:T(8,128)(2,1)S(1)}, u32[]{:S(2)}, u32[]{:S(2)}) collective-permute-start(bf16[816,128]{1,0:T(8,128)(2,1)} %get-tuple-element.32), channel_id=1, source_target_pairs={{0,248},{4,12},{8,0},{12,20},{16,8},{20,28},{24,16},{28,36},{32,24... | collective-permute-start | bytes 626696 | tf_op jit(solution)/shard_map/ppermute | solution.py:243
  108.0 14.7 %collective-permute-start.13 = (bf16[816,128]{1,0:T(8,128)(2,1)}, bf16[816,128]{1,0:T(8,128)(2,1)S(1)}, u32[]{:S(2)}, u32[]{:S(2)}) collective-permute-start(bf16[816,128]{1,0:T(8,128)(2,1)} %get-tuple-element.33), channel_id=1, source_target_pairs={{0,4},{4,0},{8,12},{12,8},{16,20},{20,16},{24,28},{28,24},{32,36},... | collective-permute-start | bytes 626696 | tf_op jit(solution)/shard_map/ppermute | solution.py:243
  113.6 9.2 %collective-permute-start.14 = (bf16[816,128]{1,0:T(8,128)(2,1)}, bf16[816,128]{1,0:T(8,128)(2,1)S(1)}, u32[]{:S(2)}, u32[]{:S(2)}) collective-permute-start(bf16[816,128]{1,0:T(8,128)(2,1)} %get-tuple-element.34), channel_id=1, source_target_pairs={{0,252},{4,8},{8,4},{12,16},{16,12},{20,24},{24,20},{28,32},{32,28... | collective-permute-start | bytes 626696 | tf_op jit(solution)/shard_map/ppermute | solution.py:243
  115.9 13.4 %copy-start.12 = (bf16[816,128]{1,0:T(8,128)(2,1)}, bf16[816,128]{1,0:T(8,128)(2,1)S(1)}, u32[]{:S(2)}) copy-start(bf16[816,128]{1,0:T(8,128)(2,1)S(1)} %collective-permute-done.10.refs_2_) | copy-start | bytes 626692
  115.9 9.0 %collective-permute-start.8 = (bf16[816,128]{1,0:T(8,128)(2,1)}, bf16[816,128]{1,0:T(8,128)(2,1)S(1)}, u32[]{:S(2)}, u32[]{:S(2)}) collective-permute-start(bf16[816,128]{1,0:T(8,128)(2,1)} %get-tuple-element.28), channel_id=1, source_target_pairs={{0,240},{4,20},{8,248},{12,28},{16,0},{20,36},{24,8},{28,44},{32,1... | collective-permute-start | bytes 626696 | tf_op jit(solution)/shard_map/ppermute | solution.py:243
  119.0 10.2 %copy-start.13 = (bf16[816,128]{1,0:T(8,128)(2,1)}, bf16[816,128]{1,0:T(8,128)(2,1)S(1)}, u32[]{:S(2)}) copy-start(bf16[816,128]{1,0:T(8,128)(2,1)S(1)} %collective-permute-done.11.refs_3_) | copy-start | bytes 626692
  119.0 10.2 %collective-permute-start.9 = (bf16[816,128]{1,0:T(8,128)(2,1)}, bf16[816,128]{1,0:T(8,128)(2,1)S(1)}, u32[]{:S(2)}, u32[]{:S(2)}) collective-permute-start(bf16[816,128]{1,0:T(8,128)(2,1)} %get-tuple-element.29), channel_id=1, source_target_pairs={{0,12},{4,248},{8,20},{12,0},{16,28},{20,8},{24,36},{28,16},{32,44... | collective-permute-start | bytes 626696 | tf_op jit(solution)/shard_map/ppermute | solution.py:243
  122.7 6.6 %copy-start.14 = (bf16[816,128]{1,0:T(8,128)(2,1)}, bf16[816,128]{1,0:T(8,128)(2,1)S(1)}, u32[]{:S(2)}) copy-start(bf16[816,128]{1,0:T(8,128)(2,1)S(1)} %collective-permute-done.12.refs_4_) | copy-start | bytes 626692
  122.7 6.6 %copy-start.15 = (bf16[816,128]{1,0:T(8,128)(2,1)}, bf16[816,128]{1,0:T(8,128)(2,1)S(1)}, u32[]{:S(2)}) copy-start(bf16[816,128]{1,0:T(8,128)(2,1)S(1)} %collective-permute-done.13.refs_5_) | copy-start | bytes 626692
  122.7 6.6 %copy-start.16 = (bf16[816,128]{1,0:T(8,128)(2,1)}, bf16[816,128]{1,0:T(8,128)(2,1)S(1)}, u32[]{:S(2)}) copy-start(bf16[816,128]{1,0:T(8,128)(2,1)S(1)} %collective-permute-done.14.refs_6_) | copy-start | bytes 626692
  124.9 4.4 %copy-start.17 = (bf16[816,128]{1,0:T(8,128)(2,1)}, bf16[816,128]{1,0:T(8,128)(2,1)S(1)}, u32[]{:S(2)}) copy-start(bf16[816,128]{1,0:T(8,128)(2,1)S(1)} %collective-permute-done.8.refs_0_) | copy-start | bytes 626692
  129.2 0.7 copy-start.18
  139.2 32.4 %collective-permute-start.18 = (bf16[4,2,192,256]{3,2,1,0:T(8,128)(2,1)}, bf16[4,2,192,256]{3,2,1,0:T(8,128)(2,1)S(1)}, u32[]{:S(2)}, u32[]{:S(2)}) collective-permute-start(bf16[4,2,192,256]{3,2,1,0:T(8,128)(2,1)} %get-tuple-element.44), channel_id=1, source_target_pairs={{0,1},{1,2},{2,3},{3,0},{4,7},{5,4},{6,5},{7,6},{8,9},{9,10},{10,1... | collective-permute-start | bytes 2359304 | tf_op jit(solution)/shard_map/ppermute | solution.py:243
  143.3 30.2 %collective-permute-start.19 = (bf16[4,2,192,256]{3,2,1,0:T(8,128)(2,1)}, bf16[4,2,192,256]{3,2,1,0:T(8,128)(2,1)S(1)}, u32[]{:S(2)}, u32[]{:S(2)}) collective-permute-start(bf16[4,2,192,256]{3,2,1,0:T(8,128)(2,1)} %get-tuple-element.45), channel_id=1, source_target_pairs={{0,2},{1,3},{2,0},{3,1},{4,6},{5,7},{6,4},{7,5},{8,10},{9,11},{10,... | collective-permute-start | bytes 2359304 | tf_op jit(solution)/shard_map/ppermute | solution.py:243
  145.7 33.9 %collective-permute-start.20 = (bf16[4,2,192,256]{3,2,1,0:T(8,128)(2,1)}, bf16[4,2,192,256]{3,2,1,0:T(8,128)(2,1)S(1)}, u32[]{:S(2)}, u32[]{:S(2)}) collective-permute-start(bf16[4,2,192,256]{3,2,1,0:T(8,128)(2,1)} %get-tuple-element.46), channel_id=1, source_target_pairs={{0,3},{1,0},{2,1},{3,2},{4,5},{5,6},{6,7},{7,4},{8,11},{9,8},{10,9... | collective-permute-start | bytes 2359304 | tf_op jit(solution)/shard_map/ppermute | solution.py:243
  148.2 42.1 %collective-permute-start.15 = (bf16[2,192,384]{2,1,0:T(8,128)(2,1)}, bf16[2,192,384]{2,1,0:T(8,128)(2,1)S(1)}, u32[]{:S(2)}, u32[]{:S(2)}) collective-permute-start(bf16[2,192,384]{2,1,0:T(8,128)(2,1)} %get-tuple-element.38), channel_id=1, source_target_pairs={{0,256},{256,512},{512,768},{768,0},{4,772},{260,4},{516,260},{772... | collective-permute-start | bytes 884744 | tf_op jit(solution)/shard_map/ppermute | solution.py:243
  151.8 101.7 %collective-permute-start.16 = (bf16[2,192,384]{2,1,0:T(8,128)(2,1)}, bf16[2,192,384]{2,1,0:T(8,128)(2,1)S(1)}, u32[]{:S(2)}, u32[]{:S(2)}) collective-permute-start(bf16[2,192,384]{2,1,0:T(8,128)(2,1)} %get-tuple-element.39), channel_id=1, source_target_pairs={{0,512},{256,768},{512,0},{768,256},{4,516},{260,772},{516,4},{772... | collective-permute-start | bytes 884744 | tf_op jit(solution)/shard_map/ppermute | solution.py:243
  171.6 8.0 %copy-start = (bf16[4,2,192,256]{3,2,1,0:T(8,128)(2,1)}, bf16[4,2,192,256]{3,2,1,0:T(8,128)(2,1)S(1)}, u32[]{:S(2)}) copy-start(bf16[4,2,192,256]{3,2,1,0:T(8,128)(2,1)S(1)} %collective-permute-done.18.refs_1_) | copy-start | bytes 2359300
  171.6 81.9 %collective-permute-start.17 = (bf16[2,192,384]{2,1,0:T(8,128)(2,1)}, bf16[2,192,384]{2,1,0:T(8,128)(2,1)S(1)}, u32[]{:S(2)}, u32[]{:S(2)}) collective-permute-start(bf16[2,192,384]{2,1,0:T(8,128)(2,1)} %get-tuple-element.40), channel_id=1, source_target_pairs={{0,768},{256,0},{512,256},{768,512},{4,260},{260,516},{516,772},{7... | collective-permute-start | bytes 884744 | tf_op jit(solution)/shard_map/ppermute | solution.py:243
  173.5 6.1 %copy-start.1 = (bf16[4,2,192,256]{3,2,1,0:T(8,128)(2,1)}, bf16[4,2,192,256]{3,2,1,0:T(8,128)(2,1)S(1)}, u32[]{:S(2)}) copy-start(bf16[4,2,192,256]{3,2,1,0:T(8,128)(2,1)S(1)} %collective-permute-done.19.refs_2_) | copy-start | bytes 2359300
  179.6 0.9 copy-start.2
  183.6 73.3 %collective-permute-start.21 = (bf16[2,192,256]{2,1,0:T(8,128)(2,1)}, bf16[2,192,256]{2,1,0:T(8,128)(2,1)S(1)}, u32[]{:S(2)}, u32[]{:S(2)}) collective-permute-start(bf16[2,192,256]{2,1,0:T(8,128)(2,1)} %get-tuple-element.48), channel_id=1, source_target_pairs={{0,256},{256,512},{512,768},{768,0},{4,772},{260,4},{516,260},{772... | collective-permute-start | bytes 589832 | tf_op jit(solution)/shard_map/ppermute | solution.py:243
  188.4 68.5 %collective-permute-start.22 = (bf16[2,192,256]{2,1,0:T(8,128)(2,1)}, bf16[2,192,256]{2,1,0:T(8,128)(2,1)S(1)}, u32[]{:S(2)}, u32[]{:S(2)}) collective-permute-start(bf16[2,192,256]{2,1,0:T(8,128)(2,1)} %get-tuple-element.49), channel_id=1, source_target_pairs={{0,512},{256,768},{512,0},{768,256},{4,516},{260,772},{516,4},{772... | collective-permute-start | bytes 589832 | tf_op jit(solution)/shard_map/ppermute | solution.py:243
  190.4 63.2 %copy-start.4 = (bf16[2,192,384]{2,1,0:T(8,128)(2,1)}, bf16[2,192,384]{2,1,0:T(8,128)(2,1)S(1)}, u32[]{:S(2)}) copy-start(bf16[2,192,384]{2,1,0:T(8,128)(2,1)S(1)} %collective-permute-done.15.refs_1_) | copy-start | bytes 884740
  190.4 66.6 %collective-permute-start.23 = (bf16[2,192,256]{2,1,0:T(8,128)(2,1)}, bf16[2,192,256]{2,1,0:T(8,128)(2,1)S(1)}, u32[]{:S(2)}, u32[]{:S(2)}) collective-permute-start(bf16[2,192,256]{2,1,0:T(8,128)(2,1)} %get-tuple-element.50), channel_id=1, source_target_pairs={{0,768},{256,0},{512,256},{768,512},{4,260},{260,516},{516,772},{7... | collective-permute-start | bytes 589832 | tf_op jit(solution)/shard_map/ppermute | solution.py:243
  253.5 0.7 copy-start.5
  253.5 0.8 copy-start.6
  256.9 0.7 copy-start.7
  256.9 0.7 copy-start.8
  256.9 0.8 copy-start.9

commit v4 on v3

--- a/solution.py
+++ b/solution.py
@@ -11,25 +11,28 @@
 OFFSETS = (0, -1, -2, -3, 1, 2, 3, 4)
 SHIFTS = (-4, 3, -3, 2, -2, 1, -1, 0)
 VMEM = pltpu.VMEM
-LIMIT = 60 * 1024 * 1024
 
 
 def spec():
     return pl.BlockSpec(memory_space=VMEM)
 
 
-def call(body, outs, *args, scratch=(), untouched=(), flops=10**6, moved=10**6):
+def call(body, outs, *args, scratch=(), untouched=(), far_outs=0, aliases=None, flops=10**6, moved=10**6, mib=60):
     smem = pl.BlockSpec(memory_space=pltpu.SMEM)
     specs = [smem if a.dtype == jnp.int32 and a.shape == (3,) else spec() for a in args]
+    out_specs = jax.tree.map(lambda _: spec(), outs)
+    for i in range(far_outs):
+        out_specs[i] = pl.BlockSpec(memory_space=pltpu.HBM)
     for i in untouched:
         specs[i] = pl.BlockSpec(memory_space=pl.ANY)
     return pl.pallas_call(
         body,
         out_shape=outs,
         in_specs=specs,
-        out_specs=jax.tree.map(lambda _: spec(), outs),
+        out_specs=out_specs,
         scratch_shapes=list(scratch),
-        compiler_params=pltpu.CompilerParams(vmem_limit_bytes=LIMIT),
+        input_output_aliases=aliases or {},
+        compiler_params=pltpu.CompilerParams(vmem_limit_bytes=mib * 1024 * 1024),
         cost_estimate=pl.CostEstimate(flops=flops, bytes_accessed=moved, transcendentals=0),
     )(*args)
 
@@ -76,48 +79,71 @@
             out_ref[t, e, :, 1024:1408] = hidden
 
 
-def select_body(self_ref, onehot_ref, code_ref, exp_ref, *refs):
-    blocks, outs = refs[:9], refs[9:]
-    s = self_ref[0]
-    routes = [b[512:520, :].astype(jnp.float32) for b in blocks[:7]]
-    routes.append(blocks[8][256:264, :].astype(jnp.float32))
+def select(self_ref, onehot_ref, code_ref, exp_ref, routes, columns, first):
+    s, tokens = self_ref[0], 64 * len(routes)
+    routes = [r.astype(jnp.float32) for r in routes]
     ids = jnp.concatenate([r[:, :64] for r in routes], axis=1)
     probs = jnp.concatenate([r[:, 64:] for r in routes], axis=1)
     mine = (2 * (s + way(self_ref) * exp_ref[:, :1]) + exp_ref[:, 1:2]) & 127
     mine = mine.astype(jnp.float32)
-    match = jnp.zeros((16, 512), jnp.float32)
-    prob = jnp.zeros((16, 512), jnp.float32)
+    match = jnp.zeros((16, tokens), jnp.float32)
+    prob = jnp.zeros((16, tokens), jnp.float32)
     for k in range(8):
         hit = ids[k : k + 1, :] == mine
         match = jnp.where(hit, 1.0, match)
         prob = jnp.where(hit, probs[k : k + 1, :], prob)
-    before = earlier_matrix(128, 64)
     low = match.astype(jnp.bfloat16)
-    pos = jnp.concatenate(
-        [dot(low[:, 128 * c : 128 * (c + 1)], before) for c in range(4)], axis=1
-    )
-    block = lax.broadcasted_iota(jnp.int32, (16, 512), 1) >> 6
+    before = earlier_matrix(min(tokens, 128), 64)
+    parts = []
+    for c in range(0, tokens, 128):
+        part = low[:, c : c + 128]
+        parts.append(dot(part, before[: part.shape[1], : part.shape[1]]))
+    pos = parts[0] if len(parts) == 1 else jnp.concatenate(parts, axis=1)
+    block = (lax.broadcasted_iota(jnp.int32, (16, tokens), 1) >> 6) + first
     code = jnp.where(match > 0.0, pos + 6.0 * block.astype(jnp.float32), -1.0)
     onehot = onehot_ref[...]
-    spread = dot(onehot, code.astype(jnp.bfloat16))
-    chosen = spread == code_ref[...]
+    chosen = dot(onehot, code.astype(jnp.bfloat16)) == code_ref[...]
     pick = jnp.where(chosen, 1.0, 0.0).astype(jnp.bfloat16)
     weights = dot(onehot, prob.astype(jnp.bfloat16))
     weighted = jnp.where(chosen, weights, 0.0).astype(jnp.bfloat16)
-    slot_probs = dot_nt(jnp.ones((8, 512), jnp.bfloat16), weighted).astype(jnp.bfloat16)
+    slot_probs = dot_nt(jnp.ones((8, tokens), jnp.bfloat16), weighted)
+    return [dot(pick, columns(c)) for c in range(8)], slot_probs
+
+
+def store_pieces(outs, rows, slot_probs, base):
     for c in range(8):
-        parts = [b[c * 64 : (c + 1) * 64, :] for b in blocks[:7]]
-        last = blocks[7] if c < 4 else blocks[8]
-        parts.append(last[(c % 4) * 64 : (c % 4 + 1) * 64, :])
-        rows = dot(pick, jnp.concatenate(parts, axis=0)).astype(jnp.bfloat16)
         for v in range(8):
             for e in range(2):
-                outs[v][c * 96 + e * 48 : c * 96 + (e + 1) * 48, :] = rows[
-                    e * 384 + v * 48 : e * 384 + (v + 1) * 48, :
-                ]
+                at = slice(c * 96 + e * 48, c * 96 + (e + 1) * 48)
+                part = rows[c][e * 384 + v * 48 : e * 384 + (v + 1) * 48, :].astype(jnp.bfloat16)
+                outs[v][at, :] = part if base is None else base[v][at, :] + part
     for v in range(8):
         for c in range(6):
-            outs[v][768 + 8 * c : 776 + 8 * c, :] = slot_probs[:, 128 * c : 128 * (c + 1)]
+            at = slice(768 + 8 * c, 776 + 8 * c)
+            part = slot_probs[:, 128 * c : 128 * (c + 1)].astype(jnp.bfloat16)
+            outs[v][at, :] = part if base is None else base[v][at, :] + part
+
+
+def near_body(self_ref, onehot_ref, code_ref, exp_ref, *refs):
+    blocks, outs = refs[:7], refs[7:]
+
+    def columns(c):
+        return jnp.concatenate([b[c * 64 : (c + 1) * 64, :] for b in blocks], axis=0)
+
+    routes = [b[512:520, :] for b in blocks]
+    rows, probs = select(self_ref, onehot_ref, code_ref, exp_ref, routes, columns, 0)
+    store_pieces(outs, rows, probs, None)
+
+
+def far_body(self_ref, onehot_ref, code_ref, exp_ref, *refs):
+    halves, base, outs = refs[:2], refs[2:10], refs[10:]
+
+    def columns(c):
+        return halves[c // 4][(c % 4) * 64 : (c % 4 + 1) * 64, :]
+
+    routes = [halves[1][256:264, :]]
+    rows, probs = select(self_ref, onehot_ref, code_ref, exp_ref, routes, columns, 7)
+    store_pieces(outs, rows, probs, base)
 
 
 def expert_body(self_ref, place_ref, *refs):
@@ -157,14 +183,6 @@
             rows_ref[here, c * 256 : (c + 1) * 256] = part.astype(jnp.bfloat16)
             scaled_ref[here, c * 256 : (c + 1) * 256] = (part * column).astype(jnp.bfloat16)
     for e in range(2):
-        hidden = jnp.concatenate([wh_ref[k, e, :, 1024:1408] for k in range(4)], axis=0)
-        for rho in range(4):
-            start = pl.multiple_of(((r + turn * rho) & 3) * 256, 256)
-            part = dot(hidden, scaled_ref[e * 384 : (e + 1) * 384, pl.ds(start, 256)])
-            part = part.astype(jnp.bfloat16)
-            for k in range(4):
-                gw_refs[rho][k, e] = part[k * 192 : (k + 1) * 192, :]
-    for e in range(2):
         total = jnp.zeros((1, 384), jnp.float32)
         for delta in range(4):
             k = (t + turn * delta) & 3
@@ -173,6 +191,14 @@
             hidden = wh_ref[k, e, :, 1024:1408].astype(jnp.float32)
             total += jnp.sum(part * hidden, axis=0, keepdims=True)
         dots_ref[e : e + 1, :] = total
+    for e in range(2):
+        hidden = jnp.concatenate([wh_ref[k, e, :, 1024:1408] for k in range(4)], axis=0)
+        for rho in range(4):
+            start = pl.multiple_of(((r + turn * rho) & 3) * 256, 256)
+            part = dot(hidden, scaled_ref[e * 384 : (e + 1) * 384, pl.ds(start, 256)])
+            part = part.astype(jnp.bfloat16)
+            for k in range(4):
+                gw_refs[rho][k, e] = part[k * 192 : (k + 1) * 192, :]
 
 
 def local_body(prob_ref, *refs):
@@ -271,7 +297,7 @@
     gate_t = jnp.transpose(gate[0], (0, 2, 1))
     up_t = jnp.transpose(up[0], (0, 2, 1))
 
-    packed = call(pack_body, shape((520, 128), bf16), own, x, ids_t, probs.T)
+    packed = call(pack_body, shape((520, 128), bf16), own, x, ids_t, probs.T, mib=60)
     blocks = {0: packed}
     for step in (1, 2, 3):
         blocks[-step] = shifted(blocks[1 - step], STRIDE, "expert")
@@ -288,23 +314,31 @@
         packed,
         untouched=(3,),
         flops=10**7,
-        moved=8 * 1024 * 1024,
-    )
+        moved=8 * 1024 * 1024, mib=60)
     wh_all = lax.all_to_all(to_send, "tensor", split_axis=0, concat_axis=0, tiled=True)
 
     onehot, code, expert, tables = slot_tables()
+    chooser = (own, jnp.asarray(onehot, bf16), jnp.asarray(code), jnp.asarray(expert))
+    near = call(
+        near_body,
+        [shape((816, 128), bf16)] * 8,
+        *chooser,
+        *[blocks[o] for o in OFFSETS[:7]],
+        flops=10**9,
+        moved=4 * 1024 * 1024,
+        mib=14,
+    )
     pieces = call(
-        select_body,
+        far_body,
         [shape((816, 128), bf16)] * 8,
-        own,
-        jnp.asarray(onehot, bf16),
-        jnp.asarray(code),
-        jnp.asarray(expert),
-        *[blocks[o] for o in OFFSETS[:7]],
+        *chooser,
         far_low,
         far_high,
-        flops=2 * 768 * 512 * 1024,
+        *near,
+        aliases={6 + v: v for v in range(8)},
+        flops=10**8,
         moved=4 * 1024 * 1024,
+        mib=14,
     )
     pieces = [p if j == 0 else shifted(p, j, "expert") for p, j in zip(pieces, SHIFTS)]
 
@@ -317,10 +351,11 @@
         jnp.asarray(tables),
         *pieces,
         wh_all,
-        scratch=[VMEM((768, 1024), bf16)] * 3,
+        scratch=[
+            *[VMEM((768, 1024), bf16)] * 3,
+        ],
         flops=6 * 10**9,
-        moved=12 * 1024 * 1024,
-    )
+        moved=12 * 1024 * 1024, mib=60)
     gh, gw, dots, prob = results[:4], results[4:8], results[8], results[9]
 
     gw = spread(gw, "dp")
@@ -330,7 +365,7 @@
     back = lax.all_to_all(cells, ("tensor", "expert"), split_axis=0, concat_axis=0, tiled=True)
     table = back.reshape(4, 2 * count, 6).sum(axis=0)
 
-    summed = call(replica_body, [shape((2, 192, 256), bf16)] * 4, own, *gw, moved=4 * 1024 * 1024, flops=10**7)
+    summed = call(replica_body, [shape((2, 192, 256), bf16)] * 4, own, *gw, moved=4 * 1024 * 1024, flops=10**7, mib=12)
     summed = spread(summed, "tensor")
     grad_gate, grad_up = call(
         local_body,
@@ -340,10 +375,9 @@
         gate_t,
         up_t,
         flops=10**7,
-        moved=4 * 1024 * 1024,
-    )
-    grad_w = call(place_body, shape((2, 192, 1024), bf16), own, *summed, moved=2 * 1024 * 1024, flops=10**6)
-    grad_probs = call(lookup_body, shape((8, 64), f32), ids_t, table, flops=10**6, moved=10**5).T
+        moved=4 * 1024 * 1024, mib=10)
+    grad_w = call(place_body, shape((2, 192, 1024), bf16), own, *summed, moved=2 * 1024 * 1024, flops=10**6, mib=6)
+    grad_probs = call(lookup_body, shape((8, 64), f32), ids_t, table, flops=10**6, moved=10**5, mib=2).T
     return (
         jnp.transpose(grad_gate, (0, 2, 1))[None],
         jnp.transpose(grad_up, (0, 2, 1))[None],

time: 261 us -> 252 us (0.966)
  Pallas kernels: 30.3 us -> 25.1 us
  waiting for transfers between devices: 57.6 us -> 54.2 us
    pallas_call x8 -> x9, Pallas kernels: 30.3 us -> 25.1 us  [call(): pl.pallas_call(body, out_shape=outs, in_specs=specs, out_specs=out_specs,...]
    ppermute x24, waiting for transfers between devices: 57.6 us -> 54.2 us  [shifted(): return lax.ppermute(x, axes, pairs)]
  transfers between devices with their start and end apart: 25 -> 25, of which waited for: 9 -> 9; matrix products, arithmetic and copies ran while one was open for 1% -> 2% of each run, Pallas kernels for 5% -> 3%
where the time goes in v4:
time: 252 us; the launch traced here: 251 us
  starting transfers between devices  107 us (42%)
  blocking collectives  55.6 us (22%)
  waiting for transfers between devices  54.2 us (22%)
  Pallas kernels  25.1 us (10%)
  local copies, waits for them, and re-layouts  5.02 us (2%)
    ppermute x24, starting transfers between devices, shifted(): return lax.ppermute(x, axes, pairs)  102 us
    all_to_all x1, blocking collectives, backward(): lax.all_to_all(cells, ('tensor', 'expert'), split_axis=0, concat_axis=0,...  55.6 us
    ppermute x24, waiting for transfers between devices, shifted(): return lax.ppermute(x, axes, pairs)  54.2 us
    pallas_call x9, Pallas kernels, call(): pl.pallas_call(body, out_shape=outs, in_specs=specs, out_specs=out_specs,...  25.1 us
    all_to_all x1, starting transfers between devices, backward(): lax.all_to_all(to_send, 'tensor', split_axis=0, concat_axis=0, tiled=True)  5.14 us
  transfers between devices with their start and end apart: 25, of which 9 were waited for; matrix products, arithmetic and copies ran while one was open for 2% of the time, Pallas kernels for 3%

profile of v4, /device:TPU:1, one launch (start us, length us, event | category | flops | bytes accessed | tf_op | source)
XLA Modules:
  0.0 250.7 jit_solution(15545115883395760675)
XLA Ops:
  0.6 0.6 pad_add_fusion.self_ref
  1.2 1.8 shard_map.129.refs_0_._
  3.0 4.5 %shard_map.132 = bf16[4,2,192,1408]{3,2,1,0:T(8,128)(2,1)} custom-call(bf16[2,192,4096]{2,1,0:T(8,128)(2,1)} %w_ref.1, bf16[2,192,384]{2,1,0:T(8,128)(2,1)} %bitcast.22, bf16[2,192,384]{2,1,0:T(8,128)(2,1)} %bitcast.24, bf16[520,128]{1,0:T(8,128)(2,1)} %shard_map.129.refs_0_._), custom_call_target="tpu_custom_call" | custom-call | flops 10000000 | bytes 8388608 | tf_op jit(solution)/shard_map/pallas_call | solution.py:28
  7.5 0.0 copy-start.12
  7.5 5.1 %all-to-all-start = ((bf16[4,2,192,1408]{3,2,1,0:T(8,128)(2,1)}), bf16[4,2,192,1408]{3,2,1,0:T(8,128)(2,1)}, u32[]{:S(2)}, u32[]{:S(2)}) async-start(bf16[4,2,192,1408]{3,2,1,0:T(8,128)(2,1)} %shard_map.132), calls=%async_computation | async-start | bytes 8650752 | tf_op jit(solution)/shard_map/all_to_all | solution.py:318
  12.7 9.5 %collective-permute-start.4 = (bf16[520,128]{1,0:T(8,128)(2,1)S(1)}, bf16[520,128]{1,0:T(8,128)(2,1)S(1)}, u32[]{:S(2)}, u32[]{:S(2)}) collective-permute-start(bf16[520,128]{1,0:T(8,128)(2,1)S(1)} %copy-done.3), channel_id=1, source_target_pairs={{0,224},{4,36},{8,232},{12,44},{16,240},{20,52},{24,248},{28,60},{... | collective-permute-start | bytes 399368 | tf_op jit(solution)/shard_map/ppermute | solution.py:269
  22.2 12.8 %collective-permute-start = (bf16[520,128]{1,0:T(8,128)(2,1)S(1)}, bf16[520,128]{1,0:T(8,128)(2,1)S(1)}, u32[]{:S(2)}, u32[]{:S(2)}) collective-permute-start(bf16[520,128]{1,0:T(8,128)(2,1)S(1)} %copy-done.3), channel_id=1, source_target_pairs={{0,32},{4,228},{8,40},{12,236},{16,48},{20,244},{24,56},{28,252},{... | collective-permute-start | bytes 399368 | tf_op jit(solution)/shard_map/ppermute | solution.py:269
  35.1 0.8 collective-permute-done.4.refs_4_
  35.9 1.9 collective-permute-start.5
  37.8 8.4 %collective-permute-done.refs_1_ = bf16[520,128]{1,0:T(8,128)(2,1)S(1)} collective-permute-done((bf16[520,128]{1,0:T(8,128)(2,1)S(1)}, bf16[520,128]{1,0:T(8,128)(2,1)S(1)}, u32[]{:S(2)}, u32[]{:S(2)}) %collective-permute-start) | collective-permute-done | bytes 133152 | tf_op jit(solution)/shard_map/ppermute | solution.py:269
  46.2 8.0 %collective-permute-start.1 = (bf16[520,128]{1,0:T(8,128)(2,1)S(1)}, bf16[520,128]{1,0:T(8,128)(2,1)S(1)}, u32[]{:S(2)}, u32[]{:S(2)}) collective-permute-start(bf16[520,128]{1,0:T(8,128)(2,1)S(1)} %collective-permute-done.refs_1_), channel_id=1, source_target_pairs={{0,32},{4,228},{8,40},{12,236},{16,48},{20,244},{24,56},{28,252},{... | collective-permute-start | bytes 399368 | tf_op jit(solution)/shard_map/ppermute | solution.py:269
  54.2 0.0 collective-permute-done.5.refs_5_
  54.2 1.9 collective-permute-start.6
  56.1 7.1 %collective-permute-done.1.refs_2_ = bf16[520,128]{1,0:T(8,128)(2,1)S(1)} collective-permute-done((bf16[520,128]{1,0:T(8,128)(2,1)S(1)}, bf16[520,128]{1,0:T(8,128)(2,1)S(1)}, u32[]{:S(2)}, u32[]{:S(2)}) %collective-permute-start.1) | collective-permute-done | bytes 133152 | tf_op jit(solution)/shard_map/ppermute | solution.py:269
  63.3 8.1 %collective-permute-start.2 = (bf16[520,128]{1,0:T(8,128)(2,1)S(1)}, bf16[520,128]{1,0:T(8,128)(2,1)S(1)}, u32[]{:S(2)}, u32[]{:S(2)}) collective-permute-start(bf16[520,128]{1,0:T(8,128)(2,1)S(1)} %collective-permute-done.1.refs_2_), channel_id=1, source_target_pairs={{0,32},{4,228},{8,40},{12,236},{16,48},{20,244},{24,56},{28,252},{... | collective-permute-start | bytes 399368 | tf_op jit(solution)/shard_map/ppermute | solution.py:269
  71.4 0.0 collective-permute-done.6.refs_6_
  71.4 1.9 collective-permute-start.7
  73.4 7.0 %collective-permute-done.2.refs_3_ = bf16[520,128]{1,0:T(8,128)(2,1)S(1)} collective-permute-done((bf16[520,128]{1,0:T(8,128)(2,1)S(1)}, bf16[520,128]{1,0:T(8,128)(2,1)S(1)}, u32[]{:S(2)}, u32[]{:S(2)}) %collective-permute-start.2) | collective-permute-done | bytes 133152 | tf_op jit(solution)/shard_map/ppermute | solution.py:269
  80.4 4.6 %collective-permute-start.3 = (bf16[256,128]{1,0:T(8,128)(2,1)S(1)}, bf16[256,128]{1,0:T(8,128)(2,1)S(1)}, u32[]{:S(2)}, u32[]{:S(2)}) collective-permute-start(bf16[256,128]{1,0:T(8,128)(2,1)S(1)} %slice.8), channel_id=1, source_target_pairs={{0,32},{4,228},{8,40},{12,236},{16,48},{20,244},{24,56},{28,252},{... | collective-permute-start | bytes 196616 | tf_op jit(solution)/shard_map/ppermute | solution.py:269
  85.1 3.2 %shard_map.130 = (bf16[816,128]{1,0:T(8,128)(2,1)S(1)}, bf16[816,128]{1,0:T(8,128)(2,1)S(1)}, bf16[816,128]{1,0:T(8,128)(2,1)S(1)}, bf16[816,128]{1,0:T(8,128)(2...) custom-call(s32[3]{0:T(128)S(1)} %copy-done.10, ...), custom_call_target="tpu_custom_call" | custom-call | flops 1000000000 | bytes 4194304 | tf_op jit(solution)/shard_map/pallas_call | solution.py:28
  88.3 1.5 collective-permute-done.3.refs_0_
  89.8 0.0 collective-permute-done.7.refs_1_
  89.8 1.7 shard_map.131
  91.5 0.7 copy-done.6
  92.1 6.5 %collective-permute-start.10 = (bf16[816,128]{1,0:T(8,128)(2,1)S(1)}, bf16[816,128]{1,0:T(8,128)(2,1)S(1)}, u32[]{:S(2)}, u32[]{:S(2)}) collective-permute-start(bf16[816,128]{1,0:T(8,128)(2,1)S(1)} %get-tuple-element.46), channel_id=1, source_target_pairs={{0,244},{4,16},{8,252},{12,24},{16,4},{20,32},{24,12},{28,40},{32,... | collective-permute-start | bytes 626696 | tf_op jit(solution)/shard_map/ppermute | solution.py:269
  98.7 3.3 %collective-permute-start.11 = (bf16[816,128]{1,0:T(8,128)(2,1)S(1)}, bf16[816,128]{1,0:T(8,128)(2,1)S(1)}, u32[]{:S(2)}, u32[]{:S(2)}) collective-permute-start(bf16[816,128]{1,0:T(8,128)(2,1)S(1)} %get-tuple-element.47), channel_id=1, source_target_pairs={{0,8},{4,252},{8,16},{12,4},{16,24},{20,12},{24,32},{28,20},{32,40... | collective-permute-start | bytes 626696 | tf_op jit(solution)/shard_map/ppermute | solution.py:269
  102.0 2.0 collective-permute-start.12
  104.0 5.5 %collective-permute-start.13 = (bf16[816,128]{1,0:T(8,128)(2,1)S(1)}, bf16[816,128]{1,0:T(8,128)(2,1)S(1)}, u32[]{:S(2)}, u32[]{:S(2)}) collective-permute-start(bf16[816,128]{1,0:T(8,128)(2,1)S(1)} %get-tuple-element.49), channel_id=1, source_target_pairs={{0,4},{4,0},{8,12},{12,8},{16,20},{20,16},{24,28},{28,24},{32,36},... | collective-permute-start | bytes 626696 | tf_op jit(solution)/shard_map/ppermute | solution.py:269
  109.5 2.3 collective-permute-start.14
  111.8 0.0 collective-permute-done.10.refs_2_
  111.9 3.1 %collective-permute-start.8 = (bf16[816,128]{1,0:T(8,128)(2,1)S(1)}, bf16[816,128]{1,0:T(8,128)(2,1)S(1)}, u32[]{:S(2)}, u32[]{:S(2)}) collective-permute-start(bf16[816,128]{1,0:T(8,128)(2,1)S(1)} %get-tuple-element.44), channel_id=1, source_target_pairs={{0,240},{4,20},{8,248},{12,28},{16,0},{20,36},{24,8},{28,44},{32,1... | collective-permute-start | bytes 626696 | tf_op jit(solution)/shard_map/ppermute | solution.py:269
  115.0 0.0 collective-permute-done.11.refs_3_
  115.0 3.6 %collective-permute-start.9 = (bf16[816,128]{1,0:T(8,128)(2,1)S(1)}, bf16[816,128]{1,0:T(8,128)(2,1)S(1)}, u32[]{:S(2)}, u32[]{:S(2)}) collective-permute-start(bf16[816,128]{1,0:T(8,128)(2,1)S(1)} %get-tuple-element.45), channel_id=1, source_target_pairs={{0,12},{4,248},{8,20},{12,0},{16,28},{20,8},{24,36},{28,16},{32,44... | collective-permute-start | bytes 626696 | tf_op jit(solution)/shard_map/ppermute | solution.py:269
  118.6 0.0 collective-permute-done.12.refs_4_
  118.7 2.0 collective-permute-done.8.refs_0_
  120.6 4.4 %collective-permute-done.9.refs_1_ = bf16[816,128]{1,0:T(8,128)(2,1)S(1)} collective-permute-done((bf16[816,128]{1,0:T(8,128)(2,1)S(1)}, bf16[816,128]{1,0:T(8,128)(2,1)S(1)}, u32[]{:S(2)}, u32[]{:S(2)}) %collective-permute-start.9) | collective-permute-done | bytes 208928 | tf_op jit(solution)/shard_map/ppermute | solution.py:269
  125.0 0.0 all-to-all-done.refs_8_
  125.1 0.6 copy-done.19
  125.7 9.5 %shard_map.133 = (bf16[2,192,384]{2,1,0:T(8,128)(2,1)}, bf16[2,192,384]{2,1,0:T(8,128)(2,1)}, bf16[2,192,384]{2,1,0:T(8,128)(2,1)}, bf16[2,192,384]{2,1,0:T(8,12...) custom-call(s32[3]{0:T(128)} %pad_add_fusion.self_ref, ...), custom_call_target="tpu_custom_call" | custom-call | flops 6000000000 | bytes 12582912 | tf_op jit(solution)/shard_map/pallas_call | solution.py:28
  135.2 0.0 copy-start
  135.2 0.0 copy-start.1
  135.2 4.2 %collective-permute-start.18 = (bf16[4,2,192,256]{3,2,1,0:T(8,128)(2,1)}, bf16[4,2,192,256]{3,2,1,0:T(8,128)(2,1)S(1)}, u32[]{:S(2)}, u32[]{:S(2)}) collective-permute-start(bf16[4,2,192,256]{3,2,1,0:T(8,128)(2,1)} %get-tuple-element.60), channel_id=1, source_target_pairs={{0,1},{1,2},{2,3},{3,0},{4,7},{5,4},{6,5},{7,6},{8,9},{9,10},{10,1... | collective-permute-start | bytes 2359304 | tf_op jit(solution)/shard_map/ppermute | solution.py:269
  139.4 2.4 collective-permute-start.19
  141.8 2.5 %collective-permute-start.20 = (bf16[4,2,192,256]{3,2,1,0:T(8,128)(2,1)}, bf16[4,2,192,256]{3,2,1,0:T(8,128)(2,1)S(1)}, u32[]{:S(2)}, u32[]{:S(2)}) collective-permute-start(bf16[4,2,192,256]{3,2,1,0:T(8,128)(2,1)} %get-tuple-element.62), channel_id=1, source_target_pairs={{0,3},{1,0},{2,1},{3,2},{4,5},{5,6},{6,7},{7,4},{8,11},{9,8},{10,9... | collective-permute-start | bytes 2359304 | tf_op jit(solution)/shard_map/ppermute | solution.py:269
  144.3 3.6 %collective-permute-start.15 = (bf16[2,192,384]{2,1,0:T(8,128)(2,1)}, bf16[2,192,384]{2,1,0:T(8,128)(2,1)S(1)}, u32[]{:S(2)}, u32[]{:S(2)}) collective-permute-start(bf16[2,192,384]{2,1,0:T(8,128)(2,1)} %get-tuple-element.54), channel_id=1, source_target_pairs={{0,256},{256,512},{512,768},{768,0},{4,772},{260,4},{516,260},{772... | collective-permute-start | bytes 884744 | tf_op jit(solution)/shard_map/ppermute | solution.py:269
  147.9 2.8 %collective-permute-start.16 = (bf16[2,192,384]{2,1,0:T(8,128)(2,1)}, bf16[2,192,384]{2,1,0:T(8,128)(2,1)S(1)}, u32[]{:S(2)}, u32[]{:S(2)}) collective-permute-start(bf16[2,192,384]{2,1,0:T(8,128)(2,1)} %get-tuple-element.55), channel_id=1, source_target_pairs={{0,512},{256,768},{512,0},{768,256},{4,516},{260,772},{516,4},{772... | collective-permute-start | bytes 884744 | tf_op jit(solution)/shard_map/ppermute | solution.py:269
  150.7 16.9 %collective-permute-done.18.refs_1_ = bf16[4,2,192,256]{3,2,1,0:T(8,128)(2,1)S(1)} collective-permute-done((bf16[4,2,192,256]{3,2,1,0:T(8,128)(2,1)}, bf16[4,2,192,256]{3,2,1,0:T(8,128)(2,1)S(1)}, u32[]{:S(2)}, u32[]{:S(2)}) %collective-permute-start.18) | collective-permute-done | bytes 786464 | tf_op jit(solution)/shard_map/ppermute | solution.py:269
  167.7 1.9 collective-permute-start.17
  169.6 6.1 %collective-permute-done.20.refs_3_ = bf16[4,2,192,256]{3,2,1,0:T(8,128)(2,1)S(1)} collective-permute-done((bf16[4,2,192,256]{3,2,1,0:T(8,128)(2,1)}, bf16[4,2,192,256]{3,2,1,0:T(8,128)(2,1)S(1)}, u32[]{:S(2)}, u32[]{:S(2)}) %collective-permute-start.20) | collective-permute-done | bytes 786464 | tf_op jit(solution)/shard_map/ppermute | solution.py:269
  175.7 1.1 copy-done.2
  176.8 0.9 shard_map.135
  177.7 5.0 %collective-permute-start.21 = (bf16[2,192,256]{2,1,0:T(8,128)(2,1)S(1)}, bf16[2,192,256]{2,1,0:T(8,128)(2,1)S(1)}, u32[]{:S(2)}, u32[]{:S(2)}) collective-permute-start(bf16[2,192,256]{2,1,0:T(8,128)(2,1)S(1)} %get-tuple-element.64), channel_id=1, source_target_pairs={{0,256},{256,512},{512,768},{768,0},{4,772},{260,4},{516,260},{772... | collective-permute-start | bytes 589832 | tf_op jit(solution)/shard_map/ppermute | solution.py:269
  182.8 1.9 collective-permute-start.22
  184.7 2.5 collective-permute-start.23
  187.2 0.8 reshape.20
  188.0 0.1 copy.24
  188.1 0.1 copy.25
  188.3 55.6 %all_to_all.14 = f32[256,1,12]{2,1,0:T(1,128)S(1)} all-to-all(f32[256,1,12]{2,1,0:T(1,128)S(1)} %bitcast.28), channel_id=1, replica_groups=mesh['tensor'=4,'expert'=64,'dp'=4] {'tensor','expert'}, dimensions={0} | all-to-all | bytes 24576 | tf_op jit(solution)/shard_map/all_to_all | solution.py:365
  243.9 0.5 broadcast.3
  244.4 1.6 reduce.3
  246.0 1.0 reshape.21
  247.1 0.9 shard_map.137
  248.0 1.2 shard_map.134
  249.2 1.5 shard_map.136
  (48 shorter events, 0.1 us)
Async XLA Ops:
  7.5 5.2 %copy-start.3 = (bf16[520,128]{1,0:T(8,128)(2,1)S(1)}, bf16[520,128]{1,0:T(8,128)(2,1)}, u32[]{:S(2)}) copy-start(bf16[520,128]{1,0:T(8,128)(2,1)} %shard_map.129.refs_0_._) | copy-start | bytes 399364
  7.5 77.5 %copy-start.4 = (f32[768,1]{1,0:T(8,128)S(1)}, f32[768,1]{1,0:T(8,128)}, u32[]{:S(2)}) copy-start(f32[768,1]{1,0:T(8,128)} %constant.24.clone.code_ref) | copy-start | bytes 9220
  7.5 77.5 %copy-start.7 = (bf16[768,16]{1,0:T(8,128)(2,1)S(1)}, bf16[768,16]{1,0:T(8,128)(2,1)}, u32[]{:S(2)}) copy-start(bf16[768,16]{1,0:T(8,128)(2,1)} %constant.23.clone.onehot_ref) | copy-start | bytes 73732
  7.5 77.6 %copy-start.10 = (s32[3]{0:T(128)S(1)}, s32[3]{0:T(128)}, u32[]{:S(2)}) copy-start(s32[3]{0:T(128)} %pad_add_fusion.self_ref) | copy-start | bytes 40
  7.5 77.6 %copy-start.12 = (s32[16,2]{1,0:T(8,128)S(1)}, s32[16,2]{1,0:T(8,128)}, u32[]{:S(2)}) copy-start(s32[16,2]{1,0:T(8,128)} %constant.25.clone.exp_ref) | copy-start | bytes 388
  7.5 117.5 %all-to-all-start = ((bf16[4,2,192,1408]{3,2,1,0:T(8,128)(2,1)}), bf16[4,2,192,1408]{3,2,1,0:T(8,128)(2,1)}, u32[]{:S(2)}, u32[]{:S(2)}) async-start(bf16[4,2,192,1408]{3,2,1,0:T(8,128)(2,1)} %shard_map.132), calls=%async_computation | async-start | bytes 8650752 | tf_op jit(solution)/shard_map/all_to_all | solution.py:318
  12.7 23.2 %collective-permute-start.4 = (bf16[520,128]{1,0:T(8,128)(2,1)S(1)}, bf16[520,128]{1,0:T(8,128)(2,1)S(1)}, u32[]{:S(2)}, u32[]{:S(2)}) collective-permute-start(bf16[520,128]{1,0:T(8,128)(2,1)S(1)} %copy-done.3), channel_id=1, source_target_pairs={{0,224},{4,36},{8,232},{12,44},{16,240},{20,52},{24,248},{28,60},{... | collective-permute-start | bytes 399368 | tf_op jit(solution)/shard_map/ppermute | solution.py:269
  22.2 23.9 %collective-permute-start = (bf16[520,128]{1,0:T(8,128)(2,1)S(1)}, bf16[520,128]{1,0:T(8,128)(2,1)S(1)}, u32[]{:S(2)}, u32[]{:S(2)}) collective-permute-start(bf16[520,128]{1,0:T(8,128)(2,1)S(1)} %copy-done.3), channel_id=1, source_target_pairs={{0,32},{4,228},{8,40},{12,236},{16,48},{20,244},{24,56},{28,252},{... | collective-permute-start | bytes 399368 | tf_op jit(solution)/shard_map/ppermute | solution.py:269
  35.9 18.3 %collective-permute-start.5 = (bf16[520,128]{1,0:T(8,128)(2,1)S(1)}, bf16[520,128]{1,0:T(8,128)(2,1)S(1)}, u32[]{:S(2)}, u32[]{:S(2)}) collective-permute-start(bf16[520,128]{1,0:T(8,128)(2,1)S(1)} %collective-permute-done.4.refs_4_), channel_id=1, source_target_pairs={{0,224},{4,36},{8,232},{12,44},{16,240},{20,52},{24,248},{28,60},{... | collective-permute-start | bytes 399368 | tf_op jit(solution)/shard_map/ppermute | solution.py:269
  46.2 17.1 %collective-permute-start.1 = (bf16[520,128]{1,0:T(8,128)(2,1)S(1)}, bf16[520,128]{1,0:T(8,128)(2,1)S(1)}, u32[]{:S(2)}, u32[]{:S(2)}) collective-permute-start(bf16[520,128]{1,0:T(8,128)(2,1)S(1)} %collective-permute-done.refs_1_), channel_id=1, source_target_pairs={{0,32},{4,228},{8,40},{12,236},{16,48},{20,244},{24,56},{28,252},{... | collective-permute-start | bytes 399368 | tf_op jit(solution)/shard_map/ppermute | solution.py:269
  54.2 17.2 %collective-permute-start.6 = (bf16[520,128]{1,0:T(8,128)(2,1)S(1)}, bf16[520,128]{1,0:T(8,128)(2,1)S(1)}, u32[]{:S(2)}, u32[]{:S(2)}) collective-permute-start(bf16[520,128]{1,0:T(8,128)(2,1)S(1)} %collective-permute-done.5.refs_5_), channel_id=1, source_target_pairs={{0,224},{4,36},{8,232},{12,44},{16,240},{20,52},{24,248},{28,60},{... | collective-permute-start | bytes 399368 | tf_op jit(solution)/shard_map/ppermute | solution.py:269
  63.3 17.1 %collective-permute-start.2 = (bf16[520,128]{1,0:T(8,128)(2,1)S(1)}, bf16[520,128]{1,0:T(8,128)(2,1)S(1)}, u32[]{:S(2)}, u32[]{:S(2)}) collective-permute-start(bf16[520,128]{1,0:T(8,128)(2,1)S(1)} %collective-permute-done.1.refs_2_), channel_id=1, source_target_pairs={{0,32},{4,228},{8,40},{12,236},{16,48},{20,244},{24,56},{28,252},{... | collective-permute-start | bytes 399368 | tf_op jit(solution)/shard_map/ppermute | solution.py:269
  71.4 18.3 %collective-permute-start.7 = (bf16[264,128]{1,0:T(8,128)(2,1)S(1)}, bf16[264,128]{1,0:T(8,128)(2,1)S(1)}, u32[]{:S(2)}, u32[]{:S(2)}) collective-permute-start(bf16[264,128]{1,0:T(8,128)(2,1)S(1)} %slice.9), channel_id=1, source_target_pairs={{0,224},{4,36},{8,232},{12,44},{16,240},{20,52},{24,248},{28,60},{... | collective-permute-start | bytes 202760 | tf_op jit(solution)/shard_map/ppermute | solution.py:269
  80.4 9.4 %collective-permute-start.3 = (bf16[256,128]{1,0:T(8,128)(2,1)S(1)}, bf16[256,128]{1,0:T(8,128)(2,1)S(1)}, u32[]{:S(2)}, u32[]{:S(2)}) collective-permute-start(bf16[256,128]{1,0:T(8,128)(2,1)S(1)} %slice.8), channel_id=1, source_target_pairs={{0,32},{4,228},{8,40},{12,236},{16,48},{20,244},{24,56},{28,252},{... | collective-permute-start | bytes 196616 | tf_op jit(solution)/shard_map/ppermute | solution.py:269
  91.5 0.7 copy-start.6
  92.1 19.7 %collective-permute-start.10 = (bf16[816,128]{1,0:T(8,128)(2,1)S(1)}, bf16[816,128]{1,0:T(8,128)(2,1)S(1)}, u32[]{:S(2)}, u32[]{:S(2)}) collective-permute-start(bf16[816,128]{1,0:T(8,128)(2,1)S(1)} %get-tuple-element.46), channel_id=1, source_target_pairs={{0,244},{4,16},{8,252},{12,24},{16,4},{20,32},{24,12},{28,40},{32,... | collective-permute-start | bytes 626696 | tf_op jit(solution)/shard_map/ppermute | solution.py:269
  98.7 16.3 %collective-permute-start.11 = (bf16[816,128]{1,0:T(8,128)(2,1)S(1)}, bf16[816,128]{1,0:T(8,128)(2,1)S(1)}, u32[]{:S(2)}, u32[]{:S(2)}) collective-permute-start(bf16[816,128]{1,0:T(8,128)(2,1)S(1)} %get-tuple-element.47), channel_id=1, source_target_pairs={{0,8},{4,252},{8,16},{12,4},{16,24},{20,12},{24,32},{28,20},{32,40... | collective-permute-start | bytes 626696 | tf_op jit(solution)/shard_map/ppermute | solution.py:269
  102.0 16.6 %collective-permute-start.12 = (bf16[816,128]{1,0:T(8,128)(2,1)S(1)}, bf16[816,128]{1,0:T(8,128)(2,1)S(1)}, u32[]{:S(2)}, u32[]{:S(2)}) collective-permute-start(bf16[816,128]{1,0:T(8,128)(2,1)S(1)} %get-tuple-element.48), channel_id=1, source_target_pairs={{0,248},{4,12},{8,0},{12,20},{16,8},{20,28},{24,16},{28,36},{32,24... | collective-permute-start | bytes 626696 | tf_op jit(solution)/shard_map/ppermute | solution.py:269
  104.0 14.7 %collective-permute-start.13 = (bf16[816,128]{1,0:T(8,128)(2,1)S(1)}, bf16[816,128]{1,0:T(8,128)(2,1)S(1)}, u32[]{:S(2)}, u32[]{:S(2)}) collective-permute-start(bf16[816,128]{1,0:T(8,128)(2,1)S(1)} %get-tuple-element.49), channel_id=1, source_target_pairs={{0,4},{4,0},{8,12},{12,8},{16,20},{20,16},{24,28},{28,24},{32,36},... | collective-permute-start | bytes 626696 | tf_op jit(solution)/shard_map/ppermute | solution.py:269
  109.5 9.1 %collective-permute-start.14 = (bf16[816,128]{1,0:T(8,128)(2,1)S(1)}, bf16[816,128]{1,0:T(8,128)(2,1)S(1)}, u32[]{:S(2)}, u32[]{:S(2)}) collective-permute-start(bf16[816,128]{1,0:T(8,128)(2,1)S(1)} %get-tuple-element.50), channel_id=1, source_target_pairs={{0,252},{4,8},{8,4},{12,16},{16,12},{20,24},{24,20},{28,32},{32,28... | collective-permute-start | bytes 626696 | tf_op jit(solution)/shard_map/ppermute | solution.py:269
  111.9 13.2 %copy-start.13 = (bf16[816,128]{1,0:T(8,128)(2,1)}, bf16[816,128]{1,0:T(8,128)(2,1)S(1)}, u32[]{:S(2)}) copy-start(bf16[816,128]{1,0:T(8,128)(2,1)S(1)} %collective-permute-done.10.refs_2_) | copy-start | bytes 626692
  111.9 8.8 %collective-permute-start.8 = (bf16[816,128]{1,0:T(8,128)(2,1)S(1)}, bf16[816,128]{1,0:T(8,128)(2,1)S(1)}, u32[]{:S(2)}, u32[]{:S(2)}) collective-permute-start(bf16[816,128]{1,0:T(8,128)(2,1)S(1)} %get-tuple-element.44), channel_id=1, source_target_pairs={{0,240},{4,20},{8,248},{12,28},{16,0},{20,36},{24,8},{28,44},{32,1... | collective-permute-start | bytes 626696 | tf_op jit(solution)/shard_map/ppermute | solution.py:269
  115.0 10.0 %copy-start.14 = (bf16[816,128]{1,0:T(8,128)(2,1)}, bf16[816,128]{1,0:T(8,128)(2,1)S(1)}, u32[]{:S(2)}) copy-start(bf16[816,128]{1,0:T(8,128)(2,1)S(1)} %collective-permute-done.11.refs_3_) | copy-start | bytes 626692
  115.0 10.0 %collective-permute-start.9 = (bf16[816,128]{1,0:T(8,128)(2,1)S(1)}, bf16[816,128]{1,0:T(8,128)(2,1)S(1)}, u32[]{:S(2)}, u32[]{:S(2)}) collective-permute-start(bf16[816,128]{1,0:T(8,128)(2,1)S(1)} %get-tuple-element.45), channel_id=1, source_target_pairs={{0,12},{4,248},{8,20},{12,0},{16,28},{20,8},{24,36},{28,16},{32,44... | collective-permute-start | bytes 626696 | tf_op jit(solution)/shard_map/ppermute | solution.py:269
  118.6 6.4 %copy-start.15 = (bf16[816,128]{1,0:T(8,128)(2,1)}, bf16[816,128]{1,0:T(8,128)(2,1)S(1)}, u32[]{:S(2)}) copy-start(bf16[816,128]{1,0:T(8,128)(2,1)S(1)} %collective-permute-done.12.refs_4_) | copy-start | bytes 626692
  118.6 6.4 %copy-start.16 = (bf16[816,128]{1,0:T(8,128)(2,1)}, bf16[816,128]{1,0:T(8,128)(2,1)S(1)}, u32[]{:S(2)}) copy-start(bf16[816,128]{1,0:T(8,128)(2,1)S(1)} %collective-permute-done.13.refs_5_) | copy-start | bytes 626692
  118.6 6.4 %copy-start.17 = (bf16[816,128]{1,0:T(8,128)(2,1)}, bf16[816,128]{1,0:T(8,128)(2,1)S(1)}, u32[]{:S(2)}) copy-start(bf16[816,128]{1,0:T(8,128)(2,1)S(1)} %collective-permute-done.14.refs_6_) | copy-start | bytes 626692
  120.6 4.4 %copy-start.18 = (bf16[816,128]{1,0:T(8,128)(2,1)}, bf16[816,128]{1,0:T(8,128)(2,1)S(1)}, u32[]{:S(2)}) copy-start(bf16[816,128]{1,0:T(8,128)(2,1)S(1)} %collective-permute-done.8.refs_0_) | copy-start | bytes 626692
  125.0 0.7 copy-start.19
  125.7 50.0 %copy-start.11 = (s32[3]{0:T(128)S(1)}, s32[3]{0:T(128)}, u32[]{:S(2)}) copy-start(s32[3]{0:T(128)} %pad_add_fusion.self_ref) | copy-start | bytes 40
  125.7 121.4 %copy-start.9 = (s32[64,8]{0,1:T(8,128)S(1)}, s32[64,8]{0,1:T(8,128)}, u32[]{:S(2)}) copy-start(s32[64,8]{0,1:T(8,128)} %param.11) | copy-start | bytes 6148
  135.2 112.8 %copy-start = (bf16[1,2,384,192]{2,3,1,0:T(8,128)(2,1)S(1)}, bf16[1,2,384,192]{2,3,1,0:T(8,128)(2,1)}, u32[]{:S(2)}) copy-start(bf16[1,2,384,192]{2,3,1,0:T(8,128)(2,1)} %param.13) | copy-start | bytes 884740
  135.2 112.8 %copy-start.1 = (bf16[1,2,384,192]{2,3,1,0:T(8,128)(2,1)S(1)}, bf16[1,2,384,192]{2,3,1,0:T(8,128)(2,1)}, u32[]{:S(2)}) copy-start(bf16[1,2,384,192]{2,3,1,0:T(8,128)(2,1)} %param.14) | copy-start | bytes 884740
  135.2 32.5 %collective-permute-start.18 = (bf16[4,2,192,256]{3,2,1,0:T(8,128)(2,1)}, bf16[4,2,192,256]{3,2,1,0:T(8,128)(2,1)S(1)}, u32[]{:S(2)}, u32[]{:S(2)}) collective-permute-start(bf16[4,2,192,256]{3,2,1,0:T(8,128)(2,1)} %get-tuple-element.60), channel_id=1, source_target_pairs={{0,1},{1,2},{2,3},{3,0},{4,7},{5,4},{6,5},{7,6},{8,9},{9,10},{10,1... | collective-permute-start | bytes 2359304 | tf_op jit(solution)/shard_map/ppermute | solution.py:269
  139.4 30.2 %collective-permute-start.19 = (bf16[4,2,192,256]{3,2,1,0:T(8,128)(2,1)}, bf16[4,2,192,256]{3,2,1,0:T(8,128)(2,1)S(1)}, u32[]{:S(2)}, u32[]{:S(2)}) collective-permute-start(bf16[4,2,192,256]{3,2,1,0:T(8,128)(2,1)} %get-tuple-element.61), channel_id=1, source_target_pairs={{0,2},{1,3},{2,0},{3,1},{4,6},{5,7},{6,4},{7,5},{8,10},{9,11},{10,... | collective-permute-start | bytes 2359304 | tf_op jit(solution)/shard_map/ppermute | solution.py:269
  141.8 33.9 %collective-permute-start.20 = (bf16[4,2,192,256]{3,2,1,0:T(8,128)(2,1)}, bf16[4,2,192,256]{3,2,1,0:T(8,128)(2,1)S(1)}, u32[]{:S(2)}, u32[]{:S(2)}) collective-permute-start(bf16[4,2,192,256]{3,2,1,0:T(8,128)(2,1)} %get-tuple-element.62), channel_id=1, source_target_pairs={{0,3},{1,0},{2,1},{3,2},{4,5},{5,6},{6,7},{7,4},{8,11},{9,8},{10,9... | collective-permute-start | bytes 2359304 | tf_op jit(solution)/shard_map/ppermute | solution.py:269
  144.3 40.4 %collective-permute-start.15 = (bf16[2,192,384]{2,1,0:T(8,128)(2,1)}, bf16[2,192,384]{2,1,0:T(8,128)(2,1)S(1)}, u32[]{:S(2)}, u32[]{:S(2)}) collective-permute-start(bf16[2,192,384]{2,1,0:T(8,128)(2,1)} %get-tuple-element.54), channel_id=1, source_target_pairs={{0,256},{256,512},{512,768},{768,0},{4,772},{260,4},{516,260},{772... | collective-permute-start | bytes 884744 | tf_op jit(solution)/shard_map/ppermute | solution.py:269
  147.9 100.0 %collective-permute-start.16 = (bf16[2,192,384]{2,1,0:T(8,128)(2,1)}, bf16[2,192,384]{2,1,0:T(8,128)(2,1)S(1)}, u32[]{:S(2)}, u32[]{:S(2)}) collective-permute-start(bf16[2,192,384]{2,1,0:T(8,128)(2,1)} %get-tuple-element.55), channel_id=1, source_target_pairs={{0,512},{256,768},{512,0},{768,256},{4,516},{260,772},{516,4},{772... | collective-permute-start | bytes 884744 | tf_op jit(solution)/shard_map/ppermute | solution.py:269
  167.7 80.3 %collective-permute-start.17 = (bf16[2,192,384]{2,1,0:T(8,128)(2,1)}, bf16[2,192,384]{2,1,0:T(8,128)(2,1)S(1)}, u32[]{:S(2)}, u32[]{:S(2)}) collective-permute-start(bf16[2,192,384]{2,1,0:T(8,128)(2,1)} %get-tuple-element.56), channel_id=1, source_target_pairs={{0,768},{256,0},{512,256},{768,512},{4,260},{260,516},{516,772},{7... | collective-permute-start | bytes 884744 | tf_op jit(solution)/shard_map/ppermute | solution.py:269
  175.7 1.1 copy-start.2
  176.8 71.1 %copy-start.5 = (bf16[2,192,384]{2,1,0:T(8,128)(2,1)S(1)}, bf16[2,192,384]{2,1,0:T(8,128)(2,1)}, u32[]{:S(2)}) copy-start(bf16[2,192,384]{2,1,0:T(8,128)(2,1)} %get-tuple-element.53.refs_0_) | copy-start | bytes 884740
  176.8 71.2 %copy-start.8 = (f32[8,768]{1,0:T(8,128)S(1)}, f32[8,768]{1,0:T(8,128)}, u32[]{:S(2)}) copy-start(f32[8,768]{1,0:T(8,128)} %get-tuple-element.52.prob_ref) | copy-start | bytes 73732
  177.7 71.4 %collective-permute-start.21 = (bf16[2,192,256]{2,1,0:T(8,128)(2,1)S(1)}, bf16[2,192,256]{2,1,0:T(8,128)(2,1)S(1)}, u32[]{:S(2)}, u32[]{:S(2)}) collective-permute-start(bf16[2,192,256]{2,1,0:T(8,128)(2,1)S(1)} %get-tuple-element.64), channel_id=1, source_target_pairs={{0,256},{256,512},{512,768},{768,0},{4,772},{260,4},{516,260},{772... | collective-permute-start | bytes 589832 | tf_op jit(solution)/shard_map/ppermute | solution.py:269
  182.8 66.4 %collective-permute-start.22 = (bf16[2,192,256]{2,1,0:T(8,128)(2,1)S(1)}, bf16[2,192,256]{2,1,0:T(8,128)(2,1)S(1)}, u32[]{:S(2)}, u32[]{:S(2)}) collective-permute-start(bf16[2,192,256]{2,1,0:T(8,128)(2,1)S(1)} %get-tuple-element.65), channel_id=1, source_target_pairs={{0,512},{256,768},{512,0},{768,256},{4,516},{260,772},{516,4},{772... | collective-permute-start | bytes 589832 | tf_op jit(solution)/shard_map/ppermute | solution.py:269
  184.7 64.4 %collective-permute-start.23 = (bf16[2,192,256]{2,1,0:T(8,128)(2,1)S(1)}, bf16[2,192,256]{2,1,0:T(8,128)(2,1)S(1)}, u32[]{:S(2)}, u32[]{:S(2)}) collective-permute-start(bf16[2,192,256]{2,1,0:T(8,128)(2,1)S(1)} %get-tuple-element.66), channel_id=1, source_target_pairs={{0,768},{256,0},{512,256},{768,512},{4,260},{260,516},{516,772},{7... | collective-permute-start | bytes 589832 | tf_op jit(solution)/shard_map/ppermute | solution.py:269
